TPU v7x, 32 devices: a whole 2x2x4 slice. The times are simulated.
32 devices in a mesh: section: 2 (over x), fsdp: 4 (over y, core), tp: 4 (over z).
Axes of the slice: x: 2, y: 2, z: 4, core: 2. Of those that a mesh axis runs over, the one named last changes fastest.
Arguments:
- ends_in: bfloat16 [2, 2, 1024, 2048], P('section', None, ('fsdp', 'tp')), may hold values from -6 to 6
- segments: int32 [2, 1024], P(None, 'fsdp'), may hold values from 0 to 15, never falling along the last dimension, each value on 1 to 256 neighbouring positions
- ln_gain: bfloat16 [2, 2048], P('section', ('fsdp', 'tp')), may hold values from 0.5 to 1.5
- ln_bias: bfloat16 [2, 2048], P('section', ('fsdp', 'tp')), may hold values from -3 to 3
- w_qkv: bfloat16 [2, 2048, 3, 2048], P('section', 'fsdp', None, 'tp'), may hold values from -2 to 2
- w_out: bfloat16 [2, 2048, 2048], P('section', 'fsdp', 'tp'), may hold values from -0.375 to 0.375
- w_fc1: bfloat16 [2, 2048, 8192], P('section', 'fsdp', 'tp'), may hold values from -0.125 to 0.125
- w_fc2: bfloat16 [2, 2048, 8192], P('section', 'fsdp', 'tp'), may hold values from -0.0625 to 0.0625
- bias_qkv: bfloat16 [2, 3, 2048], P('section', None, ('fsdp', 'tp')), may hold values from -3 to 3
- bias_out: bfloat16 [2, 2048], P('section', ('fsdp', 'tp')), may hold values from -3 to 3
- bias_fc1: bfloat16 [2, 8192], P('section', ('fsdp', 'tp')), may hold values from -3 to 3
- bias_fc2: bfloat16 [2, 2048], P('section', ('fsdp', 'tp')), may hold values from -3 to 3
Outputs:
- ends_out: float32 [2, 2, 1024, 2048], P('section', None, ('fsdp', 'tp'))
- grad_gain: float32 [2, 2048], P('section', ('fsdp', 'tp'))
- grad_bias: float32 [2, 2048], P('section', ('fsdp', 'tp'))
- grad_qkv: float32 [2, 2048, 3, 2048], P('section', 'fsdp', None, 'tp')
- grad_out: float32 [2, 2048, 2048], P('section', 'fsdp', 'tp')
- grad_fc1: float32 [2, 2048, 8192], P('section', 'fsdp', 'tp')
- grad_fc2: float32 [2, 2048, 8192], P('section', 'fsdp', 'tp')
- grad_bias_qkv: float32 [2, 3, 2048], P('section', None, ('fsdp', 'tp'))
- grad_bias_out: float32 [2, 2048], P('section', ('fsdp', 'tp'))
- grad_bias_fc1: float32 [2, 8192], P('section', ('fsdp', 'tp'))
- grad_bias_fc2: float32 [2, 2048], P('section', ('fsdp', 'tp'))
Inputs may be any that keep to these rules, and one draw needn't show every extreme that they name: `segments`: segment ids never fall along a row; a run of equal ids is one document.
All inputs are finite; a program needn't handle non-finite values.
Results may differ from a plain program's by a relative error of at most 0.015.
Values may be sent and summed in bfloat16 or wider, within the bound.
A program may use at most 256 MiB of HBM per device.

v0:
```python
import jax
import jax.numpy as jnp
from jax import lax
from jax.sharding import PartitionSpec as P

HEAD_DIM = 64
ROT_DIM = 32


EPSILON = 1e-05


def passed_along(block, axis, distance):
    devices = range(lax.axis_size(axis))
    route = [(i - distance, i) for i in devices if i - distance in devices]
    return lax.ppermute(block, axis, route)


def positions_of(segment_ids):
    length = segment_ids.shape[-1]
    places = jnp.arange(length, dtype=jnp.int32)
    before = jnp.concatenate([segment_ids[..., :1] - 1, segment_ids[..., :-1]], axis=-1)
    starts = jnp.where(segment_ids != before, places, 0)
    starts = lax.cummax(starts, axis=segment_ids.ndim - 1)
    return places - starts


def inverse_freq(rot_dim):
    half = rot_dim // 2
    return jnp.exp(-jnp.log(10000.0) * (2.0 * jnp.arange(half, dtype=jnp.float32)) / rot_dim)


def rotate(values_in, angles, rot_dim):
    half = rot_dim // 2
    cosine = jnp.cos(angles)[..., None, :]
    sine = jnp.sin(angles)[..., None, :]
    front = values_in[..., :half]
    second = values_in[..., half:rot_dim]
    return jnp.concatenate(
        [front * cosine - second * sine, second * cosine + front * sine, values_in[..., rot_dim:]],
        axis=-1,
    )


def unrotate(values_in, angles, rot_dim):
    half = rot_dim // 2
    cosine = jnp.cos(angles)[..., None, :]
    sine = jnp.sin(angles)[..., None, :]
    front = values_in[..., :half]
    second = values_in[..., half:rot_dim]
    return jnp.concatenate(
        [front * cosine + second * sine, second * cosine - front * sine, values_in[..., rot_dim:]],
        axis=-1,
    )


def normalize(rows_in, gain_full, bias_full):
    mean = jnp.mean(rows_in, axis=-1, keepdims=True)
    centred = rows_in - mean
    variance = jnp.mean(centred * centred, axis=-1, keepdims=True)
    inv_root = lax.rsqrt(variance + EPSILON)
    unit_rows = centred * inv_root
    return (unit_rows, inv_root, unit_rows * gain_full + bias_full)


def local_forward(gathered, segment_row, weights, biases):
    qkv_w, out_w, fc1_w, fc2_w = weights
    qkv_bias_local, fc1_bias_local = biases
    length = gathered.shape[0]
    width = qkv_w.shape[0]
    local_width = qkv_w.shape[2]
    local_heads = local_width // HEAD_DIM
    contract_cols = (((1,), (1,)), ((), ()))
    joined = jnp.dot(
        gathered, qkv_w.reshape(width, 3 * local_width), preferred_element_type=jnp.float32
    )
    joined = (joined + qkv_bias_local[None, :]).reshape(length, 3, local_heads, HEAD_DIM)
    angles = positions_of(segment_row).astype(jnp.float32)[:, None] * inverse_freq(ROT_DIM)[None, :]
    query = rotate(joined[:, 0], angles, ROT_DIM).astype(jnp.bfloat16)
    keys = rotate(joined[:, 1], angles, ROT_DIM).astype(jnp.bfloat16)
    values = joined[:, 2].astype(jnp.bfloat16)
    places = jnp.arange(length, dtype=jnp.int32)
    allowed = (places[:, None] >= places[None, :]) & (segment_row[:, None] == segment_row[None, :])
    scores = jnp.einsum(
        "qhe,khe->hqk", query, keys, preferred_element_type=jnp.float32
    ) * HEAD_DIM ** (-0.5)
    scores = jnp.where(allowed[None], scores, -1e30)
    top = jnp.max(scores, axis=-1, keepdims=True)
    expo = jnp.exp(scores - top)
    softmax_w = expo / jnp.sum(expo, axis=-1, keepdims=True)
    probs = softmax_w.astype(jnp.bfloat16)
    attended = jnp.einsum("hqk,khe->qhe", probs, values, preferred_element_type=jnp.float32)
    attended = attended.astype(jnp.bfloat16).reshape(length, local_width)
    attn_part = lax.dot_general(attended, out_w, contract_cols, preferred_element_type=jnp.float32)
    upward = jnp.dot(gathered, fc1_w, preferred_element_type=jnp.float32) + fc1_bias_local[None, :]
    activated = jax.nn.gelu(upward, approximate=True).astype(jnp.bfloat16)
    mlp_part = lax.dot_general(activated, fc2_w, contract_cols, preferred_element_type=jnp.float32)
    saved = (angles, query, keys, values, softmax_w, probs, attended, upward, activated)
    return (attn_part + mlp_part, saved)


def local_backward(gathered, grad_rows, weights, saved):
    qkv_w, out_w, fc1_w, fc2_w = weights
    angles, query, keys, values, softmax_w, probs, attended, upward, activated = saved
    length = gathered.shape[0]
    width = qkv_w.shape[0]
    local_width = qkv_w.shape[2]
    local_heads = local_width // HEAD_DIM
    contract_rows = (((0,), (0,)), ((), ()))
    contract_cols = (((1,), (1,)), ((), ()))
    grad_fc2 = lax.dot_general(
        grad_rows, activated, contract_rows, preferred_element_type=jnp.float32
    )
    grad_act = jnp.dot(grad_rows, fc2_w, preferred_element_type=jnp.float32)
    gelu_back = jax.vjp(lambda value_in: jax.nn.gelu(value_in, approximate=True), upward)[1]
    grad_up = gelu_back(grad_act)[0].astype(jnp.bfloat16)
    grad_fc1 = lax.dot_general(gathered, grad_up, contract_rows, preferred_element_type=jnp.float32)
    grad_norm = lax.dot_general(grad_up, fc1_w, contract_cols, preferred_element_type=jnp.float32)
    grad_out = lax.dot_general(
        grad_rows, attended, contract_rows, preferred_element_type=jnp.float32
    )
    grad_att = jnp.dot(grad_rows, out_w, preferred_element_type=jnp.float32)
    grad_att = grad_att.astype(jnp.bfloat16).reshape(length, local_heads, HEAD_DIM)
    grad_prob = jnp.einsum("qhe,khe->hqk", grad_att, values, preferred_element_type=jnp.float32)
    grad_values = jnp.einsum("hqk,qhe->khe", probs, grad_att, preferred_element_type=jnp.float32)
    delta = jnp.sum(grad_prob * softmax_w, axis=-1, keepdims=True)
    grad_score = (softmax_w * (grad_prob - delta)).astype(jnp.bfloat16)
    factor = HEAD_DIM ** (-0.5)
    grad_query = (
        jnp.einsum("hqk,khe->qhe", grad_score, keys, preferred_element_type=jnp.float32) * factor
    )
    grad_keys = (
        jnp.einsum("hqk,qhe->khe", grad_score, query, preferred_element_type=jnp.float32) * factor
    )
    grad_joined = jnp.stack(
        [unrotate(grad_query, angles, ROT_DIM), unrotate(grad_keys, angles, ROT_DIM), grad_values],
        axis=1,
    )
    grad_joined = grad_joined.astype(jnp.bfloat16).reshape(length, 3 * local_width)
    grad_qkv = lax.dot_general(
        gathered, grad_joined, contract_rows, preferred_element_type=jnp.float32
    )
    grad_qkv = grad_qkv.reshape(width, 3, local_width)
    grad_norm = grad_norm + lax.dot_general(
        grad_joined,
        qkv_w.reshape(width, 3 * local_width),
        contract_cols,
        preferred_element_type=jnp.float32,
    )
    bias_sums = (
        jnp.sum(grad_joined.astype(jnp.float32), axis=0),
        jnp.sum(grad_up.astype(jnp.float32), axis=0),
    )
    return (grad_norm, (grad_qkv, grad_out, grad_fc1, grad_fc2), bias_sums)


def shards(
    ends_in,
    segments,
    ln_gain,
    ln_bias,
    w_qkv,
    w_out,
    w_fc1,
    w_fc2,
    bias_qkv,
    bias_out,
    bias_fc1,
    bias_fc2,
):
    section_index = lax.axis_index("section")
    tp_index = lax.axis_index("tp")
    is_first = section_index == 0
    micro_count = ends_in.shape[1]
    smalls = (
        lax.all_gather(ln_gain[0], ("fsdp", "tp"), axis=0, tiled=True),
        lax.all_gather(ln_bias[0], ("fsdp", "tp"), axis=0, tiled=True),
        lax.all_gather(bias_qkv[0], ("fsdp", "tp"), axis=1, tiled=True),
        lax.all_gather(bias_out[0], ("fsdp", "tp"), axis=0, tiled=True),
        lax.all_gather(bias_fc1[0], ("fsdp", "tp"), axis=0, tiled=True),
        lax.all_gather(bias_fc2[0], ("fsdp", "tp"), axis=0, tiled=True),
    )
    gain_full, bias_full, qkv_bias_full, out_bias_full, fc1_bias_full, fc2_bias_full = [
        member.astype(jnp.float32) for member in smalls
    ]
    local_width = w_qkv.shape[3]
    fc1_width = w_fc1.shape[2]
    qkv_bias_local = lax.dynamic_slice_in_dim(
        qkv_bias_full, tp_index * local_width, local_width, 1
    ).reshape(3 * local_width)
    fc1_bias_local = lax.dynamic_slice_in_dim(fc1_bias_full, tp_index * fc1_width, fc1_width, 0)
    row_bias = out_bias_full + fc2_bias_full
    biases = (qkv_bias_local, fc1_bias_local)
    gathered_w = (
        lax.all_gather(w_qkv, "fsdp", axis=1, tiled=True),
        lax.all_gather(w_out, "fsdp", axis=1, tiled=True),
        lax.all_gather(w_fc1, "fsdp", axis=1, tiled=True),
        lax.all_gather(w_fc2, "fsdp", axis=1, tiled=True),
    )
    weights = (gathered_w[0][0], gathered_w[1][0], gathered_w[2][0], gathered_w[3][0])
    layer_inputs = []
    kept_rows = []
    layer_outputs = []
    received = jnp.zeros(ends_in.shape[2:], jnp.bfloat16)
    sent_rows = received
    for step_no in range(micro_count + 1):
        if step_no > 0:
            received = passed_along(sent_rows, "section", 1)
        own_rows = ends_in[0, min(step_no, micro_count - 1)]
        rows_in = jnp.where(is_first, own_rows, received).astype(jnp.float32)
        micro_index = jnp.clip(step_no - section_index, 0, micro_count - 1)
        segment_row = lax.dynamic_index_in_dim(segments, micro_index, 0, keepdims=False)
        unit_rows, inv_root, normed = normalize(rows_in, gain_full, bias_full)
        gathered = lax.all_gather(normed.astype(jnp.bfloat16), "tp", axis=0, tiled=True)
        branch_part, saved = local_forward(gathered, segment_row, weights, biases)
        branch = lax.psum_scatter(branch_part, "tp", scatter_dimension=0, tiled=True) + row_bias
        layer_out = rows_in + branch
        sent_rows = layer_out.astype(jnp.bfloat16)
        layer_inputs.append(rows_in)
        kept_rows.append(gathered)
        layer_outputs.append(layer_out)
    input_stack = jnp.stack(layer_inputs)
    kept_stack = jnp.stack(kept_rows)
    accum_full = tuple((jnp.zeros(w.shape, jnp.float32) for w in weights))
    gain_accum = jnp.zeros(gain_full.shape, jnp.float32)
    bias_accum = jnp.zeros(bias_full.shape, jnp.float32)
    qkv_bias_accum = jnp.zeros((3 * local_width,), jnp.float32)
    fc1_bias_accum = jnp.zeros((fc1_width,), jnp.float32)
    row_accum = jnp.zeros(gain_full.shape, jnp.float32)
    input_grads = []
    back_recv = jnp.zeros(ends_in.shape[2:], jnp.bfloat16)
    back_sent = back_recv
    for step_no in range(micro_count + 1):
        if step_no > 0:
            back_recv = passed_along(back_sent, "section", -1)
        own_rows = ends_in[0, min(step_no, micro_count - 1)]
        upstream = jnp.where(is_first, back_recv, own_rows).astype(jnp.float32)
        micro_index = jnp.clip(jnp.where(is_first, step_no - 1, step_no), 0, micro_count - 1)
        forward_step = jnp.where(is_first, micro_index, micro_index + 1)
        valid = jnp.where(is_first, step_no >= 1, step_no < micro_count).astype(jnp.float32)
        rows_in = lax.dynamic_index_in_dim(input_stack, forward_step, 0, keepdims=False)
        gathered = lax.dynamic_index_in_dim(kept_stack, forward_step, 0, keepdims=False)
        segment_row = lax.dynamic_index_in_dim(segments, micro_index, 0, keepdims=False)
        unit_rows, inv_root, normed = normalize(rows_in, gain_full, bias_full)
        branch_part, saved = local_forward(gathered, segment_row, weights, biases)
        rounded_up = upstream.astype(jnp.bfloat16)
        grad_rows = lax.all_gather(rounded_up, "tp", axis=0, tiled=True)
        grad_norm_part, weight_grads, bias_sums = local_backward(
            gathered, grad_rows, weights, saved
        )
        grad_norm = lax.psum_scatter(
            grad_norm_part.astype(jnp.bfloat16), "tp", scatter_dimension=0, tiled=True
        ).astype(jnp.float32)
        scaled = grad_norm * gain_full
        grad_in = inv_root * (
            scaled
            - jnp.mean(scaled, axis=-1, keepdims=True)
            - unit_rows * jnp.mean(scaled * unit_rows, axis=-1, keepdims=True)
        )
        grad_total = upstream + grad_in
        back_sent = grad_total.astype(jnp.bfloat16)
        input_grads.append(grad_total)
        gain_accum = gain_accum + valid * jnp.sum(grad_norm * unit_rows, axis=0)
        bias_accum = bias_accum + valid * jnp.sum(grad_norm, axis=0)
        qkv_bias_accum = qkv_bias_accum + valid * bias_sums[0]
        fc1_bias_accum = fc1_bias_accum + valid * bias_sums[1]
        row_accum = row_accum + valid * jnp.sum(rounded_up.astype(jnp.float32), axis=0)
        accum_full = tuple(
            (total + valid * member for total, member in zip(accum_full, weight_grads))
        )
    grad_shards = (
        lax.psum_scatter(
            accum_full[0][None].astype(jnp.bfloat16), "fsdp", scatter_dimension=1, tiled=True
        ).astype(jnp.float32),
        lax.psum_scatter(
            accum_full[1][None].astype(jnp.bfloat16), "fsdp", scatter_dimension=1, tiled=True
        ).astype(jnp.float32),
        lax.psum_scatter(
            accum_full[2][None].astype(jnp.bfloat16), "fsdp", scatter_dimension=1, tiled=True
        ).astype(jnp.float32),
        lax.psum_scatter(
            accum_full[3][None].astype(jnp.bfloat16), "fsdp", scatter_dimension=1, tiled=True
        ).astype(jnp.float32),
    )
    qkv_padded = lax.dynamic_update_slice_in_dim(
        jnp.zeros(qkv_bias_full.shape, jnp.float32),
        qkv_bias_accum.reshape(3, local_width),
        tp_index * local_width,
        1,
    )
    fc1_padded = lax.dynamic_update_slice_in_dim(
        jnp.zeros(fc1_bias_full.shape, jnp.float32), fc1_bias_accum, tp_index * fc1_width, 0
    )
    gain_grad, bias_grad, qkv_bias_grad, row_grad, fc1_bias_grad = (
        lax.psum_scatter(gain_accum, ("fsdp", "tp"), scatter_dimension=0, tiled=True),
        lax.psum_scatter(bias_accum, ("fsdp", "tp"), scatter_dimension=0, tiled=True),
        lax.psum_scatter(qkv_padded, ("fsdp", "tp"), scatter_dimension=1, tiled=True),
        lax.psum_scatter(row_accum, ("fsdp", "tp"), scatter_dimension=0, tiled=True),
        lax.psum_scatter(fc1_padded, ("fsdp", "tp"), scatter_dimension=0, tiled=True),
    )
    ends_rows = [
        jnp.where(is_first, input_grads[index_no + 1], layer_outputs[index_no + 1])
        for index_no in range(micro_count)
    ]
    ends_out = jnp.stack(ends_rows)[None]
    return (
        ends_out,
        gain_grad[None],
        bias_grad[None],
        grad_shards[0],
        grad_shards[1],
        grad_shards[2],
        grad_shards[3],
        qkv_bias_grad[None],
        row_grad[None],
        fc1_bias_grad[None],
        row_grad[None],
    )


def solution(mesh):
    return jax.shard_map(
        shards,
        mesh=mesh,
        in_specs=(
            P("section", None, ("fsdp", "tp"), None),
            P(None, "fsdp"),
            P("section", ("fsdp", "tp")),
            P("section", ("fsdp", "tp")),
            P("section", "fsdp", None, "tp"),
            P("section", "fsdp", "tp"),
            P("section", "fsdp", "tp"),
            P("section", "fsdp", "tp"),
            P("section", None, ("fsdp", "tp")),
            P("section", ("fsdp", "tp")),
            P("section", ("fsdp", "tp")),
            P("section", ("fsdp", "tp")),
        ),
        out_specs=(
            P("section", None, ("fsdp", "tp"), None),
            P("section", ("fsdp", "tp")),
            P("section", ("fsdp", "tp")),
            P("section", "fsdp", None, "tp"),
            P("section", "fsdp", "tp"),
            P("section", "fsdp", "tp"),
            P("section", "fsdp", "tp"),
            P("section", None, ("fsdp", "tp")),
            P("section", ("fsdp", "tp")),
            P("section", ("fsdp", "tp")),
            P("section", ("fsdp", "tp")),
        ),
        check_vma=False,
    )
```

profile of v0, /device:TPU:0, one launch (start us, length us, event | category | flops | bytes accessed | tf_op | source)
XLA Modules:
  0.0 1131.6 jit_solution(1494660978331126918)
XLA Ops:
  7.2 34.2 %all-gather = bf16[1,2048]{1,0:T(2,128)(2,1)S(1)} all-gather(bf16[1,128]{1,0:T(2,128)(2,1)} %param.14), channel_id=2, replica_groups=mesh['section'=2,'fsdp'=4,'tp'=4] {'fsdp','tp'}, dimensions={1}, use_global_device_ids=true | all-gather | bytes 4352 | tf_op jit(solution)/shard_map/all_gather | solution.py:176
  41.4 28.7 %all-gather.1 = bf16[1,2048]{1,0:T(2,128)(2,1)S(1)} all-gather(bf16[1,128]{1,0:T(2,128)(2,1)} %param.15), channel_id=3, replica_groups=mesh['section'=2,'fsdp'=4,'tp'=4] {'fsdp','tp'}, dimensions={1}, use_global_device_ids=true | all-gather | bytes 4352 | tf_op jit(solution)/shard_map/all_gather | solution.py:177
  87.7 31.4 %all-gather.2 = bf16[1,3,2048]{2,1,0:T(4,128)(2,1)S(1)} all-gather(bf16[1,3,128]{2,1,0:T(4,128)(2,1)S(1)} %copy-done.113), channel_id=4, replica_groups=mesh['section'=2,'fsdp'=4,'tp'=4] {'fsdp','tp'}, dimensions={2}, use_global_device_ids=true | all-gather | bytes 13056 | tf_op jit(solution)/shard_map/all_gather | solution.py:178
  119.1 29.6 %all-gather.3 = bf16[1,8192]{1,0:T(2,128)(2,1)S(1)} all-gather(bf16[1,512]{1,0:T(2,128)(2,1)S(1)} %copy-done.112), channel_id=5, replica_groups=mesh['section'=2,'fsdp'=4,'tp'=4] {'fsdp','tp'}, dimensions={1}, use_global_device_ids=true | all-gather | bytes 17408 | tf_op jit(solution)/shard_map/all_gather | solution.py:180
  150.9 4.9 convolution_add_fusion.8
  161.0 49.7 %all-gather.24.cloned.1.call-done = bf16[1,2048,2048]{2,1,0:T(8,128)(2,1)} async-done(((bf16[1,512,2048]{2,1,0:T(8,128)(2,1)}), bf16[1,2048,2048]{2,1,0:T(8,128)(2,1)}) %all-gather.24.cloned.1.call-update) | async-done | bytes 8388624 | tf_op jit(solution)/shard_map/all_gather | solution.py:197
  210.7 59.7 %all-gather.26.cloned.1.call-done = bf16[1,2048,2048]{2,1,0:T(8,128)(2,1)} async-done(((bf16[1,512,2048]{2,1,0:T(8,128)(2,1)}), bf16[1,2048,2048]{2,1,0:T(8,128)(2,1)}) %all-gather.26.cloned.1.call-update) | async-done | bytes 8388624 | tf_op jit(solution)/shard_map/all_gather | solution.py:198
  270.4 10.6 fusion.16
  281.0 13.4 %all-gather.22.cloned.1.call-done = bf16[1,2048,512]{2,1,0:T(8,128)(2,1)} async-done(((bf16[1,512,512]{2,1,0:T(8,128)(2,1)}), bf16[1,2048,512]{2,1,0:T(8,128)(2,1)}) %all-gather.22.cloned.1.call-update) | async-done | bytes 2097168 | tf_op jit(solution)/shard_map/all_gather | solution.py:196
  294.4 3.7 convolution_add_fusion.2
  298.7 32.7 %all-gather.4 = bf16[1,2048]{1,0:T(2,128)(2,1)S(1)} all-gather(bf16[1,128]{1,0:T(2,128)(2,1)S(1)} %copy-done.114), channel_id=6, replica_groups=mesh['section'=2,'fsdp'=4,'tp'=4] {'fsdp','tp'}, dimensions={1}, use_global_device_ids=true | all-gather | bytes 4352 | tf_op jit(solution)/shard_map/all_gather | solution.py:179
  331.4 28.7 %all-gather.5 = bf16[1,2048]{1,0:T(2,128)(2,1)S(1)} all-gather(bf16[1,128]{1,0:T(2,128)(2,1)S(1)} %copy-done.115), channel_id=7, replica_groups=mesh['section'=2,'fsdp'=4,'tp'=4] {'fsdp','tp'}, dimensions={1}, use_global_device_ids=true | all-gather | bytes 4352 | tf_op jit(solution)/shard_map/all_gather | solution.py:181
  361.3 3.4 collective-permute-start
  364.7 3.9 collective-permute-done
  371.8 27.8 %all-gather.28.cloned.1.call-done = bf16[256,2048]{1,0:T(8,128)(2,1)} async-done(((bf16[64,2048]{1,0:T(8,128)(2,1)}), bf16[256,2048]{1,0:T(8,128)(2,1)}) %all-gather.28.cloned.1.call-update) | async-done | bytes 1048592 | tf_op jit(solution)/shard_map/all_gather | solution.py:214
  399.6 6.1 convolution_add_fusion.7
  409.7 3.2 fusion.464
  414.9 12.4 %fusion.14 = f32[256,2048]{1,0:T(8,128)} fusion(bf16[1,2048,2048]{2,1,0:T(8,128)(2,1)} %all-gather.26.cloned.1.call-done, bf16[256,2048]{1,0:T(8,128)(2,1)} %all-gather.28.cloned.1.call-done, bf16[1,2048,2048]{2,1,0:T(8,128)(2,1)} %all-gather.24.cloned.1.call-done, f32[2048]{0:T(1024)S(1)} %bitcast.595), kind=kOutput, calls=%fused_computation.17 | convolution fusion | flops 4300210176 | bytes 19931136 | tf_op jit(solution)/shard_map/dot_general | solution.py:97
  427.3 3.7 convolution_add_fusion.1
  431.0 43.1 %reduce-scatter.16.cloned.1.call-done = f32[64,2048]{1,0:T(8,128)} async-done(((f32[256,2048]{1,0:T(8,128)}), f32[64,2048]{1,0:T(8,128)}) %reduce-scatter.16.cloned.1.call-update) | async-done | bytes 524304 | tf_op jit(solution)/shard_map/reduce_scatter | solution.py:216
  475.3 3.4 collective-permute-start.1
  478.7 5.0 collective-permute-done.1
  487.2 17.9 %all-gather.36.cloned.1.call-done = bf16[1,1,256,2048]{3,2,1,0:T(8,128)(2,1)} async-done(((bf16[1,1,64,2048]{3,2,1,0:T(8,128)(2,1)}), bf16[1,1,256,2048]{3,2,1,0:T(8,128)(2,1)}) %all-gather.36.cloned.1.call-update) | async-done | bytes 1048592 | tf_op jit(solution)/shard_map/all_gather | solution.py:247
  507.9 26.6 %all-gather.30.cloned.1.call-done = bf16[256,2048]{1,0:T(8,128)(2,1)} async-done(((bf16[64,2048]{1,0:T(8,128)(2,1)}), bf16[256,2048]{1,0:T(8,128)(2,1)}) %all-gather.30.cloned.1.call-update) | async-done | bytes 1048592 | tf_op jit(solution)/shard_map/all_gather | solution.py:214
  536.7 6.9 convolution_add_fusion.6
  549.5 3.8 fusion.469
  565.9 4.3 convert_reduce_fusion.2
  571.2 3.3 fusion.73
  576.3 25.0 %reduce-scatter.18.cloned.1.call-done = bf16[64,2048]{1,0:T(8,128)(2,1)} async-done(((bf16[256,2048]{1,0:T(8,128)(2,1)}), bf16[64,2048]{1,0:T(8,128)(2,1)}) %reduce-scatter.18.cloned.1.call-update) | async-done | bytes 262160 | tf_op jit(solution)/shard_map/reduce_scatter | solution.py:251
  606.8 7.5 collective-permute-done.2
  615.8 6.1 convolution_add_fusion.5
  627.7 3.2 fusion.470
  630.9 7.4 fusion.52
  638.4 3.4 all-gather.32.cloned.1.call-done
  654.3 4.1 convert_reduce_fusion.1
  659.5 3.5 fusion.70
  664.5 6.1 convolution_add_fusion.4
  673.8 5.8 convolution_add_fusion.3
  685.1 4.7 reduce-scatter.20.cloned.1.call-done
  696.5 7.2 collective-permute-done.3
  710.1 3.7 fusion.472
  716.0 7.5 fusion.58
  723.4 7.7 all-gather.34.cloned.1.call-done
  739.7 5.9 fusion.479
  747.2 7.5 convert_reduce_fusion
  755.7 6.9 fusion.67
  765.6 12.0 %fusion.6 = f32[256,2048]{1,0:T(8,128)} fusion(bf16[1,2048,2048]{2,1,0:T(8,128)(2,1)} %all-gather.26.cloned.1.call-done, bf16[256,2048]{1,0:T(8,128)(2,1)S(1)} %copy-done.44, bf16[1,2048,2048]{2,1,0:T(8,128)(2,1)} %all-gather.24.cloned.1.call-done, f32[2048]{0:T(1024)S(1)} %bitcast.599), kind=kOutput, calls=%fused_computation.9 | convolution fusion | flops 4300210176 | bytes 19931136 | tf_op jit(solution)/shard_map/dot_general | solution.py:97
  777.6 4.4 convolution_add_fusion
  794.3 7.7 fusion.174
  802.0 6.4 fusion.172
  808.4 12.4 %fusion.38 = bf16[1,2048,3,512]{3,1,2,0:T(8,128)(2,1)} fusion(f32[2048,3,512]{2,0,1:T(8,128)} %fusion.172, f32[2048,3,512]{2,0,1:T(8,128)} %fusion.174, f32[]{:T(128)S(6)} %convert_element_type.453, f32[]{:T(128)S(6)} %convert_element_type.452, bf16[3,512,256]{2,1,0:T(8,128)(2,1)S(1)} %bitcast.528, bf16[3,256,2048]{2,1,0:T(8,128)(2,1)S(1)} %copy-done.1, ...), kind=kOutput, calls=%fused_computation.41 | convolution fusion | flops 1626341376 | bytes 33292300 | tf_op jit(solution)/shard_map/dot_general | solution.py:140
  822.1 10.0 fusion.169
  832.1 8.5 fusion.170
  840.6 16.9 %fusion.37 = bf16[1,2048,2048]{2,1,0:T(8,128)(2,1)} fusion(bf16[256,2048]{1,0:T(8,128)(2,1)S(1)} %copy-done.20, f32[]{:T(128)S(6)} %convert_element_type.453, f32[2048,2048]{1,0:T(8,128)} %fusion.170, f32[2048,2048]{1,0:T(8,128)} %fusion.169, f32[]{:T(128)S(6)} %convert_element_type.452, f32[256,2048]{1,0:T(8,128)} %fusion.58), kind=kOutput, calls=%fused_computation.40 | convolution fusion | flops 2173173760 | bytes 45088776 | tf_op jit(solution)/shard_map/dot_general | solution.py:111
  858.7 9.4 fusion.183
  868.1 9.5 fusion.179
  877.6 16.6 %fusion.36 = bf16[1,2048,2048]{2,1,0:T(8,128)(2,1)} fusion(bf16[256,2048]{1,0:T(8,128)(2,1)S(1)} %copy-done.42, f32[]{:T(128)S(6)} %convert_element_type.453, f32[2048,2048]{1,0:T(8,128)} %fusion.179, f32[2048,2048]{1,0:T(8,128)} %fusion.183, f32[]{:T(128)S(6)} %convert_element_type.452, bf16[3,256,2048]{2,1,0:T(8,128)(2,1)} %copy-done, s32[]{:T(128)S(6)} %select_n.180), kind=kOutput, calls=%fused_computation.39 | convolution fusion | flops 2168455168 | bytes 44040204 | tf_op jit(solution)/shard_map/dot_general | solution.py:117
  899.8 61.1 %all-reduce.4 = (f32[2048]{0:T(1024)S(1)}, f32[2048]{0:T(1024)S(1)}, f32[2048]{0:T(1024)S(1)}, f32[8192]{0:T(1024)S(1)}) all-reduce(f32[2048]{0:T(1024)S(1)} %multiply_add_fusion.9, f32[2048]{0:T(1024)S(1)} %multiply_add_fusion.8, ...), channel_id=15, replica_groups=mesh['section'=2,'fsdp'=4,'tp'=4] {'fsdp','tp'}, use_global_device_ids=true, to_apply=%region_54.55.clone | all-reduce | flops 14336 | bytes 114688
  967.6 4.0 reduce-scatter.26.cloned.1.call-done
  971.7 3.5 convert_element_type.456
  975.2 70.3 %reduce-scatter.32.cloned.1.call-done = bf16[1,512,2048]{2,1,0:T(8,128)(2,1)} async-done(((bf16[1,2048,2048]{2,1,0:T(8,128)(2,1)}), bf16[1,512,2048]{2,1,0:T(8,128)(2,1)}) %reduce-scatter.32.cloned.1.call-update) | async-done | bytes 2097168 | tf_op jit(solution)/shard_map/reduce_scatter | solution.py:281
  1045.5 4.1 convert_element_type.474
  1049.7 69.9 %reduce-scatter.30.cloned.1.call-done = bf16[1,512,2048]{2,1,0:T(8,128)(2,1)} async-done(((bf16[1,2048,2048]{2,1,0:T(8,128)(2,1)}), bf16[1,512,2048]{2,1,0:T(8,128)(2,1)}) %reduce-scatter.30.cloned.1.call-update) | async-done | bytes 2097168 | tf_op jit(solution)/shard_map/reduce_scatter | solution.py:278
  1119.6 4.1 convert_element_type.468
  (521 shorter events, 153.3 us)
Async XLA Ops:
  7.2 68.4 %copy-start.40 = (bf16[1,512,3,512]{3,1,2,0:T(8,128)(2,1)S(1)}, bf16[1,512,3,512]{3,1,2,0:T(8,128)(2,1)}, u32[]{:S(2)}) copy-start(bf16[1,512,3,512]{3,1,2,0:T(8,128)(2,1)} %param.16) | copy-start | bytes 4718596
  7.2 142.8 %all-gather.18.cloned.1.call-start = ((), (), s32[]{:S(2)}) async-start(), calls=%async_computation.11 | async-start | bytes 1310720 | tf_op jit(solution)/shard_map/all_gather | solution.py:214
  75.5 75.3 %all-gather.20.cloned.1.call-start = ((), (), s32[]{:S(2)}) async-start(), calls=%async_computation.12 | async-start | bytes 7864320 | tf_op jit(solution)/shard_map/all_gather | solution.py:195
  77.2 10.5 copy-start.113
  77.2 41.9 %copy-start.112 = (bf16[1,512]{1,0:T(2,128)(2,1)S(1)}, bf16[1,512]{1,0:T(2,128)(2,1)}, u32[]{:S(2)}) copy-start(bf16[1,512]{1,0:T(2,128)(2,1)} %param.22) | copy-start | bytes 3076
  77.2 133.5 %all-gather.24.cloned.1.call-start = ((), (), s32[]{:S(2)}) async-start(), calls=%async_computation.14 | async-start | bytes 10485760 | tf_op jit(solution)/shard_map/all_gather | solution.py:197
  77.9 192.4 %all-gather.26.cloned.1.call-start = ((), (), s32[]{:S(2)}) async-start(), calls=%async_computation.15 | async-start | bytes 10485760 | tf_op jit(solution)/shard_map/all_gather | solution.py:198
  78.5 215.9 %all-gather.22.cloned.1.call-start = ((), (), s32[]{:S(2)}) async-start(), calls=%async_computation.13 | async-start | bytes 2621440 | tf_op jit(solution)/shard_map/all_gather | solution.py:196
  79.1 281.0 %reduce-scatter.14.cloned.1.call-start = ((), (), s32[]{:S(2)}) async-start(), calls=%async_computation.16 | async-start | bytes 2621440 | tf_op jit(solution)/shard_map/reduce_scatter | solution.py:216
  79.8 71.1 %copy-start.84 = (s32[1,256]{1,0:T(1,128)}, s32[1,256]{1,0:T(1,128)S(1)}, u32[]{:S(2)}) copy-start(s32[1,256]{1,0:T(1,128)S(1)} %get-tuple-element.140) | copy-start | bytes 3076
  79.8 71.1 %copy-start.86 = (s32[1,256]{1,0:T(1,128)}, s32[1,256]{1,0:T(1,128)S(1)}, u32[]{:S(2)}) copy-start(s32[1,256]{1,0:T(1,128)S(1)} %get-tuple-element.145) | copy-start | bytes 3076
  79.8 71.0 %copy-start.88 = (s32[1,256]{1,0:T(1,128)}, s32[1,256]{1,0:T(1,128)S(1)}, u32[]{:S(2)}) copy-start(s32[1,256]{1,0:T(1,128)S(1)} %get-tuple-element.141) | copy-start | bytes 3076
  148.9 121.5 %copy-start.96 = (f32[1,2048]{1,0:T(1,128)}, f32[1,2048]{1,0:T(1,128)S(1)}, u32[]{:S(2)}) copy-start(f32[1,2048]{1,0:T(1,128)S(1)} %dynamic-slice_convert_fusion) | copy-start | bytes 24580
  149.9 249.6 %copy-start.102 = (f32[1536]{0:T(1024)}, f32[1536]{0:T(1024)S(1)}, u32[]{:S(2)}) copy-start(f32[1536]{0:T(1024)S(1)} %add.455) | copy-start | bytes 18436
  158.7 111.7 %copy-start.45 = (bf16[256,2048]{1,0:T(8,128)(2,1)S(1)}, bf16[256,2048]{1,0:T(8,128)(2,1)}, u32[]{:S(2)}) copy-start(bf16[256,2048]{1,0:T(8,128)(2,1)} %all-gather.18.cloned.1.call-done) | copy-start | bytes 3145732
  298.1 33.3 %copy-start.115 = (bf16[1,128]{1,0:T(2,128)(2,1)S(1)}, bf16[1,128]{1,0:T(2,128)(2,1)}, u32[]{:S(2)}) copy-start(bf16[1,128]{1,0:T(2,128)(2,1)} %param.23) | copy-start | bytes 772
  298.1 62.1 %copy-start.3 = (bf16[1,2,64,2048]{3,2,1,0:T(8,128)(2,1)S(1)}, bf16[1,2,64,2048]{3,2,1,0:T(8,128)(2,1)}, u32[]{:S(2)}) copy-start(bf16[1,2,64,2048]{3,2,1,0:T(8,128)(2,1)} %param.12) | copy-start | bytes 1572868
  298.1 101.5 %all-gather.28.cloned.1.call-start = ((), (), s32[]{:S(2)}) async-start(), calls=%async_computation.17 | async-start | bytes 1310720 | tf_op jit(solution)/shard_map/all_gather | solution.py:214
  361.3 7.3 collective-permute-start
  370.7 103.4 %reduce-scatter.16.cloned.1.call-start = ((), (), s32[]{:S(2)}) async-start(), calls=%async_computation.18 | async-start | bytes 2621440 | tf_op jit(solution)/shard_map/reduce_scatter | solution.py:216
  414.9 12.4 %copy-start.2 = (bf16[1,2048,512]{2,1,0:T(8,128)(2,1)S(1)}, bf16[1,2048,512]{2,1,0:T(8,128)(2,1)}, u32[]{:S(2)}) copy-start(bf16[1,2048,512]{2,1,0:T(8,128)(2,1)} %all-gather.22.cloned.1.call-done) | copy-start | bytes 6291460
  431.0 74.1 %all-gather.36.cloned.1.call-start = ((), (), s32[]{:S(2)}) async-start(), calls=%async_computation.30 | async-start | bytes 1310720 | tf_op jit(solution)/shard_map/all_gather | solution.py:247
  475.3 8.5 collective-permute-start.1
  478.7 55.8 %all-gather.30.cloned.1.call-start = ((), (), s32[]{:S(2)}) async-start(), calls=%async_computation.19 | async-start | bytes 1310720 | tf_op jit(solution)/shard_map/all_gather | solution.py:214
  484.6 22.4 %copy-start.15 = (bf16[64,2048]{1,0:T(8,128)(2,1)}, bf16[64,2048]{1,0:T(8,128)(2,1)S(1)}, u32[]{:S(2)}) copy-start(bf16[64,2048]{1,0:T(8,128)(2,1)S(1)} %get-tuple-element.60) | copy-start | bytes 786436
  485.9 115.4 %reduce-scatter.18.cloned.1.call-start = ((), (), s32[]{:S(2)}) async-start(), calls=%async_computation.20 | async-start | bytes 1310720 | tf_op jit(solution)/shard_map/reduce_scatter | solution.py:251
  536.7 25.5 %copy-start = (bf16[3,256,2048]{2,1,0:T(8,128)(2,1)}, bf16[3,256,2048]{2,1,0:T(8,128)(2,1)S(1)}, u32[]{:S(2)}) copy-start(bf16[3,256,2048]{2,1,0:T(8,128)(2,1)S(1)} %pad_maximum_fusion) | copy-start | bytes 9437188
  574.5 67.2 %all-gather.32.cloned.1.call-start = ((), (), s32[]{:S(2)}) async-start(), calls=%async_computation.21 | async-start | bytes 1310720 | tf_op jit(solution)/shard_map/all_gather | solution.py:247
  575.8 27.6 %copy-start.21 = (bf16[1,1,64,2048]{3,2,1,0:T(8,128)(2,1)S(1)}, bf16[1,1,64,2048]{3,2,1,0:T(8,128)(2,1)}, u32[]{:S(2)}) copy-start(bf16[1,1,64,2048]{3,2,1,0:T(8,128)(2,1)} %get-tuple-element.50) | copy-start | bytes 786436
  576.0 30.0 %copy-start.89 = (s32[1,256]{1,0:T(1,128)S(1)}, s32[1,256]{1,0:T(1,128)}, u32[]{:S(2)}) copy-start(s32[1,256]{1,0:T(1,128)} %copy-done.88) | copy-start | bytes 3076
  576.3 39.4 %copy-start.108 = (f32[64]{0:T(128)}, f32[64]{0:T(128)S(1)}, u32[]{:S(2)}) copy-start(f32[64]{0:T(128)S(1)} %broadcast_multiply_fusion.2) | copy-start | bytes 772
  576.3 39.4 %copy-start.110 = (f32[64]{0:T(128)}, f32[64]{0:T(128)S(1)}, u32[]{:S(2)}) copy-start(f32[64]{0:T(128)S(1)} %broadcast_multiply_fusion.5) | copy-start | bytes 772
  576.3 39.4 %copy-start.104 = (f32[1536]{0:T(1024)S(1)}, f32[1536]{0:T(1024)}, u32[]{:S(2)}) copy-start(f32[1536]{0:T(1024)} %copy-done.102) | copy-start | bytes 18436
  604.7 9.6 collective-permute-start.2
  615.7 74.2 %reduce-scatter.20.cloned.1.call-start = ((), (), s32[]{:S(2)}) async-start(), calls=%async_computation.22 | async-start | bytes 1310720 | tf_op jit(solution)/shard_map/reduce_scatter | solution.py:251
  630.9 17.5 %copy-start.92 = (f32[8,256]{1,0:T(8,128)}, f32[8,256]{1,0:T(8,128)S(1)}, u32[]{:S(2)}) copy-start(f32[8,256]{1,0:T(8,128)S(1)} %get-tuple-element.176) | copy-start | bytes 24580
  646.7 7.3 slice-start.10
  663.0 68.1 %all-gather.34.cloned.1.call-start = ((), (), s32[]{:S(2)}) async-start(), calls=%async_computation.23 | async-start | bytes 1310720 | tf_op jit(solution)/shard_map/all_gather | solution.py:247
  679.7 10.2 copy-start.111
  682.8 9.0 copy-start.23
  682.8 9.0 copy-start.31
  694.0 11.5 %copy-start.37 = (f32[256,8,64]{0,2,1:T(8,128)S(1)}, f32[256,8,64]{0,2,1:T(8,128)}, u32[]{:S(2)}) copy-start(f32[256,8,64]{0,2,1:T(8,128)} %get-tuple-element.64) | copy-start | bytes 1572868
  694.0 11.5 %copy-start.38 = (f32[256,8,64]{0,2,1:T(8,128)S(1)}, f32[256,8,64]{0,2,1:T(8,128)}, u32[]{:S(2)}) copy-start(f32[256,8,64]{0,2,1:T(8,128)} %get-tuple-element.63) | copy-start | bytes 1572868
  694.0 9.7 collective-permute-start.3
  705.1 191.8 %reduce-scatter.34.cloned.1.call-start = ((), (), s32[]{:S(2)}) async-start(), calls=%async_computation.31 | async-start | bytes 1114112
  716.0 21.7 %copy-start.94 = (f32[8,256]{1,0:T(8,128)}, f32[8,256]{1,0:T(8,128)S(1)}, u32[]{:S(2)}) copy-start(f32[8,256]{1,0:T(8,128)S(1)} %get-tuple-element.180) | copy-start | bytes 24580
  747.0 151.4 %reduce-scatter.22.cloned.1.call-start = ((), (), s32[]{:S(2)}) async-start(), calls=%async_computation.24 | async-start | bytes 1310720 | tf_op jit(solution)/shard_map/reduce_scatter | solution.py:251
  747.2 8.5 copy-start.32
  762.6 200.2 %reduce-scatter.24.cloned.1.call-start = ((), (), s32[]{:S(2)}) async-start(), calls=%async_computation.25 | async-start | bytes 2621440 | tf_op jit(solution)/shard_map/reduce_scatter | solution.py:216
  782.1 183.4 %reduce-scatter.28.cloned.1.call-start = ((), (), s32[]{:S(2)}) async-start(), calls=%async_computation.27 | async-start | bytes 2621440 | tf_op jit(solution)/shard_map/reduce_scatter | solution.py:275
  793.2 178.5 %reduce-scatter.26.cloned.1.call-start = ((), (), s32[]{:S(2)}) async-start(), calls=%async_computation.26 | async-start | bytes 7864320 | tf_op jit(solution)/shard_map/reduce_scatter | solution.py:272
  794.3 7.8 copy-start.1
  794.3 7.8 copy-start.8
  820.9 224.6 %reduce-scatter.32.cloned.1.call-start = ((), (), s32[]{:S(2)}) async-start(), calls=%async_computation.29 | async-start | bytes 10485760 | tf_op jit(solution)/shard_map/reduce_scatter | solution.py:281
  822.1 10.0 copy-start.14
  822.1 10.0 copy-start.36
  832.1 8.5 copy-start.20
  857.5 262.1 %reduce-scatter.30.cloned.1.call-start = ((), (), s32[]{:S(2)}) async-start(), calls=%async_computation.28 | async-start | bytes 10485760 | tf_op jit(solution)/shard_map/reduce_scatter | solution.py:278
  858.7 9.4 copy-start.49
  868.1 9.5 copy-start.42
  894.3 68.5 %copy-start.16 = (bf16[64,2048]{1,0:T(8,128)(2,1)S(1)}, bf16[64,2048]{1,0:T(8,128)(2,1)}, u32[]{:S(2)}) copy-start(bf16[64,2048]{1,0:T(8,128)(2,1)} %copy-done.15) | copy-start | bytes 786436
  894.3 68.5 %copy-start.22 = (bf16[64,2048]{1,0:T(8,128)(2,1)S(1)}, bf16[64,2048]{1,0:T(8,128)(2,1)}, u32[]{:S(2)}) copy-start(bf16[64,2048]{1,0:T(8,128)(2,1)} %get-tuple-element.54) | copy-start | bytes 786436
  894.3 70.1 %copy-start.33 = (f32[1,64,2048]{2,1,0:T(8,128)S(1)}, f32[1,64,2048]{2,1,0:T(8,128)}, u32[]{:S(2)}) copy-start(f32[1,64,2048]{2,1,0:T(8,128)} %get-tuple-element.55) | copy-start | bytes 1572868
  961.0 162.7 %copy-start.119 = (f32[1,128]{1,0:T(1,128)}, f32[1,128]{1,0:T(1,128)S(1)}, u32[]{:S(2)}) copy-start(f32[1,128]{1,0:T(1,128)S(1)} %dynamic-slice_bitcast_fusion) | copy-start | bytes 1540
  (94 other events, 233.4 us)
Sparse Core Ops, SparseCore 0:
  75.6 27.1 all-gather.17
  105.0 45.8 all-gather.19
  152.4 58.2 all-gather.23
  212.1 58.2 all-gather.25
  271.8 22.5 all-gather.21
  298.2 43.7 reduce-scatter.13
  370.8 28.7 all-gather.27
  431.1 43.0 reduce-scatter.15
  478.8 26.2 all-gather.35
  507.1 27.3 all-gather.29
  574.6 26.6 reduce-scatter.17
  615.8 25.8 all-gather.31
  663.1 26.6 reduce-scatter.19
  705.2 25.9 all-gather.33
  747.1 57.0 reduce-scatter.33
  806.9 26.2 reduce-scatter.21
  835.3 42.1 reduce-scatter.23
  880.4 30.3 reduce-scatter.27
  913.4 58.2 reduce-scatter.25
  974.1 71.3 reduce-scatter.31
  1048.1 71.4 reduce-scatter.29
where the time goes:
time: 1140 us; the launch traced here: 1130 us
  waiting for transfers between devices  450 us (39%)
  matrix products  291 us (26%)
  blocking collectives  246 us (22%)
  other arithmetic  58.9 us (5%)
  local copies, waits for them, and re-layouts  50.6 us (4%)
  between operations  21.9 us (2%)
  starting transfers between devices  12.5 us (1%)
    reduce_scatter x1, waiting for transfers between devices, shards(): lax.psum_scatter(accum_full[3][None].astype(jnp.bfloat16), 'fsdp', scatte...  70.3 us
    reduce_scatter x1, waiting for transfers between devices, shards(): lax.psum_scatter(accum_full[2][None].astype(jnp.bfloat16), 'fsdp', scatte...  69.9 us
    unnamed x1, blocking collectives  61.1 us
    all_gather x1, waiting for transfers between devices, shards(): lax.all_gather(w_fc2, 'fsdp', axis=1, tiled=True)  59.7 us
    all_gather x3, waiting for transfers between devices, shards(): lax.all_gather(normed.astype(jnp.bfloat16), 'tp', axis=0, tiled=True)  54.4 us
    all_gather x1, waiting for transfers between devices, shards(): lax.all_gather(w_fc1, 'fsdp', axis=1, tiled=True)  49.7 us
    reduce_scatter x3, waiting for transfers between devices, shards(): lax.psum_scatter(branch_part, 'tp', scatter_dimension=0, tiled=True)  43.1 us
    dot_general x6, matrix products, local_forward(): jnp.dot(gathered, qkv_w.reshape(width, 3 * local_width), preferred_elemen...  36 us
  transfers between devices with their start and end apart: 25, of which 19 were waited for; matrix products, arithmetic and copies ran while one was open for 23% of the time, Pallas kernels for 0%

commit v1 on v0

v1 whole, which is shorter than its diff:
```python
import functools

import jax
import jax.numpy as jnp
from jax import lax
from jax.experimental import pallas as pl
from jax.experimental.pallas import tpu as pltpu
from jax.sharding import PartitionSpec as P

HEAD_DIM = 64
ROT_DIM = 32
EPSILON = 1e-05
LANES = 128
TILE = 256
MESH = pl.DeviceIdType.MESH
F32 = jnp.float32
BF16 = jnp.bfloat16
COLS = (((1,), (1,)), ((), ()))
ROWS = (((0,), (0,)), ((), ()))
VMEM_LIMIT = 62 * 1024 * 1024


def positions_of(segment_ids):
    length = segment_ids.shape[-1]
    places = jnp.arange(length, dtype=jnp.int32)
    before = jnp.concatenate([segment_ids[..., :1] - 1, segment_ids[..., :-1]], axis=-1)
    starts = jnp.where(segment_ids != before, places, 0)
    starts = lax.cummax(starts, axis=segment_ids.ndim - 1)
    return places - starts


def rope_tables(segments):
    half = ROT_DIM // 2
    freq = jnp.exp(-jnp.log(10000.0) * (2.0 * jnp.arange(half, dtype=F32)) / ROT_DIM)
    angles = positions_of(segments).astype(F32)[..., None] * freq
    cosine, sine = jnp.cos(angles), jnp.sin(angles)
    none = jnp.zeros_like(sine)
    rest = jnp.zeros(angles.shape[:-1] + (HEAD_DIM - ROT_DIM,), F32)
    keep = jnp.concatenate([cosine, cosine, rest + 1.0], axis=-1)
    ahead = jnp.concatenate([-sine, none, rest], axis=-1)
    behind = jnp.concatenate([none, sine, rest], axis=-1)
    tables = jnp.stack([keep, ahead, behind], axis=1)
    return jnp.concatenate([tables, tables], axis=-1)


def send(src, dst, send_sem, recv_sem, device):
    return pltpu.make_async_remote_copy(
        src_ref=src,
        dst_ref=dst,
        send_sem=send_sem,
        recv_sem=recv_sem,
        device_id=device,
        device_id_type=MESH,
    )


def greet(peers):
    barrier = pltpu.get_barrier_semaphore()
    for peer in peers:
        pl.semaphore_signal(barrier, inc=1, device_id=peer, device_id_type=MESH)
    pl.semaphore_wait(barrier, len(peers))


def group_peers(nf, nt):
    me = lax.axis_index("fsdp") * nt + lax.axis_index("tp")
    found = []
    for k in range(1, nf * nt):
        to = lax.rem(me + k, nf * nt)
        found.append((k, to, {"fsdp": to // nt, "tp": lax.rem(to, nt)}))
    return me, found


def gather_small_kernel(nf, nt, own, out, send_sems, recv_sems, local_sem):
    me, peers = group_peers(nf, nt)
    greet([peer for _, _, peer in peers])
    mine = pltpu.make_async_copy(own, out.at[me], local_sem)
    mine.start()
    copies = []
    for k, _, peer in peers:
        copy = send(own, out.at[me], send_sems.at[k], recv_sems.at[k], peer)
        copy.start()
        copies.append(copy)
    mine.wait()
    for copy in copies:
        copy.wait()


def gather_small(own, nf, nt):
    count = nf * nt
    return pl.pallas_call(
        functools.partial(gather_small_kernel, nf, nt),
        out_shape=jax.ShapeDtypeStruct((count,) + own.shape, own.dtype),
        in_specs=[pl.BlockSpec(memory_space=pltpu.VMEM)],
        out_specs=pl.BlockSpec(memory_space=pltpu.VMEM),
        scratch_shapes=[
            pltpu.SemaphoreType.DMA((count,)),
            pltpu.SemaphoreType.DMA((count,)),
            pltpu.SemaphoreType.DMA,
        ],
        compiler_params=pltpu.CompilerParams(collective_id=0, has_side_effects=True),
        name="gather_small",
    )(own)


def sum_small_kernel(nf, nt, own, out, got, send_sems, recv_sems):
    me, peers = group_peers(nf, nt)
    greet([peer for _, _, peer in peers])
    copies = []
    for k, to, peer in peers:
        copy = send(own.at[to], got.at[k], send_sems.at[k], recv_sems.at[k], peer)
        copy.start()
        copies.append(copy)
    total = own[me]
    for k, copy in enumerate(copies):
        copy.wait()
        total = total + got[k + 1]
    out[...] = total


def sum_small(own, nf, nt):
    count = nf * nt
    return pl.pallas_call(
        functools.partial(sum_small_kernel, nf, nt),
        out_shape=jax.ShapeDtypeStruct(own.shape[1:], own.dtype),
        in_specs=[pl.BlockSpec(memory_space=pltpu.VMEM)],
        out_specs=pl.BlockSpec(memory_space=pltpu.VMEM),
        scratch_shapes=[
            pltpu.VMEM(own.shape, own.dtype),
            pltpu.SemaphoreType.DMA((count,)),
            pltpu.SemaphoreType.DMA((count,)),
        ],
        compiler_params=pltpu.CompilerParams(collective_id=1, has_side_effects=True),
        name="sum_small",
    )(own)


def cols(n, width=TILE):
    return pl.ds(pl.multiple_of(n * width, width), width)


def loop(count, body):
    def step(i, carry):
        body(i)
        return carry

    lax.fori_loop(0, count, step, 0)


def turn(x, tables, sign):
    keep, ahead, behind = tables
    left = pltpu.roll(x, LANES - ROT_DIM // 2, 1)
    right = pltpu.roll(x, ROT_DIM // 2, 1)
    return x * keep + sign * (left * ahead + right * behind)


def low_half(length):
    return lax.broadcasted_iota(jnp.int32, (length, LANES), 1) < HEAD_DIM


def allowed_mask(segc, segr, m, length):
    query = lax.broadcasted_iota(jnp.int32, (length, length), 0)
    key = lax.broadcasted_iota(jnp.int32, (length, length), 1)
    return (query >= key) & (segc[m] == segr[m])


class Ring:
    def __init__(self, nt, rows):
        self.nt, self.rows = nt, rows
        self.me = lax.axis_index("tp")
        self.others = [(k, lax.rem(self.me + k, nt)) for k in range(1, nt)]

    def block(self, who):
        return pl.ds(pl.multiple_of(who * self.rows, self.rows), self.rows)

    def gather(self, buf, m, sems):
        return [
            send(
                buf.at[m, self.block(self.me)],
                buf.at[m, self.block(self.me)],
                sems[0].at[m, k],
                sems[1].at[m, k],
                {"tp": to},
            )
            for k, to in self.others
        ]

    def scatter(self, buf, got, m, sems, part=None):
        at = slice(None) if part is None else part
        return [
            send(
                buf.at[m, self.block(to), at],
                got.at[m, k, :, at],
                sems[0].at[m, k],
                sems[1].at[m, k],
                {"tp": to},
            )
            for k, to in self.others
        ]

    def total(self, buf, got, m):
        acc = buf[m, self.block(self.me)].astype(F32)
        for k, _ in self.others:
            acc = acc + got[m, k].astype(F32)
        return acc


def stats(rows):
    mean = jnp.mean(rows, axis=-1, keepdims=True)
    centred = rows - mean
    variance = jnp.mean(centred * centred, axis=-1, keepdims=True)
    inv_root = lax.rsqrt(variance + EPSILON)
    return centred * inv_root, inv_root


def forward_kernel(
    nt,
    rows_h, wq_h, wo_h, w1_h, w2_h, vec, qb, fb, rope, segc, segr,
    rows_o, xg_o, qkv_o, lse_o, att_o, gp_o, act_o, y_o,
    wq, wo, w1, w2, rin, xg, qkv, lse, att, gp, act, branch, got, out_f, out_b,
    w_sem, in_sem, o_sem, ag_s, ag_r, rs_s, rs_r, x_s, x_r,
):
    micro, length, width = xg.shape
    section = lax.axis_index("section")
    first, second = section == 0, section == 1
    ring = Ring(nt, length // nt)
    own = wo.shape[1]
    loads = []
    for i, (src, dst) in enumerate(((wq_h, wq), (w1_h, w1), (wo_h, wo), (w2_h, w2))):
        loads.append(pltpu.make_async_copy(src, dst, w_sem.at[i]))
        loads[-1].start()
    mine = pltpu.make_async_copy(rows_h, rin, in_sem)

    @pl.when(first)
    def _():
        mine.start()

    greet([{"tp": to} for _, to in ring.others] + [{"section": 1 - section}])

    @pl.when(first)
    def _():
        mine.wait()

    def hop(m):
        return send(out_b.at[m], rin.at[m], x_s.at[m], x_r.at[m], {"section": 1 - section})

    def front(m):
        unit, _ = stats(rin[m].astype(F32))
        normed = unit * vec[0:1, :] + vec[1:2, :]
        xg[m, ring.block(ring.me)] = normed.astype(BF16)
        for copy in ring.gather(xg, m, (ag_s, ag_r)):
            copy.start()

    def arrive(m):
        @pl.when(second)
        def _():
            hop(m).wait_recv()
            front(m)

    stores = []

    def store(src, dst, m, i):
        copy = pltpu.make_async_copy(src.at[m], dst.at[m], o_sem.at[m, i])
        copy.start()
        stores.append(copy)

    def body(m):
        for copy in ring.gather(xg, m, (ag_s, ag_r)):
            copy.wait()
        store(xg, xg_o, m, 0)
        store(rin, rows_o, m, 1)
        tables = (rope[m, 0], rope[m, 1], rope[m, 2])
        if m == 0:
            loads[0].wait()
        per = own // TILE
        for part in range(3):
            def qkv_tile(n, part=part):
                at = cols(n)
                acc = jnp.dot(xg[m], wq[part, :, at], preferred_element_type=F32)
                acc = acc + qb[part:part + 1, at]
                if part < 2:
                    acc = jnp.concatenate(
                        [
                            turn(acc[:, c:c + LANES], tables, 1.0)
                            for c in range(0, TILE, LANES)
                        ],
                        axis=1,
                    )
                qkv[m, part, :, at] = acc.astype(BF16)

            loop(per, qkv_tile)
        store(qkv, qkv_o, m, 2)
        allowed = allowed_mask(segc, segr, m, length)
        low = low_half(length)
        lane = lax.broadcasted_iota(jnp.int32, (length, LANES), 1)

        def pair(p):
            at = cols(p, LANES)
            query, key, value = qkv[m, 0, :, at], qkv[m, 1, :, at], qkv[m, 2, :, at]
            outs = []
            for h in range(2):
                mask = low if h == 0 else ~low
                one = jnp.where(mask, query, jnp.zeros_like(query))
                s = lax.dot_general(one, key, COLS, preferred_element_type=F32)
                s = jnp.where(allowed, s * HEAD_DIM ** (-0.5), -1e30)
                top = jnp.max(s, axis=-1, keepdims=True)
                e = jnp.exp(s - top)
                total = jnp.sum(e, axis=-1, keepdims=True)
                probs = (e / total).astype(BF16)
                outs.append(jnp.dot(probs, value, preferred_element_type=F32))
                lse[m] = jnp.where(lane == 2 * p + h, top + jnp.log(total), lse[m])
            att[m, :, at] = jnp.where(low, outs[0], outs[1]).astype(BF16)

        lse[m] = jnp.zeros((length, LANES), F32)
        loop(own // LANES, pair)
        store(lse, lse_o, m, 3)
        store(att, att_o, m, 4)
        if m == 0:
            loads[1].wait()

        def up_tile(n):
            at = cols(n)
            u = jnp.dot(xg[m], w1[:, at], preferred_element_type=F32) + fb[0:1, at]
            c = 0.7978845608028654
            square = u * u
            t = jnp.tanh(c * u * (1.0 + 0.044715 * square))
            act[m, :, at] = (0.5 * u * (1.0 + t)).astype(BF16)
            slope = 0.5 * (1.0 + t) + 0.5 * u * (1.0 - t * t) * (c * (1.0 + 3 * 0.044715 * square))
            gp[m, :, at] = slope.astype(BF16)

        loop(act.shape[2] // TILE, up_tile)
        store(act, act_o, m, 5)
        store(gp, gp_o, m, 6)
        if m == 0:
            loads[2].wait()
            loads[3].wait()

        def out_tile(n):
            at = cols(n)
            acc = lax.dot_general(att[m], wo[at, :], COLS, preferred_element_type=F32)
            acc = acc + lax.dot_general(act[m], w2[at, :], COLS, preferred_element_type=F32)
            branch[m, :, at] = acc.astype(BF16)
            for copy in ring.scatter(branch, got, m, (rs_s, rs_r), at):
                copy.start()

        loop(width // TILE, out_tile)

    def finish(m):
        for copy in ring.scatter(branch, got, m, (rs_s, rs_r)):
            copy.wait()
        y = rin[m].astype(F32) + ring.total(branch, got, m) + vec[2:3, :]
        out_f[m] = y
        out_b[m] = y.astype(BF16)
        store(out_f, y_o, m, 7)

        @pl.when(first)
        def _():
            hop(m).start()

    @pl.when(first)
    def _():
        for m in range(micro):
            front(m)

    for m in range(micro):
        arrive(m)
        body(m)
    for m in range(micro):
        finish(m)
    for copy in stores:
        copy.wait()

    @pl.when(first)
    def _():
        for m in range(micro):
            hop(m).wait_send()


def forward(rows, weights, vec, qb, fb, rope, segc, segr, nt):
    wq, wo, w1, w2 = weights
    micro, per, width = rows.shape
    length = per * nt
    own, hidden = wo.shape[1], w1.shape[1]
    anywhere = pl.BlockSpec(memory_space=pl.ANY)
    inside = pl.BlockSpec(memory_space=pltpu.VMEM)
    out_shape = [
        jax.ShapeDtypeStruct(rows.shape, BF16),
        jax.ShapeDtypeStruct((micro, length, width), BF16),
        jax.ShapeDtypeStruct((micro, 3, length, own), BF16),
        jax.ShapeDtypeStruct((micro, length, LANES), F32),
        jax.ShapeDtypeStruct((micro, length, own), BF16),
        jax.ShapeDtypeStruct((micro, length, hidden), BF16),
        jax.ShapeDtypeStruct((micro, length, hidden), BF16),
        jax.ShapeDtypeStruct(rows.shape, F32),
    ]
    dma = pltpu.SemaphoreType.DMA
    return pl.pallas_call(
        functools.partial(forward_kernel, nt),
        out_shape=out_shape,
        in_specs=[anywhere] * 5 + [inside] * 6,
        out_specs=[anywhere] * 8,
        scratch_shapes=[
            pltpu.VMEM(wq.shape, BF16),
            pltpu.VMEM(wo.shape, BF16),
            pltpu.VMEM(w1.shape, BF16),
            pltpu.VMEM(w2.shape, BF16),
            pltpu.VMEM(rows.shape, BF16),
            pltpu.VMEM((micro, length, width), BF16),
            pltpu.VMEM((micro, 3, length, own), BF16),
            pltpu.VMEM((micro, length, LANES), F32),
            pltpu.VMEM((micro, length, own), BF16),
            pltpu.VMEM((micro, length, hidden), BF16),
            pltpu.VMEM((micro, length, hidden), BF16),
            pltpu.VMEM((micro, length, width), BF16),
            pltpu.VMEM((micro, nt, per, width), BF16),
            pltpu.VMEM(rows.shape, F32),
            pltpu.VMEM(rows.shape, BF16),
            dma((4,)),
            dma,
            dma((micro, 8)),
            dma((micro, nt)),
            dma((micro, nt)),
            dma((micro, nt)),
            dma((micro, nt)),
            dma((micro,)),
            dma((micro,)),
        ],
        compiler_params=pltpu.CompilerParams(
            collective_id=2, has_side_effects=True, vmem_limit_bytes=VMEM_LIMIT
        ),
        name="forward",
    )(rows, wq, wo, w1, w2, vec, qb, fb, rope, segc, segr)


def backward_kernel(
    nt,
    dy_h, wq_h, wo_h, w1_h, w2_h, rows_h, qkv_h, lse_h, gp_h, vec, rope, segc, segr,
    gr_o, up_o, dj_o, dx_o, own_sums, head_sums, up_sums,
    wq, wo, w1, w2, dyr, rin, qkv, lse, gp, gr, gatt, up, dj, branch, got, out_f, out_b,
    w_sem, in_sem, o_sem, ag_s, ag_r, rs_s, rs_r, x_s, x_r,
):
    micro, length, width = gr.shape
    section = lax.axis_index("section")
    first, second = section == 0, section == 1
    ring = Ring(nt, length // nt)
    own = wo.shape[1]
    mine = pltpu.make_async_copy(dy_h, dyr, in_sem.at[4])

    @pl.when(second)
    def _():
        mine.start()

    loads = []
    for i, (src, dst) in enumerate(((wo_h, wo), (w2_h, w2), (wq_h, wq), (w1_h, w1))):
        loads.append(pltpu.make_async_copy(src, dst, w_sem.at[i]))
    kept = []
    for i, (src, dst) in enumerate(((qkv_h, qkv), (lse_h, lse), (gp_h, gp), (rows_h, rin))):
        kept.append(pltpu.make_async_copy(src, dst, in_sem.at[i]))
    for copy in (loads[0], kept[0], kept[1], loads[1], kept[2], loads[2], loads[3], kept[3]):
        copy.start()
    greet([{"tp": to} for _, to in ring.others] + [{"section": 1 - section}])

    @pl.when(second)
    def _():
        mine.wait()

    def hop(m):
        return send(out_b.at[m], dyr.at[m], x_s.at[m], x_r.at[m], {"section": 1 - section})

    def front(m):
        gr[m, ring.block(ring.me)] = dyr[m]
        for copy in ring.gather(gr, m, (ag_s, ag_r)):
            copy.start()

    def arrive(m):
        @pl.when(first)
        def _():
            hop(m).wait_recv()
            front(m)

    stores = []

    def store(src, dst, m, i):
        copy = pltpu.make_async_copy(src.at[m], dst.at[m], o_sem.at[m, i])
        copy.start()
        stores.append(copy)

    def body(m):
        for copy in ring.gather(gr, m, (ag_s, ag_r)):
            copy.wait()
        store(gr, gr_o, m, 0)
        if m == 0:
            loads[0].wait()

        def att_tile(n):
            at = cols(n)
            gatt[:, at] = jnp.dot(gr[m], wo[:, at], preferred_element_type=F32).astype(BF16)

        loop(own // TILE, att_tile)
        if m == 0:
            kept[0].wait()
            kept[1].wait()
        tables = (rope[m, 0], rope[m, 1], rope[m, 2])
        allowed = allowed_mask(segc, segr, m, length)
        low = low_half(length)
        lane = lax.broadcasted_iota(jnp.int32, (length, LANES), 1)
        factor = HEAD_DIM ** (-0.5)

        def pair(p):
            at = cols(p, LANES)
            query, key, value = qkv[m, 0, :, at], qkv[m, 1, :, at], qkv[m, 2, :, at]
            grad = gatt[:, at]
            dqs, dks, dvs = [], [], []
            for h in range(2):
                mask = low if h == 0 else ~low
                one = jnp.where(mask, query, jnp.zeros_like(query))
                s = lax.dot_general(one, key, COLS, preferred_element_type=F32)
                s = jnp.where(allowed, s * factor, -1e30)
                log_total = jnp.sum(
                    jnp.where(lane == 2 * p + h, lse[m], 0.0), axis=-1, keepdims=True
                )
                soft = jnp.exp(s - log_total)
                probs = soft.astype(BF16)
                one_grad = jnp.where(mask, grad, jnp.zeros_like(grad))
                dp = lax.dot_general(one_grad, value, COLS, preferred_element_type=F32)
                delta = jnp.sum(dp * soft, axis=-1, keepdims=True)
                ds = (soft * (dp - delta)).astype(BF16)
                dvs.append(lax.dot_general(probs, grad, ROWS, preferred_element_type=F32))
                dqs.append(jnp.dot(ds, key, preferred_element_type=F32))
                dks.append(lax.dot_general(ds, query, ROWS, preferred_element_type=F32))
            dq = jnp.where(low, dqs[0], dqs[1]) * factor
            dk = jnp.where(low, dks[0], dks[1]) * factor
            dj[m, 0, :, at] = turn(dq, tables, -1.0).astype(BF16)
            dj[m, 1, :, at] = turn(dk, tables, -1.0).astype(BF16)
            dj[m, 2, :, at] = jnp.where(low, dvs[0], dvs[1]).astype(BF16)

        loop(own // LANES, pair)
        store(dj, dj_o, m, 1)
        for part in range(3):
            sums = jnp.sum(dj[m, part].astype(F32), axis=0, keepdims=True)
            if m == 0:
                head_sums[part:part + 1, :] = sums
            else:
                head_sums[part:part + 1, :] += sums
        if m == 0:
            loads[1].wait()
            kept[2].wait()

        def up_tile(n):
            at = cols(n)
            acc = jnp.dot(gr[m], w2[:, at], preferred_element_type=F32)
            rounded = (acc * gp[m, :, at].astype(F32)).astype(BF16)
            up[m, :, at] = rounded
            sums = jnp.sum(rounded.astype(F32), axis=0, keepdims=True)
            if m == 0:
                up_sums[0:1, at] = sums
            else:
                up_sums[0:1, at] += sums

        loop(up.shape[2] // TILE, up_tile)
        store(up, up_o, m, 2)
        if m == 0:
            loads[2].wait()
            loads[3].wait()

        def norm_tile(n):
            at = cols(n)
            acc = lax.dot_general(up[m], w1[at, :], COLS, preferred_element_type=F32)
            for part in range(3):
                acc = acc + lax.dot_general(
                    dj[m, part], wq[part, at, :], COLS, preferred_element_type=F32
                )
            branch[m, :, at] = acc.astype(BF16)
            for copy in ring.scatter(branch, got, m, (rs_s, rs_r), at):
                copy.start()

        loop(width // TILE, norm_tile)

    def finish(m):
        for copy in ring.scatter(branch, got, m, (rs_s, rs_r)):
            copy.wait()
        if m == 0:
            kept[3].wait()
        grad_norm = ring.total(branch, got, m)
        unit, inv_root = stats(rin[m].astype(F32))
        scaled = grad_norm * vec[0:1, :]
        upstream = dyr[m].astype(F32)
        dx = upstream + inv_root * (
            scaled
            - jnp.mean(scaled, axis=-1, keepdims=True)
            - unit * jnp.mean(scaled * unit, axis=-1, keepdims=True)
        )
        out_f[m] = dx
        out_b[m] = dx.astype(BF16)

        @pl.when(second)
        def _():
            hop(m).start()

        store(out_f, dx_o, m, 3)
        for i, term in enumerate((grad_norm * unit, grad_norm, upstream)):
            sums = jnp.sum(term, axis=0, keepdims=True)
            if m == 0:
                own_sums[i:i + 1, :] = sums
            else:
                own_sums[i:i + 1, :] += sums

    @pl.when(second)
    def _():
        for m in range(micro):
            front(m)

    for m in range(micro):
        arrive(m)
        body(m)
    for m in range(micro):
        finish(m)
    for copy in stores:
        copy.wait()

    @pl.when(second)
    def _():
        for m in range(micro):
            hop(m).wait_send()


def backward(dy, weights, rows, qkv, lse, gp, vec, rope, segc, segr, nt):
    wq, wo, w1, w2 = weights
    micro, per, width = rows.shape
    length = per * nt
    own, hidden = wo.shape[1], w1.shape[1]
    anywhere = pl.BlockSpec(memory_space=pl.ANY)
    inside = pl.BlockSpec(memory_space=pltpu.VMEM)
    out_shape = [
        jax.ShapeDtypeStruct((micro, length, width), BF16),
        jax.ShapeDtypeStruct((micro, length, hidden), BF16),
        jax.ShapeDtypeStruct((micro, 3, length, own), BF16),
        jax.ShapeDtypeStruct(rows.shape, F32),
        jax.ShapeDtypeStruct((8, width), F32),
        jax.ShapeDtypeStruct((8, own), F32),
        jax.ShapeDtypeStruct((8, hidden), F32),
    ]
    dma = pltpu.SemaphoreType.DMA
    return pl.pallas_call(
        functools.partial(backward_kernel, nt),
        out_shape=out_shape,
        in_specs=[anywhere] * 9 + [inside] * 4,
        out_specs=[anywhere] * 4 + [inside] * 3,
        scratch_shapes=[
            pltpu.VMEM(wq.shape, BF16),
            pltpu.VMEM(wo.shape, BF16),
            pltpu.VMEM(w1.shape, BF16),
            pltpu.VMEM(w2.shape, BF16),
            pltpu.VMEM(rows.shape, BF16),
            pltpu.VMEM(rows.shape, BF16),
            pltpu.VMEM(qkv.shape, BF16),
            pltpu.VMEM(lse.shape, F32),
            pltpu.VMEM(gp.shape, BF16),
            pltpu.VMEM((micro, length, width), BF16),
            pltpu.VMEM((length, own), BF16),
            pltpu.VMEM((micro, length, hidden), BF16),
            pltpu.VMEM((micro, 3, length, own), BF16),
            pltpu.VMEM((micro, length, width), BF16),
            pltpu.VMEM((micro, nt, per, width), BF16),
            pltpu.VMEM(rows.shape, F32),
            pltpu.VMEM(rows.shape, BF16),
            dma((4,)),
            dma((5,)),
            dma((micro, 4)),
            dma((micro, nt)),
            dma((micro, nt)),
            dma((micro, nt)),
            dma((micro, nt)),
            dma((micro,)),
            dma((micro,)),
        ],
        compiler_params=pltpu.CompilerParams(
            collective_id=3, has_side_effects=True, vmem_limit_bytes=VMEM_LIMIT
        ),
        name="backward",
    )(dy, wq, wo, w1, w2, rows, qkv, lse, gp, vec, rope, segc, segr)


def padded(flat):
    size = -(-flat.shape[-1] // (8 * LANES)) * (8 * LANES)
    room = [(0, 0)] * (flat.ndim - 1) + [(0, size - flat.shape[-1])]
    flat = jnp.pad(flat, room)
    return flat.reshape(flat.shape[:-1] + (size // LANES, LANES))


def shards(
    ends_in, segments, ln_gain, ln_bias, w_qkv, w_out, w_fc1, w_fc2,
    bias_qkv, bias_out, bias_fc1, bias_fc2,
):
    nf, nt = lax.axis_size("fsdp"), lax.axis_size("tp")
    count = nf * nt
    section, tp_index = lax.axis_index("section"), lax.axis_index("tp")
    is_first = section == 0
    piece = ln_gain.shape[1]
    hidden_piece = bias_fc1.shape[1]
    own, hidden = w_out.shape[2], w_fc1.shape[2]
    width = piece * count

    pack = jnp.concatenate(
        [ln_gain[0], ln_bias[0], bias_out[0], bias_fc2[0], bias_qkv[0].reshape(-1), bias_fc1[0]]
    ).astype(F32)
    used = pack.shape[0]
    smalls = gather_small(padded(pack), nf, nt).reshape(count, -1)[:, :used]
    wide = smalls[:, :7 * piece].reshape(count, 7, piece).transpose(1, 0, 2).reshape(7, width)
    vec = jnp.stack([wide[0], wide[1], wide[2] + wide[3]])
    vec = jnp.pad(vec, ((0, 5), (0, 0)))
    qb = lax.dynamic_slice_in_dim(wide[4:7], tp_index * own, own, 1)
    qb = jnp.pad(qb, ((0, 5), (0, 0)))
    fb = lax.dynamic_slice_in_dim(smalls[:, 7 * piece:], tp_index * nf, nf, 0).reshape(1, hidden)
    fb = jnp.pad(fb, ((0, 7), (0, 0)))
    rope = rope_tables(segments)
    segc, segr = segments[:, :, None], segments[:, None, :]

    wq = lax.all_gather(w_qkv[0].transpose(1, 0, 2), "fsdp", axis=1, tiled=True)
    w1 = lax.all_gather(w_fc1[0], "fsdp", axis=0, tiled=True)
    wo = lax.all_gather(w_out[0], "fsdp", axis=0, tiled=True)
    w2 = lax.all_gather(w_fc2[0], "fsdp", axis=0, tiled=True)
    weights = (wq, wo, w1, w2)
    rows, xg, qkv, lse, att, gp, act, y = forward(
        ends_in[0], weights, vec, qb, fb, rope, segc, segr, nt
    )
    gr, up, dj, dx, own_sums, head_sums, up_sums = backward(
        ends_in[0], weights, rows, qkv, lse, gp, vec, rope, segc, segr, nt
    )

    def everywhere(arr):
        return lax.all_gather(arr, "fsdp", axis=arr.ndim - 2, tiled=True)

    def columns(arr):
        return lax.all_to_all(arr, "fsdp", split_axis=2, concat_axis=1, tiled=True)

    xc, gc = columns(xg), columns(gr)

    def product(left, right):
        return lax.dot_general(
            left, right, (((0, 1), (0, 1)), ((), ())), preferred_element_type=F32
        )

    act_all, att_all, up_all, dj_all = (everywhere(a) for a in (act, att, up, dj))
    grad_fc2 = product(gc, act_all)
    grad_out = product(gc, att_all)
    grad_fc1 = product(xc, up_all)
    grad_qkv = jnp.stack([product(xc, dj_all[:, part]) for part in range(3)], axis=1)

    mine = own_sums[:3].reshape(3, count, piece).transpose(1, 0, 2).reshape(count, 3 * piece)
    head = lax.dynamic_update_slice_in_dim(
        jnp.zeros((3, width), F32), head_sums[:3], tp_index * own, 1
    )
    head = head.reshape(3, count, piece).transpose(1, 0, 2).reshape(count, 3 * piece)
    ups = lax.dynamic_update_slice_in_dim(
        jnp.zeros((count, hidden_piece), F32),
        up_sums[0].reshape(nf, hidden_piece),
        tp_index * nf,
        0,
    )
    sums = sum_small(padded(jnp.concatenate([mine, head, ups], axis=1)), nf, nt).reshape(-1)
    gain_grad, bias_grad, row_grad = (sums[i * piece:(i + 1) * piece] for i in range(3))
    qkv_bias_grad = sums[3 * piece:6 * piece].reshape(3, piece)
    fc1_bias_grad = sums[6 * piece:6 * piece + hidden_piece]
    ends_out = jnp.where(is_first, dx, y)[None]
    return (
        ends_out,
        gain_grad[None],
        bias_grad[None],
        grad_qkv[None],
        grad_out[None],
        grad_fc1[None],
        grad_fc2[None],
        qkv_bias_grad[None],
        row_grad[None],
        fc1_bias_grad[None],
        row_grad[None],
    )


def solution(mesh):
    both = P("section", ("fsdp", "tp"))
    square = P("section", "fsdp", "tp")
    tokens = P("section", None, ("fsdp", "tp"), None)
    heads = P("section", "fsdp", None, "tp")
    bias3 = P("section", None, ("fsdp", "tp"))
    return jax.shard_map(
        shards,
        mesh=mesh,
        in_specs=(
            tokens, P(None, "fsdp"), both, both, heads, square, square, square,
            bias3, both, both, both,
        ),
        out_specs=(
            tokens, both, both, heads, square, square, square, bias3, both, both, both,
        ),
        check_vma=False,
    )
```

time: 1140 us -> 824 us (0.72)
  Pallas kernels: 0 us -> 458 us
  matrix products: 291 us -> 30 us
  blocking collectives: 246 us -> 0 us
  waiting for transfers between devices: 450 us -> 268 us
  other arithmetic: 58.9 us -> 9.05 us
  local copies, waits for them, and re-layouts: 50.6 us -> 35.3 us
    pallas_call x0 -> x4, Pallas kernels: none -> 458 us  [the longest x1 300 us: backward(): pl.pallas_call(functools.partial(backward_kernel, nt), out_shape=out_shap...]
    dot_general x57 -> x6, matrix products: 273 us -> 30 us  [product(): lax.dot_general(left, right, (((0, 1), (0, 1)), ((), ())), preferred_elem...]
    reduce_scatter x10 -> x0, waiting for transfers between devices: 217 us -> none  [the longest x1 70.3 us: shards(): lax.psum_scatter(accum_full[3][None].astype(jnp.bfloat16), 'fsdp', scatte...]
    all_gather x6 -> x0, blocking collectives: 185 us -> none  [the longest x1 34.2 us: shards(): lax.all_gather(ln_gain[0], ('fsdp', 'tp'), axis=0, tiled=True)]
    unnamed x1 -> x0, blocking collectives: 61.1 us -> none
    all_to_all x0 -> x2, waiting for transfers between devices: none -> 41.5 us  [columns(): return lax.all_to_all(arr, 'fsdp', split_axis=2, concat_axis=1, tiled=True)]
    ppermute x4 -> x0, waiting for transfers between devices: 23.6 us -> none  [passed_along(): return lax.ppermute(block, axis, route)]
    convert_element_type x24 -> x1, other arithmetic: 22.7 us -> 0.01 us  [rope_tables(): angles = positions_of(segments).astype(F32)[..., None] * freq]
  transfers between devices with their start and end apart: 25 -> 10, of which waited for: 19 -> 7; matrix products, arithmetic and copies ran while one was open for 23% -> 7% of each run, Pallas kernels for 0% -> 42%
where the time goes in v1:
time: 824 us; the launch traced here: 823 us
  Pallas kernels  458 us (56%)
  waiting for transfers between devices  268 us (33%)
  local copies, waits for them, and re-layouts  35.3 us (4%)
  matrix products  30 us (4%)
  between operations  14.5 us (2%)
  other arithmetic  9.05 us (1%)
  starting transfers between devices  8.67 us (1%)
    pallas_call x1, Pallas kernels, backward(): pl.pallas_call(functools.partial(backward_kernel, nt), out_shape=out_shap...  300 us
    pallas_call x1, Pallas kernels, forward(): pl.pallas_call(functools.partial(forward_kernel, nt), out_shape=out_shape...  109 us
    all_gather x1, waiting for transfers between devices, shards(): w1 = lax.all_gather(w_fc1[0], 'fsdp', axis=0, tiled=True)  59.9 us
    all_gather x1, waiting for transfers between devices, shards(): w2 = lax.all_gather(w_fc2[0], 'fsdp', axis=0, tiled=True)  59.7 us
    all_gather x4, waiting for transfers between devices, everywhere(): return lax.all_gather(arr, 'fsdp', axis=arr.ndim - 2, tiled=True)  51.8 us
    all_gather x1, waiting for transfers between devices, shards(): wq = lax.all_gather(w_qkv[0].transpose(1, 0, 2), 'fsdp', axis=1, tiled=True)  48.1 us
    all_to_all x2, waiting for transfers between devices, columns(): return lax.all_to_all(arr, 'fsdp', split_axis=2, concat_axis=1, tiled=True)  41.5 us
    pallas_call x1, Pallas kernels, sum_small(): pl.pallas_call(functools.partial(sum_small_kernel, nf, nt), out_shape=jax...  37.1 us
  transfers between devices with their start and end apart: 10, of which 7 were waited for; matrix products, arithmetic and copies ran while one was open for 7% of the time, Pallas kernels for 42%

profile of v1, /device:TPU:0, one launch (start us, length us, event | category | flops | bytes accessed | tf_op | source)
XLA Modules:
  0.0 823.3 jit_solution(18066995235244299847)
XLA Ops:
  7.2 0.7 all-gather.22.cloned.1.call-update
  8.0 0.7 all-gather.12.cloned.1.call-update
  8.8 0.7 all-gather.24.cloned.1.call-update
  9.5 0.5 all-gather.26.cloned.1.call-update
  10.1 0.2 dynamic-update-slice
  10.4 0.2 dynamic-update-slice.1
  10.6 0.2 dynamic-update-slice.2
  10.8 0.2 dynamic-update-slice.3
  11.1 0.2 dynamic-update-slice.4
  11.3 0.2 dynamic-update-slice.5
  11.5 0.6 bitcast_convert_fusion.own
  12.1 11.9 %gather_small.1 = f32[16,16,128]{2,1,0:T(8,128)} custom-call(f32[16,128]{1,0:T(8,128)} %bitcast_convert_fusion.own), custom_call_target="tpu_custom_call" | custom-call | tf_op jit(solution)/shard_map/gather_small/pallas_call | solution.py:90
  24.0 0.9 copy.58
  25.0 0.6 broadcast_in_dim.56.segr
  25.6 0.1 compare_select_fusion
  25.7 0.6 reduce-window.6
  26.3 0.2 slice_reduce_fusion.1
  26.5 0.2 reduce-window.9
  26.7 0.1 pad.43.clone
  26.9 0.6 pad.23.qb
  27.6 0.6 pad.24.fb
  28.2 0.9 copy.36.segc
  29.1 1.0 multiply_cosine_fusion
  30.1 0.1 maximum_bitcast_fusion.1
  30.3 0.2 maximum_bitcast_fusion.2
  30.5 1.2 maximum_maximum_fusion.rope
  31.7 0.7 select_maximum_fusion.2.vec
  32.4 2.7 all-gather.22.cloned.1.call-done
  35.0 48.1 %all-gather.12.cloned.1.call-done.wq_h = bf16[3,2048,512]{2,1,0:T(8,128)(2,1)} async-done(((bf16[3,512,512]{2,1,0:T(8,128)(2,1)}), bf16[3,2048,512]{2,1,0:T(8,128)(2,1)}) %all-gather.12.cloned.1.call-update) | async-done | bytes 6291472 | tf_op jit(solution)/shard_map/all_gather | solution.py:718
  83.1 59.9 %all-gather.24.cloned.1.call-done = bf16[1,2048,2048]{2,1,0:T(8,128)(2,1)} async-done(((bf16[1,512,2048]{2,1,0:T(8,128)(2,1)}), bf16[1,2048,2048]{2,1,0:T(8,128)(2,1)}) %all-gather.24.cloned.1.call-update) | async-done | bytes 8388624 | tf_op jit(solution)/shard_map/all_gather | solution.py:719
  143.0 59.7 %all-gather.26.cloned.1.call-done = bf16[1,2048,2048]{2,1,0:T(8,128)(2,1)} async-done(((bf16[1,512,2048]{2,1,0:T(8,128)(2,1)}), bf16[1,2048,2048]{2,1,0:T(8,128)(2,1)}) %all-gather.26.cloned.1.call-update) | async-done | bytes 8388624 | tf_op jit(solution)/shard_map/all_gather | solution.py:721
  202.7 108.6 %forward.1 = (bf16[2,64,2048]{2,1,0:T(8,128)(2,1)}, bf16[2,256,2048]{2,1,0:T(8,128)(2,1)}, bf16[2,3,256,512]{3,2,1,0:T(8,128)(2,1)}, f32[2,256,128]{2,1,0:T(8,12...) custom-call(bf16[2,64,2048]{2,1,0:T(8,128)(2,1)} %bitcast.134, ...), custom_call_target="tpu_custom_call" | custom-call | tf_op jit(solution)/shard_map/forward/pallas_call | solution.py:396
  311.4 300.5 %backward.1 = (bf16[2,256,2048]{2,1,0:T(8,128)(2,1)}, bf16[2,256,2048]{2,1,0:T(8,128)(2,1)}, bf16[2,3,256,512]{3,2,1,0:T(8,128)(2,1)}, f32[2,64,2048]{2,1,0:T(8,...) custom-call(bf16[2,64,2048]{2,1,0:T(8,128)(2,1)} %bitcast.135, ...), custom_call_target="tpu_custom_call" | custom-call | tf_op jit(solution)/shard_map/backward/pallas_call | solution.py:643
  612.0 0.7 all-gather.20.cloned.1.call-update
  612.7 0.7 all-gather.18.cloned.1.call-update
  613.4 0.1 copy-done
  613.6 3.8 copy.41
  617.4 3.7 all-to-all-start.1
  621.1 6.1 copy.39
  627.2 0.9 slice_reduce_fusion
  628.1 41.5 %all-to-all-done.1 = bf16[2,256,2048]{1,0,2:T(2,128)(2,1)S(1)} async-done(((bf16[2,256,2048]{1,0,2:T(2,128)(2,1)}), bf16[2,256,2048]{1,0,2:T(2,128)(2,1)S(1)}, u32[]{:S(2)}, u32[]{:S(2)}) %all-to-all-start.1) | async-done | bytes 2097184 | tf_op jit(solution)/shard_map/all_to_all | solution.py:734
  669.6 4.7 all-to-all-start
  674.4 0.7 copy.49
  675.1 37.1 %sum_small.1 = f32[16,128]{1,0:T(8,128)} custom-call(f32[16,16,128]{2,1,0:T(8,128)} %bitcast.138), custom_call_target="tpu_custom_call" | custom-call | tf_op jit(solution)/shard_map/sum_small/pallas_call | solution.py:122
  712.2 1.3 slice.109
  713.5 0.7 slice_bitcast_fusion.15
  714.2 0.6 copy.43
  714.8 1.3 fusion.10
  716.1 2.3 select_bitcast_fusion
  718.4 2.9 copy.56
  721.3 4.4 all_to_all.33
  725.7 3.2 copy.57
  729.0 2.8 all_to_all.29
  731.7 4.6 convolution_bitcast_fusion.2
  736.3 3.0 fusion.3
  739.3 0.4 copy-done.14
  739.7 1.2 fusion.4
  741.0 1.3 fusion.5
  742.3 2.0 maximum_bitcast_fusion
  744.2 3.6 all-gather.20.cloned.1.call-done
  747.8 9.4 %convolution_bitcast_fusion = f32[1,512,2048]{2,1,0:T(8,128)} fusion(bf16[2,1024,512]{1,2,0:T(8,128)(2,1)S(1)} %copy-done.1, bf16[2,1024,2048]{2,1,0:T(8,128)(2,1)} %all-gather.20.cloned.1.call-done), kind=kOutput, calls=%fused_computation | convolution fusion | flops 4294967296 | bytes 14680064 | tf_op jit(solution)/shard_map/dot_general | solution.py:739
  757.2 48.2 %all-gather.18.cloned.1.call-done = bf16[2,1024,2048]{2,1,0:T(8,128)(2,1)} async-done(((bf16[2,256,2048]{2,1,0:T(8,128)(2,1)}), bf16[2,1024,2048]{2,1,0:T(8,128)(2,1)}) %all-gather.18.cloned.1.call-update) | async-done | bytes 8388624 | tf_op jit(solution)/shard_map/all_gather | solution.py:731
  805.4 10.5 %convolution_bitcast_fusion.1 = f32[1,512,2048]{2,1,0:T(8,128)} fusion(bf16[2,1024,512]{1,2,0:T(8,128)(2,1)} %all_to_all.29, bf16[2,1024,2048]{2,1,0:T(8,128)(2,1)} %all-gather.18.cloned.1.call-done), kind=kOutput, calls=%fused_computation.1 | convolution fusion | flops 4294967296 | bytes 14680064 | tf_op jit(solution)/shard_map/dot_general | solution.py:739
  816.0 0.5 copy.68
  (68 shorter events, 0.8 us)
Async XLA Ops:
  7.2 27.9 %all-gather.22.cloned.1.call-start = ((), (), s32[]{:S(2)}) async-start(), calls=%async_computation.7 | async-start | bytes 2621440 | tf_op jit(solution)/shard_map/all_gather | solution.py:720
  7.9 75.2 %all-gather.12.cloned.1.call-start = ((), (), s32[]{:S(2)}) async-start(), calls=%async_computation.2 | async-start | bytes 7864320 | tf_op jit(solution)/shard_map/all_gather | solution.py:718
  8.7 1.4 copy-start.7
  8.7 1.5 copy-start.9
  8.7 1.7 copy-start.10
  8.7 1.9 copy-start.11
  8.7 2.1 copy-start.12
  8.7 2.3 copy-start.8
  8.7 16.3 %copy-start.4 = (s32[2,256]{1,0:T(2,128)S(1)}, s32[2,256]{1,0:T(2,128)}, u32[]{:S(2)}) copy-start(s32[2,256]{1,0:T(2,128)} %param.13) | copy-start | bytes 6148
  8.7 134.3 %all-gather.24.cloned.1.call-start = ((), (), s32[]{:S(2)}) async-start(), calls=%async_computation.8 | async-start | bytes 10485760 | tf_op jit(solution)/shard_map/all_gather | solution.py:719
  9.5 193.3 %all-gather.26.cloned.1.call-start = ((), (), s32[]{:S(2)}) async-start(), calls=%async_computation.9 | async-start | bytes 10485760 | tf_op jit(solution)/shard_map/all_gather | solution.py:721
  10.0 721.7 %all-gather.16.cloned.1.call-start = ((), (), s32[]{:S(2)}) async-start(), calls=%async_computation.4 | async-start | bytes 2621440 | tf_op jit(solution)/shard_map/all_gather | solution.py:731
  311.4 424.9 %all-gather.14.cloned.1.call-start = ((), (), s32[]{:S(2)}) async-start(), calls=%async_computation.3 | async-start | bytes 7864320 | tf_op jit(solution)/shard_map/all_gather | solution.py:731
  611.9 135.9 %all-gather.20.cloned.1.call-start = ((), (), s32[]{:S(2)}) async-start(), calls=%async_computation.6 | async-start | bytes 10485760 | tf_op jit(solution)/shard_map/all_gather | solution.py:731
  612.0 1.6 copy-start
  612.7 192.8 %all-gather.18.cloned.1.call-start = ((), (), s32[]{:S(2)}) async-start(), calls=%async_computation.5 | async-start | bytes 10485760 | tf_op jit(solution)/shard_map/all_gather | solution.py:731
  617.4 52.2 %all-to-all-start.1 = ((bf16[2,256,2048]{1,0,2:T(2,128)(2,1)}), bf16[2,256,2048]{1,0,2:T(2,128)(2,1)S(1)}, u32[]{:S(2)}, u32[]{:S(2)}) async-start(bf16[2,256,2048]{1,0,2:T(2,128)(2,1)} %copy.41), calls=%async_computation.1 | async-start | bytes 4194304 | tf_op jit(solution)/shard_map/all_to_all | solution.py:734
  628.1 46.2 %copy-start.5 = (f32[8,2048]{1,0:T(8,128)S(1)}, f32[8,2048]{1,0:T(8,128)}, u32[]{:S(2)}) copy-start(f32[8,2048]{1,0:T(8,128)} %get-tuple-element.32) | copy-start | bytes 196612
  628.1 46.3 %copy-start.6 = (f32[8,512]{1,0:T(8,128)S(1)}, f32[8,512]{1,0:T(8,128)}, u32[]{:S(2)}) copy-start(f32[8,512]{1,0:T(8,128)} %get-tuple-element.33) | copy-start | bytes 49156
  628.1 88.0 %copy-start.3 = (f32[2,64,2048]{2,1,0:T(8,128)S(1)}, f32[2,64,2048]{2,1,0:T(8,128)}, u32[]{:S(2)}) copy-start(f32[2,64,2048]{2,1,0:T(8,128)} %get-tuple-element.31) | copy-start | bytes 3145732
  669.6 56.2 %all-to-all-start = ((bf16[2,256,2048]{1,0,2:T(2,128)(2,1)}), bf16[2,256,2048]{1,0,2:T(2,128)(2,1)}, u32[]{:S(2)}, u32[]{:S(2)}) async-start(bf16[2,256,2048]{1,0,2:T(2,128)(2,1)} %copy.39), calls=%async_computation | async-start | bytes 4194304 | tf_op jit(solution)/shard_map/all_to_all | solution.py:734
  716.1 99.9 %copy-start.13 = (f32[1,128]{1,0:T(1,128)}, f32[1,128]{1,0:T(1,128)S(1)}, u32[]{:S(2)}) copy-start(f32[1,128]{1,0:T(1,128)S(1)} %get-tuple-element.108) | copy-start | bytes 1540
  731.7 4.6 copy-start.2
  736.3 3.4 copy-start.14
  742.2 5.6 copy-start.1
Sparse Core Ops, SparseCore 0:
  9.5 25.4 all-gather.21
  36.6 46.5 all-gather.11
  84.7 58.2 all-gather.23
  144.4 58.2 all-gather.25
  311.5 123.5 all-gather.15
  612.0 65.4 all-gather.13
  679.1 68.6 all-gather.19
  749.4 56.0 all-gather.17

commit v2 on v1

--- a/solution.py
+++ b/solution.py
@@ -680,6 +680,603 @@
     )(dy, wq, wo, w1, w2, rows, qkv, lse, gp, vec, rope, segc, segr)
 
 
+ROWS_OF_PACK = 16
+
+
+def masks_of(nf):
+    return range(nf)
+
+
+def bits_below(mask, nf):
+    low = mask & -mask if mask else nf
+    return [(i, 1 << i) for i in range(nf.bit_length() - 1) if (1 << i) < low]
+
+
+def flipped(index, mask, nf):
+    for i in range(nf.bit_length() - 1):
+        if mask >> i & 1:
+            index = index + (1 << i) * (1 - 2 * lax.rem(index // (1 << i), 2))
+    return index
+
+
+def fused_kernel(
+    nf, nt,
+    ends_h, pack, wq_h, wo_h, w1_h, w2_h, rope, segc, segr,
+    ends_o, sums_o, act_x, att_x, up_x, dj_x, xc_x, gc_x,
+    wq, wo, w1, w2, packs, wide, fb, rin, dyr, xg, qkv, lse, att, gp, act,
+    gr, gatt, up, dj, out_bf, out_got, in_bf, in_got, y_f, y_b, dx_f, dx_b,
+    own_sums, head_sums, up_sums, s_src, s_got,
+    in_sem, wl_sem, ws_sem, wr_sem, pk_s, pk_r, sm_s, sm_r,
+    ag_s, ag_r, gg_s, gg_r, rs_s, rs_r, rb_s, rb_r, hx_s, hx_r, hb_s, hb_r,
+    xl_sem, xs_s, xs_r, cl_sem, ca_s, ca_r, o_sem,
+):
+    micro, length, width = xg.shape
+    section, f, t = (lax.axis_index(a) for a in ("section", "fsdp", "tp"))
+    first, second = section == 0, section == 1
+    ring = Ring(nt, length // nt)
+    own, hidden = wo.shape[1], w1.shape[1]
+    depth = width // nf
+    count = nf * nt
+    other = {"section": 1 - section}
+    me, group = group_peers(nf, nt)
+    fblock = [flipped(f, mask, nf) for mask in masks_of(nf)]
+
+    def rows_at(block):
+        return pl.ds(pl.multiple_of(block * depth, depth), depth)
+
+    load_rows = pltpu.make_async_copy(ends_h, rin, in_sem)
+    load_dy = pltpu.make_async_copy(ends_h, dyr, in_sem)
+
+    @pl.when(first)
+    def _():
+        load_rows.start()
+
+    @pl.when(second)
+    def _():
+        load_dy.start()
+
+    greet([peer for _, _, peer in group] + [other])
+
+    pack_local = pltpu.make_async_copy(pack, packs.at[me], pk_s.at[0])
+    pack_copies = [
+        send(pack, packs.at[me], pk_s.at[k], pk_r.at[k], peer) for k, _, peer in group
+    ]
+    pack_local.start()
+    for copy in pack_copies:
+        copy.start()
+
+    table = ((wq_h, wq), (w1_h, w1), (wo_h, wo), (w2_h, w2))
+
+    def w_at(ref, block):
+        return ref.at[:, rows_at(block), :] if len(ref.shape) == 3 else ref.at[rows_at(block), :]
+
+    def w_local(a):
+        return pltpu.make_async_copy(table[a][0], w_at(table[a][1], f), wl_sem.at[a])
+
+    def w_send(a, mask, i, bit):
+        block = w_at(table[a][1], fblock[mask])
+        src = table[a][0] if mask == 0 else block
+        peer = {"fsdp": flipped(f, bit, nf)}
+        return send(src, block, ws_sem.at[a, mask, i], wr_sem.at[a, mask | bit], peer)
+
+    def w_recv(a, mask):
+        block = w_at(table[a][1], fblock[mask])
+        return send(block, block, ws_sem.at[a, mask, 0], wr_sem.at[a, mask], other)
+
+    def w_start(a):
+        w_local(a).start()
+        for i, bit in reversed(bits_below(0, nf)):
+            w_send(a, 0, i, bit).start()
+
+    def w_ready(a, mask):
+        if mask == 0:
+            w_local(a).wait()
+            return
+        w_recv(a, mask).wait_recv()
+        for i, bit in bits_below(mask, nf):
+            w_send(a, mask, i, bit).start()
+
+    order = sorted(masks_of(nf), key=lambda m: (m != 0, -(m & -m), m))
+    out_order = list(masks_of(nf))
+    w_start(0)
+    w_start(1)
+
+    pack_local.wait()
+    for copy in pack_copies:
+        copy.wait()
+    for j in range(count):
+        wide[:, j * LANES:(j + 1) * LANES] = packs[j]
+    per_row = hidden // nf // LANES
+    for j in range(nf):
+        for r in range(per_row):
+            c = (j * per_row + r) * LANES
+            fb[0:1, c:c + LANES] = packs[t * nf + j, 6 + r:7 + r, :]
+
+    def hop_out(m):
+        return send(y_b.at[m], rin.at[m], hx_s.at[m], hx_r.at[m], other)
+
+    def hop_back(m):
+        return send(dx_b.at[m], dyr.at[m], hb_s.at[m], hb_r.at[m], other)
+
+    def front(m):
+        unit, _ = stats(rin[m].astype(F32))
+        normed = unit * wide[0:1, :] + wide[1:2, :]
+        xg[m, ring.block(ring.me)] = normed.astype(BF16)
+        for copy in ring.gather(xg, m, (ag_s, ag_r)):
+            copy.start()
+
+    def front_back(m):
+        gr[m, ring.block(ring.me)] = dyr[m]
+        for copy in ring.gather(gr, m, (gg_s, gg_r)):
+            copy.start()
+
+    def x_dst(a, m, block):
+        if a == 3:
+            return dj_x.at[:, m, block]
+        return (act_x, att_x, up_x)[a].at[m, block]
+
+    def x_src(a, m):
+        return (act, att, up, dj)[a].at[m]
+
+    def x_local(a, m):
+        return pltpu.make_async_copy(x_src(a, m), x_dst(a, m, f), xl_sem.at[a, m])
+
+    def x_send(a, m, mask, i, bit):
+        block = x_dst(a, m, fblock[mask])
+        src = x_src(a, m) if mask == 0 else block
+        peer = {"fsdp": flipped(f, bit, nf)}
+        return send(src, block, xs_s.at[a, m, mask, i], xs_r.at[a, m, mask | bit], peer)
+
+    def x_recv(a, m, mask):
+        block = x_dst(a, m, fblock[mask])
+        return send(block, block, xs_s.at[a, m, mask, 0], xs_r.at[a, m, mask], other)
+
+    def x_start(a, m):
+        x_local(a, m).start()
+        for i, bit in reversed(bits_below(0, nf)):
+            x_send(a, m, 0, i, bit).start()
+
+    def x_relay(a, m):
+        for mask in order[1:]:
+            x_recv(a, m, mask).wait_recv()
+            for i, bit in bits_below(mask, nf):
+                x_send(a, m, mask, i, bit).start()
+
+    def x_done(a, m):
+        x_local(a, m).wait()
+        for mask in masks_of(nf):
+            for i, bit in bits_below(mask, nf):
+                x_send(a, m, mask, i, bit).wait_send()
+
+    def c_copies(which, m):
+        src, dst = ((xg, xc_x), (gr, gc_x))[which]
+        copies = []
+        for k in range(1, nf):
+            to = lax.rem(f + k, nf)
+            copies.append(
+                send(
+                    src.at[m, :, rows_at(to)],
+                    dst.at[m, f],
+                    ca_s.at[which, m, k],
+                    ca_r.at[which, m, k],
+                    {"fsdp": to},
+                )
+            )
+        return copies
+
+    def c_local(which, m):
+        src, dst = ((xg, xc_x), (gr, gc_x))[which]
+        return pltpu.make_async_copy(src.at[m, :, rows_at(f)], dst.at[m, f], cl_sem.at[which, m])
+
+    def c_start(which, m):
+        c_local(which, m).start()
+        for copy in c_copies(which, m):
+            copy.start()
+
+    def attention_masks(m):
+        low = low_half(length)
+        lane = lax.broadcasted_iota(jnp.int32, (length, LANES), 1)
+        tables = (rope[m, 0], rope[m, 1], rope[m, 2])
+        return low, lane, tables, allowed_mask(segc, segr, m, length)
+
+    factor = HEAD_DIM ** (-0.5)
+
+    def forward_stage(m, fresh):
+        for copy in ring.gather(xg, m, (ag_s, ag_r)):
+            copy.wait()
+        c_start(0, m)
+
+        @pl.when(fresh)
+        def _():
+            for mask in order:
+                w_ready(0, mask)
+            w_start(2)
+            w_start(3)
+
+        low, lane, tables, allowed = attention_masks(m)
+        for part in range(3):
+            def qkv_tile(n, part=part):
+                at = cols(n)
+                acc = jnp.dot(xg[m], wq[part, :, at], preferred_element_type=F32)
+                acc = acc + wide[3 + part:4 + part, pl.ds(
+                    pl.multiple_of(t * own + n * TILE, TILE), TILE)]
+                if part < 2:
+                    acc = jnp.concatenate(
+                        [
+                            turn(acc[:, c:c + LANES], tables, 1.0)
+                            for c in range(0, TILE, LANES)
+                        ],
+                        axis=1,
+                    )
+                qkv[m, part, :, at] = acc.astype(BF16)
+
+            loop(own // TILE, qkv_tile)
+
+        def pair(p):
+            at = cols(p, LANES)
+            query, key, value = qkv[m, 0, :, at], qkv[m, 1, :, at], qkv[m, 2, :, at]
+            outs = []
+            for h in range(2):
+                mask = low if h == 0 else ~low
+                one = jnp.where(mask, query, jnp.zeros_like(query))
+                s = lax.dot_general(one, key, COLS, preferred_element_type=F32)
+                s = jnp.where(allowed, s * factor, -1e30)
+                top = jnp.max(s, axis=-1, keepdims=True)
+                e = jnp.exp(s - top)
+                total = jnp.sum(e, axis=-1, keepdims=True)
+                probs = (e / total).astype(BF16)
+                outs.append(jnp.dot(probs, value, preferred_element_type=F32))
+                lse[m] = jnp.where(lane == 2 * p + h, top + jnp.log(total), lse[m])
+            att[m, :, at] = jnp.where(low, outs[0], outs[1]).astype(BF16)
+
+        lse[m] = jnp.zeros((length, LANES), F32)
+        loop(own // LANES, pair)
+        x_start(1, m)
+
+        @pl.when(fresh)
+        def _():
+            for mask in order:
+                w_ready(1, mask)
+
+        def up_tile(n):
+            at = cols(n)
+            u = jnp.dot(xg[m], w1[:, at], preferred_element_type=F32) + fb[0:1, at]
+            c = 0.7978845608028654
+            square = u * u
+            th = jnp.tanh(c * u * (1.0 + 0.044715 * square))
+            act[m, :, at] = (0.5 * u * (1.0 + th)).astype(BF16)
+            slope = 0.5 * (1.0 + th)
+            slope = slope + 0.5 * u * (1.0 - th * th) * (c * (1.0 + 3 * 0.044715 * square))
+            gp[m, :, at] = slope.astype(BF16)
+
+        loop(hidden // TILE, up_tile)
+        x_start(0, m)
+
+    def output_stage(m, fresh):
+        for mask in out_order:
+            @pl.when(fresh)
+            def _(mask=mask):
+                w_ready(2, mask)
+                w_ready(3, mask)
+
+            def out_tile(n, mask=mask):
+                start = pl.multiple_of(fblock[mask] * depth + n * TILE, TILE)
+                at = pl.ds(start, TILE)
+                acc = lax.dot_general(att[m], wo[at, :], COLS, preferred_element_type=F32)
+                acc = acc + lax.dot_general(act[m], w2[at, :], COLS, preferred_element_type=F32)
+                out_bf[m, :, at] = acc.astype(BF16)
+                for copy in ring.scatter(out_bf, out_got, m, (rs_s, rs_r), at):
+                    copy.start()
+
+            loop(depth // TILE, out_tile)
+
+    def store_ends(src, m):
+        return pltpu.make_async_copy(src.at[m], ends_o.at[m], o_sem.at[m])
+
+    def output_finish(m):
+        for copy in ring.scatter(out_bf, out_got, m, (rs_s, rs_r)):
+            copy.wait()
+        y = rin[m].astype(F32) + ring.total(out_bf, out_got, m) + wide[2:3, :]
+        y_b[m] = y.astype(BF16)
+
+        @pl.when(first)
+        def _():
+            hop_out(m).start()
+
+        @pl.when(second)
+        def _():
+            y_f[m] = y
+            store_ends(y_f, m).start()
+
+    def backward_stage(m, k):
+        @pl.when(first)
+        def _():
+            for copy in ring.gather(gr, m, (gg_s, gg_r)):
+                copy.wait()
+            c_start(1, m)
+
+        def att_tile(n):
+            at = cols(n)
+            gatt[:, at] = jnp.dot(gr[m], wo[:, at], preferred_element_type=F32).astype(BF16)
+
+        loop(own // TILE, att_tile)
+        low, lane, tables, allowed = attention_masks(m)
+
+        def pair(p):
+            at = cols(p, LANES)
+            query, key, value = qkv[m, 0, :, at], qkv[m, 1, :, at], qkv[m, 2, :, at]
+            grad = gatt[:, at]
+            dqs, dks, dvs = [], [], []
+            for h in range(2):
+                mask = low if h == 0 else ~low
+                one = jnp.where(mask, query, jnp.zeros_like(query))
+                s = lax.dot_general(one, key, COLS, preferred_element_type=F32)
+                s = jnp.where(allowed, s * factor, -1e30)
+                log_total = jnp.sum(
+                    jnp.where(lane == 2 * p + h, lse[m], 0.0), axis=-1, keepdims=True
+                )
+                soft = jnp.exp(s - log_total)
+                probs = soft.astype(BF16)
+                one_grad = jnp.where(mask, grad, jnp.zeros_like(grad))
+                dp = lax.dot_general(one_grad, value, COLS, preferred_element_type=F32)
+                delta = jnp.sum(dp * soft, axis=-1, keepdims=True)
+                ds = (soft * (dp - delta)).astype(BF16)
+                dvs.append(lax.dot_general(probs, grad, ROWS, preferred_element_type=F32))
+                dqs.append(jnp.dot(ds, key, preferred_element_type=F32))
+                dks.append(lax.dot_general(ds, query, ROWS, preferred_element_type=F32))
+            dq = jnp.where(low, dqs[0], dqs[1]) * factor
+            dk = jnp.where(low, dks[0], dks[1]) * factor
+            dj[m, 0, :, at] = turn(dq, tables, -1.0).astype(BF16)
+            dj[m, 1, :, at] = turn(dk, tables, -1.0).astype(BF16)
+            dj[m, 2, :, at] = jnp.where(low, dvs[0], dvs[1]).astype(BF16)
+
+        loop(own // LANES, pair)
+        x_start(3, m)
+
+        @pl.when(second & (k == 3))
+        def _():
+            backward_finish(0)
+
+        for part in range(3):
+            head_sums[part:part + 1, :] += jnp.sum(
+                dj[m, part].astype(F32), axis=0, keepdims=True
+            )
+
+        def up_tile(n):
+            at = cols(n)
+            acc = jnp.dot(gr[m], w2[:, at], preferred_element_type=F32)
+            rounded = (acc * gp[m, :, at].astype(F32)).astype(BF16)
+            up[m, :, at] = rounded
+            up_sums[0:1, at] += jnp.sum(rounded.astype(F32), axis=0, keepdims=True)
+
+        loop(hidden // TILE, up_tile)
+        x_start(2, m)
+
+        @pl.when(first & (k == 2))
+        def _():
+            hop_back(1).wait_recv()
+            front_back(1)
+
+        def norm_tile(n):
+            at = cols(n)
+            acc = lax.dot_general(up[m], w1[at, :], COLS, preferred_element_type=F32)
+            for part in range(3):
+                acc = acc + lax.dot_general(
+                    dj[m, part], wq[part, at, :], COLS, preferred_element_type=F32
+                )
+            in_bf[m, :, at] = acc.astype(BF16)
+            for copy in ring.scatter(in_bf, in_got, m, (rb_s, rb_r), at):
+                copy.start()
+
+        loop(width // TILE, norm_tile)
+
+    def backward_finish(m):
+        for copy in ring.scatter(in_bf, in_got, m, (rb_s, rb_r)):
+            copy.wait()
+        grad_norm = ring.total(in_bf, in_got, m)
+        unit, inv_root = stats(rin[m].astype(F32))
+        scaled = grad_norm * wide[0:1, :]
+        upstream = dyr[m].astype(F32)
+        dx = upstream + inv_root * (
+            scaled
+            - jnp.mean(scaled, axis=-1, keepdims=True)
+            - unit * jnp.mean(scaled * unit, axis=-1, keepdims=True)
+        )
+        dx_b[m] = dx.astype(BF16)
+
+        @pl.when(second)
+        def _():
+            hop_back(m).start()
+
+        @pl.when(first)
+        def _():
+            dx_f[m] = dx
+            store_ends(dx_f, m).start()
+
+        for i, term in enumerate((grad_norm * unit, grad_norm, upstream)):
+            own_sums[i:i + 1, :] += jnp.sum(term, axis=0, keepdims=True)
+
+    own_sums[...] = jnp.zeros_like(own_sums)
+    head_sums[...] = jnp.zeros_like(head_sums)
+    up_sums[...] = jnp.zeros_like(up_sums)
+
+    @pl.when(first)
+    def _():
+        load_rows.wait()
+        loop(micro, front)
+
+    @pl.when(second)
+    def _():
+        load_dy.wait()
+        loop(micro, front_back)
+        for mask in order:
+            w_ready(0, mask)
+        w_start(2)
+        w_start(3)
+        for a in (1, 2, 3):
+            for mask in order:
+                w_ready(a, mask)
+
+        def columns_out(m):
+            for copy in ring.gather(gr, m, (gg_s, gg_r)):
+                copy.wait()
+            c_start(1, m)
+
+        loop(micro, columns_out)
+
+    def slot(k):
+        is_f = jnp.where(first, k < 2, (k == 0) | (k == 2))
+        is_b = jnp.where(first, (k == 2) | (k == 3), (k == 1) | (k == 3))
+        is_o = jnp.where(first, k < 2, k >= 4)
+        fresh = first & (k == 0)
+        m = jnp.where(first | (k >= 4), lax.rem(k, 2), k // 2)
+
+        @pl.when(second & (k < 2))
+        def _():
+            hop_out(k).wait_recv()
+            front(k)
+
+        @pl.when(first & (k == 2))
+        def _():
+            for i in range(micro):
+                for a in (1, 0):
+                    x_relay(a, i)
+            hop_back(0).wait_recv()
+            front_back(0)
+
+        @pl.when(is_f)
+        def _():
+            forward_stage(m, fresh)
+
+        @pl.when(is_o)
+        def _():
+            output_stage(m, fresh)
+
+        @pl.when(is_b)
+        def _():
+            backward_stage(m, k)
+
+        @pl.when((first & (k == 1)) | (second & (k == 5)))
+        def _():
+            loop(micro, output_finish)
+
+        @pl.when(first & (k == 3))
+        def _():
+            backward_finish(0)
+
+        @pl.when(k == 3)
+        def _():
+            backward_finish(1)
+
+    loop(6, slot)
+
+    s_src[...] = jnp.zeros_like(s_src)
+    for j in range(count):
+        s_src[j, 0:3, :] = own_sums[0:3, j * LANES:(j + 1) * LANES]
+    for j in range(nf):
+        s_src[t * nf + j, 3:6, :] = head_sums[0:3, j * LANES:(j + 1) * LANES]
+        for r in range(per_row):
+            c = (j * per_row + r) * LANES
+            s_src[t * nf + j, 6 + r:7 + r, :] = up_sums[0:1, c:c + LANES]
+    small = [
+        send(s_src.at[to], s_got.at[k], sm_s.at[k], sm_r.at[k], peer) for k, to, peer in group
+    ]
+    for copy in small:
+        copy.start()
+
+    @pl.when(second)
+    def _():
+        for a, m in ((1, 0), (0, 0), (3, 0), (2, 0), (1, 1), (0, 1), (3, 1), (2, 1)):
+            x_relay(a, m)
+        for m in range(micro):
+            hop_back(m).wait_send()
+
+    @pl.when(first)
+    def _():
+        for a, m in ((3, 0), (2, 0), (3, 1), (2, 1)):
+            x_relay(a, m)
+        for m in range(micro):
+            hop_out(m).wait_send()
+
+    total = s_src[me]
+    for k, copy in enumerate(small):
+        copy.wait()
+        total = total + s_got[k + 1]
+    sums_o[...] = total
+    for m in range(micro):
+        for a in range(4):
+            x_done(a, m)
+        for which in range(2):
+            c_local(which, m).wait()
+            for copy in c_copies(which, m):
+                copy.wait()
+        store_ends(y_f, m).wait()
+    for a in range(4):
+        for mask in masks_of(nf):
+            for i, bit in bits_below(mask, nf):
+                w_send(a, mask, i, bit).wait_send()
+
+
+def fused(ends, pack, wq, wo, w1, w2, rope, segc, segr, nf, nt):
+    micro, per, width = ends.shape
+    length = per * nt
+    own, hidden = wo.shape[1], w1.shape[1]
+    depth = width // nf
+    count = nf * nt
+    bits = nf.bit_length() - 1
+    anywhere = pl.BlockSpec(memory_space=pl.ANY)
+    inside = pl.BlockSpec(memory_space=pltpu.VMEM)
+    dma = pltpu.SemaphoreType.DMA
+    vm = pltpu.VMEM
+    small = (count,) + pack.shape
+    tokens = (micro, length)
+    out_shape = [
+        jax.ShapeDtypeStruct(ends.shape, F32),
+        jax.ShapeDtypeStruct(pack.shape, F32),
+        jax.ShapeDtypeStruct((micro, nf, length, hidden), BF16),
+        jax.ShapeDtypeStruct((micro, nf, length, own), BF16),
+        jax.ShapeDtypeStruct((micro, nf, length, hidden), BF16),
+        jax.ShapeDtypeStruct((3, micro, nf, length, own), BF16),
+        jax.ShapeDtypeStruct((micro, nf, length, depth), BF16),
+        jax.ShapeDtypeStruct((micro, nf, length, depth), BF16),
+    ]
+    scratch = [
+        vm((3, width, own), BF16), vm((width, own), BF16),
+        vm((width, hidden), BF16), vm((width, hidden), BF16),
+        vm(small, F32), vm((pack.shape[0], width), F32), vm((8, hidden), F32),
+        vm(ends.shape, BF16), vm(ends.shape, BF16),
+        vm(tokens + (width,), BF16), vm((micro, 3, length, own), BF16),
+        vm(tokens + (LANES,), F32), vm(tokens + (own,), BF16),
+        vm(tokens + (hidden,), BF16), vm(tokens + (hidden,), BF16),
+        vm(tokens + (width,), BF16), vm((length, own), BF16),
+        vm(tokens + (hidden,), BF16), vm((micro, 3, length, own), BF16),
+        vm(tokens + (width,), BF16), vm((micro, nt, per, width), BF16),
+        vm(tokens + (width,), BF16), vm((micro, nt, per, width), BF16),
+        vm(ends.shape, F32), vm(ends.shape, BF16),
+        vm(ends.shape, F32), vm(ends.shape, BF16),
+        vm((8, width), F32), vm((8, own), F32), vm((8, hidden), F32),
+        vm(small, F32), vm(small, F32),
+        dma, dma((4,)), dma((4, nf, bits)), dma((4, nf)),
+        dma((count,)), dma((count,)), dma((count,)), dma((count,)),
+        dma((micro, nt)), dma((micro, nt)), dma((micro, nt)), dma((micro, nt)),
+        dma((micro, nt)), dma((micro, nt)), dma((micro, nt)), dma((micro, nt)),
+        dma((micro,)), dma((micro,)), dma((micro,)), dma((micro,)),
+        dma((4, micro)), dma((4, micro, nf, bits)), dma((4, micro, nf)),
+        dma((2, micro)), dma((2, micro, nf)), dma((2, micro, nf)), dma((micro,)),
+    ]
+    return pl.pallas_call(
+        functools.partial(fused_kernel, nf, nt),
+        out_shape=out_shape,
+        in_specs=[anywhere, inside] + [anywhere] * 4 + [inside] * 3,
+        out_specs=[anywhere, inside] + [anywhere] * 6,
+        scratch_shapes=scratch,
+        compiler_params=pltpu.CompilerParams(
+            collective_id=4, has_side_effects=True, vmem_limit_bytes=VMEM_LIMIT
+        ),
+        name="fused",
+    )(ends, pack, wq, wo, w1, w2, rope, segc, segr)
+
+
 def padded(flat):
     size = -(-flat.shape[-1] // (8 * LANES)) * (8 * LANES)
     room = [(0, 0)] * (flat.ndim - 1) + [(0, size - flat.shape[-1])]
@@ -687,7 +1284,7 @@
     return flat.reshape(flat.shape[:-1] + (size // LANES, LANES))
 
 
-def shards(
+def split_shards(
     ends_in, segments, ln_gain, ln_bias, w_qkv, w_out, w_fc1, w_fc2,
     bias_qkv, bias_out, bias_fc1, bias_fc2,
 ):
@@ -777,6 +1374,56 @@
     )
 
 
+def fused_shards(
+    ends_in, segments, ln_gain, ln_bias, w_qkv, w_out, w_fc1, w_fc2,
+    bias_qkv, bias_out, bias_fc1, bias_fc2,
+):
+    nf, nt = lax.axis_size("fsdp"), lax.axis_size("tp")
+    pack = jnp.concatenate(
+        [
+            ln_gain, ln_bias, (bias_out.astype(F32) + bias_fc2.astype(F32)),
+            bias_qkv[0], bias_fc1[0].reshape(-1, LANES),
+        ]
+    ).astype(F32)
+    used = pack.shape[0]
+    pack = jnp.pad(pack, ((0, ROWS_OF_PACK - used), (0, 0)))
+    ends_out, sums, act_x, att_x, up_x, dj_x, xc, gc = fused(
+        ends_in[0], pack, w_qkv[0].transpose(1, 0, 2), w_out[0], w_fc1[0], w_fc2[0],
+        rope_tables(segments), segments[:, :, None], segments[:, None, :], nf, nt,
+    )
+
+    def product(left, right):
+        left = left.reshape(-1, left.shape[-1])
+        right = right.reshape(-1, right.shape[-1])
+        return lax.dot_general(left, right, ROWS, preferred_element_type=F32)
+
+    grad_fc2 = product(gc, act_x)
+    grad_out = product(gc, att_x)
+    grad_fc1 = product(xc, up_x)
+    grad_qkv = jnp.stack([product(xc, dj_x[part]) for part in range(3)], axis=1)
+    row_grad = sums[2:3]
+    return (
+        ends_out[None],
+        sums[0:1],
+        sums[1:2],
+        grad_qkv[None],
+        grad_out[None],
+        grad_fc1[None],
+        grad_fc2[None],
+        sums[3:6][None],
+        row_grad,
+        sums[6:used].reshape(1, -1),
+        row_grad,
+    )
+
+
+def shards(*args):
+    rows, piece = args[0].shape[2], args[2].shape[1]
+    small = rows * lax.axis_size("tp") <= 256
+    tidy = piece == LANES and args[10].shape[1] // LANES <= ROWS_OF_PACK - 6
+    return (fused_shards if small and tidy else split_shards)(*args)
+
+
 def solution(mesh):
     both = P("section", ("fsdp", "tp"))
     square = P("section", "fsdp", "tp")

time: 824 us -> 455 us (0.55)
  waiting for transfers between devices: 268 us -> 0 us
  Pallas kernels: 458 us -> 404 us
  local copies, waits for them, and re-layouts: 35.3 us -> 10.5 us
  between operations: 14.5 us -> 0.73 us
  starting transfers between devices: 8.67 us -> 0 us
    all_gather x8 -> x0, waiting for transfers between devices: 222 us -> none  [the longest x1 59.9 us: shards(): w1 = lax.all_gather(w_fc1[0], 'fsdp', axis=0, tiled=True)]
    pallas_call x4 -> x1, Pallas kernels: 458 us -> 404 us  [fused(): pl.pallas_call(functools.partial(fused_kernel, nf, nt), out_shape=out_sha...]
    all_to_all x2 -> x0, waiting for transfers between devices: 41.5 us -> none  [columns(): return lax.all_to_all(arr, 'fsdp', split_axis=2, concat_axis=1, tiled=True)]
    all_to_all x4 -> x0, local copies, waits for them, and re-layouts: 13.3 us -> none  [columns(): return lax.all_to_all(arr, 'fsdp', split_axis=2, concat_axis=1, tiled=True)]
    pallas_call x2 -> x0, local copies, waits for them, and re-layouts: 9.97 us -> none  [the longest x1 6.14 us: forward(): pl.pallas_call(functools.partial(forward_kernel, nt), out_shape=out_shape...]
    all_to_all x2 -> x0, starting transfers between devices: 8.36 us -> none  [columns(): return lax.all_to_all(arr, 'fsdp', split_axis=2, concat_axis=1, tiled=True)]
  transfers between devices with their start and end apart: 10 -> 0, of which waited for: 7 -> 0; matrix products, arithmetic and copies ran while one was open for 7% -> 0% of each run, Pallas kernels for 42% -> 0%
where the time goes in v2:
time: 455 us; the launch traced here: 448 us
  Pallas kernels  404 us (89%)
  matrix products  24.3 us (5%)
  local copies, waits for them, and re-layouts  10.5 us (2%)
  other arithmetic  8.83 us (2%)
    pallas_call x1, Pallas kernels, fused(): pl.pallas_call(functools.partial(fused_kernel, nf, nt), out_shape=out_sha...  404 us
    dot_general x6, matrix products, product(): return lax.dot_general(left, right, ROWS, preferred_element_type=F32)  24.3 us

profile of v2, /device:TPU:0, one launch (start us, length us, event | category | flops | bytes accessed | tf_op | source)
XLA Modules:
  0.0 448.1 jit_solution(18328060964925344044)
XLA Ops:
  0.6 0.7 convert_add_fusion
  1.3 0.1 pad.19.clone
  1.4 0.1 pad.22.clone
  1.5 0.7 slice_add_fusion
  2.2 0.8 compare_select_fusion
  3.0 0.6 reduce-window.6
  3.6 0.2 slice_reduce_fusion
  3.8 0.2 reduce-window.9
  4.0 0.1 maximum_bitcast_fusion.4
  4.1 0.7 bitcast_convert_fusion
  4.8 0.7 convert_element_type.43
  5.5 1.3 broadcast_in_dim.46.segr
  6.7 0.8 concatenate.18
  7.5 0.6 pad.4.pack
  8.1 1.5 copy.29.segc
  9.7 1.0 multiply_cosine_fusion
  10.7 0.3 maximum_bitcast_fusion.2
  10.9 1.2 maximum_maximum_fusion.rope
  12.1 403.8 %fused.1 = (f32[2,64,2048]{2,1,0:T(8,128)}, f32[16,128]{1,0:T(8,128)}, bf16[2,4,256,2048]{3,2,1,0:T(8,128)(2,1)}, bf16[2,4,256,512]{3,2,1,0:T(8,128)(2,1)}, bf16...) custom-call(bf16[2,64,2048]{2,1,0:T(8,128)(2,1)} %bitcast.83, ...), custom_call_target="tpu_custom_call" | custom-call | tf_op jit(solution)/shard_map/fused/pallas_call | solution.py:1267
  415.9 1.3 fusion.3
  417.2 0.0 copy-start.2
  417.2 0.7 slice_bitcast_fusion
  417.9 1.3 slice.47
  419.2 0.6 copy.33
  419.7 0.0 copy-start
  419.7 4.6 %convolution_bitcast_fusion.2 = f32[1,512,512]{2,1,0:T(8,128)} fusion(bf16[2,4,256,512]{3,2,1,0:T(8,128)(2,1)} %get-tuple-element.23, bf16[2,4,256,512]{3,2,1,0:T(8,128)(2,1)} %get-tuple-element.24), kind=kOutput, calls=%fused_computation.3 | convolution fusion | flops 1073741824 | bytes 5242880 | tf_op jit(solution)/shard_map/dot_general | solution.py:1398
  424.4 0.0 copy-done
  424.4 0.0 copy-start.3
  424.4 0.0 copy-start.4
  424.4 0.0 slice-start
  424.4 9.6 %convolution_bitcast_fusion = f32[1,512,2048]{2,1,0:T(8,128)} fusion(bf16[2,4,256,512]{3,2,1,0:T(8,128)(2,1)S(1)} %copy-done, bf16[2,4,256,2048]{3,2,1,0:T(8,128)(2,1)} %get-tuple-element.26), kind=kOutput, calls=%fused_computation | convolution fusion | flops 4294967296 | bytes 14680064 | tf_op jit(solution)/shard_map/dot_general | solution.py:1398
  434.0 0.0 copy-done.3
  434.0 0.0 copy-done.4
  434.0 0.0 slice-start.1
  434.0 6.2 %convolution_bitcast_fusion.1 = f32[1,512,2048]{2,1,0:T(8,128)} fusion(bf16[2,4,256,512]{3,2,1,0:T(8,128)(2,1)S(1)} %copy-done.4, bf16[2,4,256,2048]{3,2,1,0:T(8,128)(2,1)S(1)} %copy-done.3), kind=kOutput, calls=%fused_computation.1 | convolution fusion | flops 4294967296 | bytes 14680064 | tf_op jit(solution)/shard_map/dot_general | solution.py:1398
  440.2 0.0 slice-done
  440.2 0.0 slice-done.1
  440.2 0.6 fusion.2
  440.8 1.3 convolution_bitcast_fusion.5
  442.1 1.3 convolution_bitcast_fusion.3
  443.4 1.3 convolution_bitcast_fusion.4
  444.7 0.0 copy-start.1
  444.7 2.0 maximum_bitcast_fusion
  446.7 0.0 copy-done.2
  446.7 0.5 copy.44
  447.2 0.0 copy-done.1
  447.2 1.0 copy.45
  (7 shorter events, 0.1 us)
Async XLA Ops:
  417.2 29.4 %copy-start.2 = (f32[1,128]{1,0:T(1,128)}, f32[1,128]{1,0:T(1,128)S(1)}, u32[]{:S(2)}) copy-start(f32[1,128]{1,0:T(1,128)S(1)} %get-tuple-element.102) | copy-start | bytes 1540
  419.7 4.6 %copy-start = (bf16[2,4,256,512]{3,2,1,0:T(8,128)(2,1)S(1)}, bf16[2,4,256,512]{3,2,1,0:T(8,128)(2,1)}, u32[]{:S(2)}) copy-start(bf16[2,4,256,512]{3,2,1,0:T(8,128)(2,1)} %get-tuple-element.23) | copy-start | bytes 6291460
  424.4 9.6 %copy-start.3 = (bf16[2,4,256,2048]{3,2,1,0:T(8,128)(2,1)S(1)}, bf16[2,4,256,2048]{3,2,1,0:T(8,128)(2,1)}, u32[]{:S(2)}) copy-start(bf16[2,4,256,2048]{3,2,1,0:T(8,128)(2,1)} %get-tuple-element.25) | copy-start | bytes 25165828
  424.4 9.6 %copy-start.4 = (bf16[2,4,256,512]{3,2,1,0:T(8,128)(2,1)S(1)}, bf16[2,4,256,512]{3,2,1,0:T(8,128)(2,1)}, u32[]{:S(2)}) copy-start(bf16[2,4,256,512]{3,2,1,0:T(8,128)(2,1)} %get-tuple-element.21) | copy-start | bytes 6291460
  424.4 15.8 %slice-start = ((s8[6291456]{0:T(1024)(128)(4,1)}), s8[4194304]{0:T(1024)(128)(4,1)S(1)}, s32[]{:S(2)}) async-start(s8[6291456]{0:T(1024)(128)(4,1)} %bitcast.74), calls=%async_computation | async-start | bytes 8388608
  434.0 6.2 %slice-start.1 = ((s8[6291456]{0:T(1024)(128)(4,1)}), s8[2097152]{0:T(1024)(128)(4,1)S(1)}, s32[]{:S(2)}) async-start(s8[6291456]{0:T(1024)(128)(4,1)} %bitcast.74), calls=%async_computation.1 | async-start | bytes 4194304
  444.7 2.5 copy-start.1

commit v3 on v2

--- a/solution.py
+++ b/solution.py
@@ -17,7 +17,7 @@
 BF16 = jnp.bfloat16
 COLS = (((1,), (1,)), ((), ()))
 ROWS = (((0,), (0,)), ((), ()))
-VMEM_LIMIT = 62 * 1024 * 1024
+VMEM_LIMIT = 66_900_000
 
 
 def positions_of(segment_ids):
@@ -189,7 +189,7 @@
         return [
             send(
                 buf.at[m, self.block(to), at],
-                got.at[m, k, :, at],
+                got.at[m, k - 1, :, at],
                 sems[0].at[m, k],
                 sems[1].at[m, k],
                 {"tp": to},
@@ -200,7 +200,7 @@
     def total(self, buf, got, m):
         acc = buf[m, self.block(self.me)].astype(F32)
         for k, _ in self.others:
-            acc = acc + got[m, k].astype(F32)
+            acc = acc + got[m, k - 1].astype(F32)
         return acc
 
 
@@ -411,7 +411,7 @@
             pltpu.VMEM((micro, length, hidden), BF16),
             pltpu.VMEM((micro, length, hidden), BF16),
             pltpu.VMEM((micro, length, width), BF16),
-            pltpu.VMEM((micro, nt, per, width), BF16),
+            pltpu.VMEM((micro, nt - 1, per, width), BF16),
             pltpu.VMEM(rows.shape, F32),
             pltpu.VMEM(rows.shape, BF16),
             dma((4,)),
@@ -660,7 +660,7 @@
             pltpu.VMEM((micro, length, hidden), BF16),
             pltpu.VMEM((micro, 3, length, own), BF16),
             pltpu.VMEM((micro, length, width), BF16),
-            pltpu.VMEM((micro, nt, per, width), BF16),
+            pltpu.VMEM((micro, nt - 1, per, width), BF16),
             pltpu.VMEM(rows.shape, F32),
             pltpu.VMEM(rows.shape, BF16),
             dma((4,)),
@@ -683,6 +683,13 @@
 ROWS_OF_PACK = 16
 
 
+def twist(x, tables, sign):
+    keep, sine, ahead = tables
+    left = pltpu.roll(x, LANES - ROT_DIM // 2, 1)
+    right = pltpu.roll(x, ROT_DIM // 2, 1)
+    return x * keep + jnp.where(ahead, left, right) * (sign * sine)
+
+
 def masks_of(nf):
     return range(nf)
 
@@ -701,21 +708,23 @@
 
 def fused_kernel(
     nf, nt,
-    ends_h, pack, wq_h, wo_h, w1_h, w2_h, rope, segc, segr,
+    ends_h, gain, shift, b_out, b_fc2, b_qkv, b_fc1, seg_in, wq_h, wo_h, w1_h, w2_h,
     ends_o, sums_o, act_x, att_x, up_x, dj_x, xc_x, gc_x,
-    wq, wo, w1, w2, packs, wide, fb, rin, dyr, xg, qkv, lse, att, gp, act,
-    gr, gatt, up, dj, out_bf, out_got, in_bf, in_got, y_f, y_b, dx_f, dx_b,
+    wq, wo, w1, w2, pack, packs, wide, fb, segs, rope, rin, dyr, xg, qkv, lse, att, gp, act,
+    gr, gatt, up, dj, out_bf, out_got, in_bf, in_got, y_f, y_b,
     own_sums, head_sums, up_sums, s_src, s_got,
     in_sem, wl_sem, ws_sem, wr_sem, pk_s, pk_r, sm_s, sm_r,
     ag_s, ag_r, gg_s, gg_r, rs_s, rs_r, rb_s, rb_r, hx_s, hx_r, hb_s, hb_r,
-    xl_sem, xs_s, xs_r, cl_sem, ca_s, ca_r, o_sem,
+    xl_sem, xs_s, xs_r, cl_sem, ca_s, ca_r, mx_s, mx_r, o_sem,
 ):
-    micro, length, width = xg.shape
+    micro, per, width = rin.shape
+    length = per * nt
     section, f, t = (lax.axis_index(a) for a in ("section", "fsdp", "tp"))
     first, second = section == 0, section == 1
-    ring = Ring(nt, length // nt)
+    ring = Ring(nt, per)
     own, hidden = wo.shape[1], w1.shape[1]
     depth = width // nf
+    mirror, sibling = {"fsdp": flipped(f, 2, nf)}, {"fsdp": flipped(f, 1, nf)}
     count = nf * nt
     other = {"section": 1 - section}
     me, group = group_peers(nf, nt)
@@ -737,11 +746,23 @@
 
     greet([peer for _, _, peer in group] + [other])
 
+    per_row = hidden // nf // LANES
+    segs[0] = jnp.zeros((8, length), F32)
+    segs[0, 0:micro, :] = seg_in[...].astype(F32)
+    pack[...] = jnp.zeros_like(pack)
+    pack[0:1, :] = gain[...].astype(F32)
+    pack[1:2, :] = shift[...].astype(F32)
+    pack[2:3, :] = b_out[...].astype(F32) + b_fc2[...].astype(F32)
+    pack[3:6, :] = b_qkv[...].astype(F32)
+    for r in range(per_row):
+        pack[6 + r:7 + r, :] = b_fc1[:, r * LANES:(r + 1) * LANES].astype(F32)
+    seg_copy = send(segs.at[0], segs.at[1], mx_s.at[2, 0], mx_r.at[2, 0], mirror)
     pack_local = pltpu.make_async_copy(pack, packs.at[me], pk_s.at[0])
     pack_copies = [
         send(pack, packs.at[me], pk_s.at[k], pk_r.at[k], peer) for k, _, peer in group
     ]
     pack_local.start()
+    seg_copy.start()
     for copy in pack_copies:
         copy.start()
 
@@ -786,17 +807,40 @@
         copy.wait()
     for j in range(count):
         wide[:, j * LANES:(j + 1) * LANES] = packs[j]
-    per_row = hidden // nf // LANES
     for j in range(nf):
         for r in range(per_row):
             c = (j * per_row + r) * LANES
             fb[0:1, c:c + LANES] = packs[t * nf + j, 6 + r:7 + r, :]
 
+    def segment_parts(q):
+        row = segs[q // micro, pl.ds(lax.rem(q, micro), 1), :]
+        query = lax.broadcasted_iota(jnp.int32, (length, length), 0)
+        key = lax.broadcasted_iota(jnp.int32, (length, length), 1)
+        column = jnp.sum(jnp.where(query == key, row, 0.0), axis=1, keepdims=True)
+        return row, column, query >= key
+
+    def allowed_of(q):
+        row, column, causal = segment_parts(q)
+        return causal & (row == column)
+
+    def rope_of(q):
+        row, column, _ = segment_parts(q)
+        before = jnp.sum(jnp.where(row < column, 1.0, 0.0), axis=1, keepdims=True)
+        lane = lax.rem(lax.broadcasted_iota(jnp.int32, (length, LANES), 1), HEAD_DIM)
+        place = lax.broadcasted_iota(jnp.int32, (length, LANES), 0).astype(F32) - before
+        half = ROT_DIM // 2
+        power = lax.rem(lane, half).astype(F32)
+        freq = jnp.exp(-jnp.log(10000.0) * (2.0 * power) / ROT_DIM)
+        angles = place * freq
+        rope[q, 0] = jnp.where(lane < ROT_DIM, jnp.cos(angles), 1.0)
+        sine = jnp.where(lane < ROT_DIM, jnp.sin(angles), 0.0)
+        rope[q, 1] = jnp.where(lane < half, -sine, sine)
+
     def hop_out(m):
         return send(y_b.at[m], rin.at[m], hx_s.at[m], hx_r.at[m], other)
 
     def hop_back(m):
-        return send(dx_b.at[m], dyr.at[m], hb_s.at[m], hb_r.at[m], other)
+        return send(y_b.at[m], dyr.at[m], hb_s.at[m], hb_r.at[m], other)
 
     def front(m):
         unit, _ = stats(rin[m].astype(F32))
@@ -810,81 +854,94 @@
         for copy in ring.gather(gr, m, (gg_s, gg_r)):
             copy.start()
 
-    def x_dst(a, m, block):
+    def mirror_copy(which, m):
+        buf = (xg, gr)[which]
+        return send(
+            buf.at[m], buf.at[micro + m], mx_s.at[which, m], mx_r.at[which, m], mirror
+        )
+
+    def x_block(who):
+        return fblock[2 * who] if isinstance(who, int) else jnp.where(who == 0, f, fblock[2])
+
+    def x_dst(a, m, who):
+        block = x_block(who)
         if a == 3:
             return dj_x.at[:, m, block]
         return (act_x, att_x, up_x)[a].at[m, block]
 
-    def x_src(a, m):
-        return (act, att, up, dj)[a].at[m]
-
-    def x_local(a, m):
-        return pltpu.make_async_copy(x_src(a, m), x_dst(a, m, f), xl_sem.at[a, m])
-
-    def x_send(a, m, mask, i, bit):
-        block = x_dst(a, m, fblock[mask])
-        src = x_src(a, m) if mask == 0 else block
-        peer = {"fsdp": flipped(f, bit, nf)}
-        return send(src, block, xs_s.at[a, m, mask, i], xs_r.at[a, m, mask | bit], peer)
-
-    def x_recv(a, m, mask):
-        block = x_dst(a, m, fblock[mask])
-        return send(block, block, xs_s.at[a, m, mask, 0], xs_r.at[a, m, mask], other)
-
-    def x_start(a, m):
-        x_local(a, m).start()
-        for i, bit in reversed(bits_below(0, nf)):
-            x_send(a, m, 0, i, bit).start()
-
-    def x_relay(a, m):
-        for mask in order[1:]:
-            x_recv(a, m, mask).wait_recv()
-            for i, bit in bits_below(mask, nf):
-                x_send(a, m, mask, i, bit).start()
-
-    def x_done(a, m):
-        x_local(a, m).wait()
-        for mask in masks_of(nf):
-            for i, bit in bits_below(mask, nf):
-                x_send(a, m, mask, i, bit).wait_send()
-
-    def c_copies(which, m):
+    def x_src(a, m, who):
+        place = (m, micro)[who] if isinstance(who, int) else jnp.where(who == 0, m, micro)
+        return (act, att, up, dj)[a].at[place]
+
+    def x_local(a, m, who):
+        return pltpu.make_async_copy(
+            x_src(a, m, who), x_dst(a, m, who), xl_sem.at[a, m, who]
+        )
+
+    def x_send(a, m, who):
+        return send(
+            x_src(a, m, who), x_dst(a, m, who), xs_s.at[a, m, who], xs_r.at[a, m, who], sibling
+        )
+
+    def x_start(a, m, who):
+        x_local(a, m, who).start()
+        x_send(a, m, who).start()
+
+    def x_sent(a, m, who):
+        x_local(a, m, who).wait()
+        x_send(a, m, who).wait_send()
+
+    def c_pair(which, m, who):
         src, dst = ((xg, xc_x), (gr, gc_x))[which]
-        copies = []
-        for k in range(1, nf):
-            to = lax.rem(f + k, nf)
-            copies.append(
-                send(
-                    src.at[m, :, rows_at(to)],
-                    dst.at[m, f],
-                    ca_s.at[which, m, k],
-                    ca_r.at[which, m, k],
-                    {"fsdp": to},
-                )
-            )
-        return copies
-
-    def c_local(which, m):
-        src, dst = ((xg, xc_x), (gr, gc_x))[which]
-        return pltpu.make_async_copy(src.at[m, :, rows_at(f)], dst.at[m, f], cl_sem.at[which, m])
-
-    def c_start(which, m):
-        c_local(which, m).start()
-        for copy in c_copies(which, m):
+        block = x_block(who)
+        q = who * micro + m
+        mine = pltpu.make_async_copy(
+            src.at[q, :, rows_at(f)], dst.at[m, block], cl_sem.at[which, m, who]
+        )
+        theirs = send(
+            src.at[q, :, rows_at(fblock[1])],
+            dst.at[m, block],
+            ca_s.at[which, m, who],
+            ca_r.at[which, m, who],
+            sibling,
+        )
+        return mine, theirs
+
+    def c_start(which, m, who):
+        for copy in c_pair(which, m, who):
             copy.start()
 
-    def attention_masks(m):
+    def attention_masks(q):
         low = low_half(length)
         lane = lax.broadcasted_iota(jnp.int32, (length, LANES), 1)
-        tables = (rope[m, 0], rope[m, 1], rope[m, 2])
-        return low, lane, tables, allowed_mask(segc, segr, m, length)
+        tables = (rope[q, 0], rope[q, 1], lax.rem(lane, HEAD_DIM) < ROT_DIM // 2)
+        return low, lane, tables, allowed_of(q)
 
     factor = HEAD_DIM ** (-0.5)
 
-    def forward_stage(m, fresh):
-        for copy in ring.gather(xg, m, (ag_s, ag_r)):
-            copy.wait()
-        c_start(0, m)
+    def forward_stage(m, who, k, fresh):
+        q = who * micro + m
+        place = jnp.where(who == 0, m, micro)
+
+        @pl.when(who == 0)
+        def _():
+            for copy in ring.gather(xg, m, (ag_s, ag_r)):
+                copy.wait()
+            c_start(0, m, 0)
+
+            @pl.when(second | (k == 1))
+            def _():
+                mirror_copy(0, m).start()
+
+        @pl.when(who == 1)
+        def _():
+            mirror_copy(0, m).wait_recv()
+            c_start(0, m, 1)
+
+            @pl.when(m == 1)
+            def _():
+                x_sent(0, 0, 1)
+                x_sent(1, 0, 1)
 
         @pl.when(fresh)
         def _():
@@ -893,28 +950,28 @@
             w_start(2)
             w_start(3)
 
-        low, lane, tables, allowed = attention_masks(m)
+        low, lane, tables, allowed = attention_masks(q)
         for part in range(3):
             def qkv_tile(n, part=part):
                 at = cols(n)
-                acc = jnp.dot(xg[m], wq[part, :, at], preferred_element_type=F32)
+                acc = jnp.dot(xg[q], wq[part, :, at], preferred_element_type=F32)
                 acc = acc + wide[3 + part:4 + part, pl.ds(
                     pl.multiple_of(t * own + n * TILE, TILE), TILE)]
                 if part < 2:
                     acc = jnp.concatenate(
                         [
-                            turn(acc[:, c:c + LANES], tables, 1.0)
+                            twist(acc[:, c:c + LANES], tables, 1.0)
                             for c in range(0, TILE, LANES)
                         ],
                         axis=1,
                     )
-                qkv[m, part, :, at] = acc.astype(BF16)
+                qkv[q, part, :, at] = acc.astype(BF16)
 
             loop(own // TILE, qkv_tile)
 
         def pair(p):
             at = cols(p, LANES)
-            query, key, value = qkv[m, 0, :, at], qkv[m, 1, :, at], qkv[m, 2, :, at]
+            query, key, value = qkv[q, 0, :, at], qkv[q, 1, :, at], qkv[q, 2, :, at]
             outs = []
             for h in range(2):
                 mask = low if h == 0 else ~low
@@ -926,12 +983,16 @@
                 total = jnp.sum(e, axis=-1, keepdims=True)
                 probs = (e / total).astype(BF16)
                 outs.append(jnp.dot(probs, value, preferred_element_type=F32))
-                lse[m] = jnp.where(lane == 2 * p + h, top + jnp.log(total), lse[m])
-            att[m, :, at] = jnp.where(low, outs[0], outs[1]).astype(BF16)
-
-        lse[m] = jnp.zeros((length, LANES), F32)
+                lse[q] = jnp.where(lane == 2 * p + h, top + jnp.log(total), lse[q])
+            att[place, :, at] = jnp.where(low, outs[0], outs[1]).astype(BF16)
+
+        lse[q] = jnp.zeros((length, LANES), F32)
         loop(own // LANES, pair)
-        x_start(1, m)
+        x_start(1, m, who)
+
+        @pl.when(first & (k == 1))
+        def _():
+            output_finish(0)
 
         @pl.when(fresh)
         def _():
@@ -940,17 +1001,17 @@
 
         def up_tile(n):
             at = cols(n)
-            u = jnp.dot(xg[m], w1[:, at], preferred_element_type=F32) + fb[0:1, at]
+            u = jnp.dot(xg[q], w1[:, at], preferred_element_type=F32) + fb[0:1, at]
             c = 0.7978845608028654
             square = u * u
             th = jnp.tanh(c * u * (1.0 + 0.044715 * square))
-            act[m, :, at] = (0.5 * u * (1.0 + th)).astype(BF16)
+            act[place, :, at] = (0.5 * u * (1.0 + th)).astype(BF16)
             slope = 0.5 * (1.0 + th)
             slope = slope + 0.5 * u * (1.0 - th * th) * (c * (1.0 + 3 * 0.044715 * square))
-            gp[m, :, at] = slope.astype(BF16)
+            gp[q, :, at] = slope.astype(BF16)
 
         loop(hidden // TILE, up_tile)
-        x_start(0, m)
+        x_start(0, m, who)
 
     def output_stage(m, fresh):
         for mask in out_order:
@@ -970,41 +1031,59 @@
 
             loop(depth // TILE, out_tile)
 
-    def store_ends(src, m):
-        return pltpu.make_async_copy(src.at[m], ends_o.at[m], o_sem.at[m])
+        @pl.when(fresh)
+        def _():
+            mirror_copy(0, 0).start()
+
+    def store_ends(m):
+        return pltpu.make_async_copy(y_f.at[m], ends_o.at[m], o_sem.at[m])
 
     def output_finish(m):
         for copy in ring.scatter(out_bf, out_got, m, (rs_s, rs_r)):
             copy.wait()
         y = rin[m].astype(F32) + ring.total(out_bf, out_got, m) + wide[2:3, :]
-        y_b[m] = y.astype(BF16)
 
         @pl.when(first)
         def _():
+            y_b[m] = y.astype(BF16)
             hop_out(m).start()
 
         @pl.when(second)
         def _():
             y_f[m] = y
-            store_ends(y_f, m).start()
-
-    def backward_stage(m, k):
-        @pl.when(first)
+            store_ends(m).start()
+
+    def backward_stage(m, who, k):
+        q = who * micro + m
+        place = jnp.where(who == 0, m, micro)
+
+        @pl.when(first & (who == 0))
         def _():
             for copy in ring.gather(gr, m, (gg_s, gg_r)):
                 copy.wait()
-            c_start(1, m)
+            mirror_copy(1, m).start()
+            c_start(1, m, 0)
+
+        @pl.when(who == 1)
+        def _():
+            mirror_copy(1, m).wait_recv()
+            c_start(1, m, 1)
+
+            @pl.when(m == 1)
+            def _():
+                x_sent(2, 0, 1)
+                x_sent(3, 0, 1)
 
         def att_tile(n):
             at = cols(n)
-            gatt[:, at] = jnp.dot(gr[m], wo[:, at], preferred_element_type=F32).astype(BF16)
+            gatt[:, at] = jnp.dot(gr[q], wo[:, at], preferred_element_type=F32).astype(BF16)
 
         loop(own // TILE, att_tile)
-        low, lane, tables, allowed = attention_masks(m)
+        low, lane, tables, allowed = attention_masks(q)
 
         def pair(p):
             at = cols(p, LANES)
-            query, key, value = qkv[m, 0, :, at], qkv[m, 1, :, at], qkv[m, 2, :, at]
+            query, key, value = qkv[q, 0, :, at], qkv[q, 1, :, at], qkv[q, 2, :, at]
             grad = gatt[:, at]
             dqs, dks, dvs = [], [], []
             for h in range(2):
@@ -1013,7 +1092,7 @@
                 s = lax.dot_general(one, key, COLS, preferred_element_type=F32)
                 s = jnp.where(allowed, s * factor, -1e30)
                 log_total = jnp.sum(
-                    jnp.where(lane == 2 * p + h, lse[m], 0.0), axis=-1, keepdims=True
+                    jnp.where(lane == 2 * p + h, lse[q], 0.0), axis=-1, keepdims=True
                 )
                 soft = jnp.exp(s - log_total)
                 probs = soft.astype(BF16)
@@ -1026,33 +1105,36 @@
                 dks.append(lax.dot_general(ds, query, ROWS, preferred_element_type=F32))
             dq = jnp.where(low, dqs[0], dqs[1]) * factor
             dk = jnp.where(low, dks[0], dks[1]) * factor
-            dj[m, 0, :, at] = turn(dq, tables, -1.0).astype(BF16)
-            dj[m, 1, :, at] = turn(dk, tables, -1.0).astype(BF16)
-            dj[m, 2, :, at] = jnp.where(low, dvs[0], dvs[1]).astype(BF16)
+            dj[place, 0, :, at] = twist(dq, tables, -1.0).astype(BF16)
+            dj[place, 1, :, at] = twist(dk, tables, -1.0).astype(BF16)
+            dj[place, 2, :, at] = jnp.where(low, dvs[0], dvs[1]).astype(BF16)
 
         loop(own // LANES, pair)
-        x_start(3, m)
+        x_start(3, m, who)
 
         @pl.when(second & (k == 3))
         def _():
             backward_finish(0)
 
-        for part in range(3):
-            head_sums[part:part + 1, :] += jnp.sum(
-                dj[m, part].astype(F32), axis=0, keepdims=True
-            )
+        @pl.when(who == 0)
+        def _():
+            for part in range(3):
+                head_sums[part:part + 1, :] += jnp.sum(
+                    dj[m, part].astype(F32), axis=0, keepdims=True
+                )
 
         def up_tile(n):
             at = cols(n)
-            acc = jnp.dot(gr[m], w2[:, at], preferred_element_type=F32)
-            rounded = (acc * gp[m, :, at].astype(F32)).astype(BF16)
-            up[m, :, at] = rounded
-            up_sums[0:1, at] += jnp.sum(rounded.astype(F32), axis=0, keepdims=True)
+            acc = jnp.dot(gr[q], w2[:, at], preferred_element_type=F32)
+            rounded = (acc * gp[q, :, at].astype(F32)).astype(BF16)
+            up[place, :, at] = rounded
+            sums = jnp.sum(rounded.astype(F32), axis=0, keepdims=True)
+            up_sums[0:1, at] += jnp.where(who == 0, sums, 0.0)
 
         loop(hidden // TILE, up_tile)
-        x_start(2, m)
-
-        @pl.when(first & (k == 2))
+        x_start(2, m, who)
+
+        @pl.when(first & (k == 4))
         def _():
             hop_back(1).wait_recv()
             front_back(1)
@@ -1068,7 +1150,10 @@
             for copy in ring.scatter(in_bf, in_got, m, (rb_s, rb_r), at):
                 copy.start()
 
-        loop(width // TILE, norm_tile)
+        @pl.when(who == 0)
+        def _():
+            loop(width // TILE, norm_tile)
+
 
     def backward_finish(m):
         for copy in ring.scatter(in_bf, in_got, m, (rb_s, rb_r)):
@@ -1082,16 +1167,16 @@
             - jnp.mean(scaled, axis=-1, keepdims=True)
             - unit * jnp.mean(scaled * unit, axis=-1, keepdims=True)
         )
-        dx_b[m] = dx.astype(BF16)
 
         @pl.when(second)
         def _():
+            y_b[m] = dx.astype(BF16)
             hop_back(m).start()
 
         @pl.when(first)
         def _():
-            dx_f[m] = dx
-            store_ends(dx_f, m).start()
+            y_f[m] = dx
+            store_ends(m).start()
 
         for i, term in enumerate((grad_norm * unit, grad_norm, upstream)):
             own_sums[i:i + 1, :] += jnp.sum(term, axis=0, keepdims=True)
@@ -1109,6 +1194,12 @@
     def _():
         load_dy.wait()
         loop(micro, front_back)
+
+    seg_copy.wait()
+    loop(2 * micro, rope_of)
+
+    @pl.when(second)
+    def _():
         for mask in order:
             w_ready(0, mask)
         w_start(2)
@@ -1117,58 +1208,61 @@
             for mask in order:
                 w_ready(a, mask)
 
-        def columns_out(m):
+        def dy_out(m):
             for copy in ring.gather(gr, m, (gg_s, gg_r)):
                 copy.wait()
-            c_start(1, m)
-
-        loop(micro, columns_out)
+            mirror_copy(1, m).start()
+            c_start(1, m, 0)
+
+        loop(micro, dy_out)
 
     def slot(k):
-        is_f = jnp.where(first, k < 2, (k == 0) | (k == 2))
-        is_b = jnp.where(first, (k == 2) | (k == 3), (k == 1) | (k == 3))
-        is_o = jnp.where(first, k < 2, k >= 4)
+        is_f = jnp.where(first, k < 4, (k < 8) & (lax.rem(k, 2) == 0))
+        is_o = jnp.where(first, k < 2, (k == 5) | (k == 6))
+        who = jnp.where(first, (k // 2) % 2 * (k < 4) + lax.rem(k, 2) * (k >= 4), k // 4)
+        m = jnp.where(first, jnp.where(k < 4, lax.rem(k, 2), (k - 4) // 2), lax.rem(k // 2, 2))
+        m_o = jnp.where(first, m, k - 5)
         fresh = first & (k == 0)
-        m = jnp.where(first | (k >= 4), lax.rem(k, 2), k // 2)
-
-        @pl.when(second & (k < 2))
+
+        @pl.when(second & ((k == 0) | (k == 1)))
         def _():
             hop_out(k).wait_recv()
             front(k)
 
-        @pl.when(first & (k == 2))
-        def _():
-            for i in range(micro):
-                for a in (1, 0):
-                    x_relay(a, i)
+        @pl.when(first & (k == 4))
+        def _():
             hop_back(0).wait_recv()
             front_back(0)
 
         @pl.when(is_f)
         def _():
-            forward_stage(m, fresh)
+            forward_stage(m, who, k, fresh)
 
         @pl.when(is_o)
         def _():
-            output_stage(m, fresh)
-
-        @pl.when(is_b)
-        def _():
-            backward_stage(m, k)
-
-        @pl.when((first & (k == 1)) | (second & (k == 5)))
+            output_stage(m_o, fresh)
+
+        @pl.when(jnp.logical_not(is_f))
+        def _():
+            backward_stage(m, who, k)
+
+        @pl.when(first & (k == 2))
+        def _():
+            output_finish(1)
+
+        @pl.when(first & (k == 6))
+        def _():
+            backward_finish(0)
+
+        @pl.when((first & (k == 7)) | (second & (k == 4)))
+        def _():
+            backward_finish(1)
+
+        @pl.when(second & (k == 7))
         def _():
             loop(micro, output_finish)
 
-        @pl.when(first & (k == 3))
-        def _():
-            backward_finish(0)
-
-        @pl.when(k == 3)
-        def _():
-            backward_finish(1)
-
-    loop(6, slot)
+    loop(8, slot)
 
     s_src[...] = jnp.zeros_like(s_src)
     for j in range(count):
@@ -1186,15 +1280,11 @@
 
     @pl.when(second)
     def _():
-        for a, m in ((1, 0), (0, 0), (3, 0), (2, 0), (1, 1), (0, 1), (3, 1), (2, 1)):
-            x_relay(a, m)
         for m in range(micro):
             hop_back(m).wait_send()
 
     @pl.when(first)
     def _():
-        for a, m in ((3, 0), (2, 0), (3, 1), (2, 1)):
-            x_relay(a, m)
         for m in range(micro):
             hop_out(m).wait_send()
 
@@ -1204,20 +1294,25 @@
         total = total + s_got[k + 1]
     sums_o[...] = total
     for m in range(micro):
-        for a in range(4):
-            x_done(a, m)
+        for who in range(2):
+            for a in range(4):
+                if (m, who) != (0, 1):
+                    x_sent(a, m, who)
+                x_send(a, m, who).wait_recv()
+            for which in range(2):
+                mine, theirs = c_pair(which, m, who)
+                mine.wait()
+                theirs.wait()
         for which in range(2):
-            c_local(which, m).wait()
-            for copy in c_copies(which, m):
-                copy.wait()
-        store_ends(y_f, m).wait()
+            mirror_copy(which, m).wait_send()
+        store_ends(m).wait()
     for a in range(4):
         for mask in masks_of(nf):
             for i, bit in bits_below(mask, nf):
                 w_send(a, mask, i, bit).wait_send()
 
 
-def fused(ends, pack, wq, wo, w1, w2, rope, segc, segr, nf, nt):
+def fused(ends, smalls, segments, wq, wo, w1, w2, nf, nt):
     micro, per, width = ends.shape
     length = per * nt
     own, hidden = wo.shape[1], w1.shape[1]
@@ -1228,11 +1323,12 @@
     inside = pl.BlockSpec(memory_space=pltpu.VMEM)
     dma = pltpu.SemaphoreType.DMA
     vm = pltpu.VMEM
-    small = (count,) + pack.shape
-    tokens = (micro, length)
+    piece = (ROWS_OF_PACK, LANES)
+    packs = 2 * micro
+    some = micro + 1
     out_shape = [
         jax.ShapeDtypeStruct(ends.shape, F32),
-        jax.ShapeDtypeStruct(pack.shape, F32),
+        jax.ShapeDtypeStruct(piece, F32),
         jax.ShapeDtypeStruct((micro, nf, length, hidden), BF16),
         jax.ShapeDtypeStruct((micro, nf, length, own), BF16),
         jax.ShapeDtypeStruct((micro, nf, length, hidden), BF16),
@@ -1243,38 +1339,40 @@
     scratch = [
         vm((3, width, own), BF16), vm((width, own), BF16),
         vm((width, hidden), BF16), vm((width, hidden), BF16),
-        vm(small, F32), vm((pack.shape[0], width), F32), vm((8, hidden), F32),
+        vm(piece, F32), vm((count,) + piece, F32),
+        vm((ROWS_OF_PACK, width), F32), vm((8, hidden), F32),
+        vm((2, 8, length), F32), vm((packs, 2, length, LANES), F32),
         vm(ends.shape, BF16), vm(ends.shape, BF16),
-        vm(tokens + (width,), BF16), vm((micro, 3, length, own), BF16),
-        vm(tokens + (LANES,), F32), vm(tokens + (own,), BF16),
-        vm(tokens + (hidden,), BF16), vm(tokens + (hidden,), BF16),
-        vm(tokens + (width,), BF16), vm((length, own), BF16),
-        vm(tokens + (hidden,), BF16), vm((micro, 3, length, own), BF16),
-        vm(tokens + (width,), BF16), vm((micro, nt, per, width), BF16),
-        vm(tokens + (width,), BF16), vm((micro, nt, per, width), BF16),
-        vm(ends.shape, F32), vm(ends.shape, BF16),
+        vm((packs, length, width), BF16), vm((packs, 3, length, own), BF16),
+        vm((packs, length, LANES), F32), vm((some, length, own), BF16),
+        vm((packs, length, hidden), BF16), vm((some, length, hidden), BF16),
+        vm((packs, length, width), BF16), vm((length, own), BF16),
+        vm((some, length, hidden), BF16), vm((some, 3, length, own), BF16),
+        vm((micro, length, width), BF16), vm((micro, nt - 1, per, width), BF16),
+        vm((micro, length, width), BF16), vm((micro, nt - 1, per, width), BF16),
         vm(ends.shape, F32), vm(ends.shape, BF16),
         vm((8, width), F32), vm((8, own), F32), vm((8, hidden), F32),
-        vm(small, F32), vm(small, F32),
+        vm((count,) + piece, F32), vm((count,) + piece, F32),
         dma, dma((4,)), dma((4, nf, bits)), dma((4, nf)),
         dma((count,)), dma((count,)), dma((count,)), dma((count,)),
         dma((micro, nt)), dma((micro, nt)), dma((micro, nt)), dma((micro, nt)),
         dma((micro, nt)), dma((micro, nt)), dma((micro, nt)), dma((micro, nt)),
         dma((micro,)), dma((micro,)), dma((micro,)), dma((micro,)),
-        dma((4, micro)), dma((4, micro, nf, bits)), dma((4, micro, nf)),
-        dma((2, micro)), dma((2, micro, nf)), dma((2, micro, nf)), dma((micro,)),
+        dma((4, micro, 2)), dma((4, micro, 2)), dma((4, micro, 2)),
+        dma((2, micro, 2)), dma((2, micro, 2)), dma((2, micro, 2)),
+        dma((3, micro)), dma((3, micro)), dma((micro,)),
     ]
     return pl.pallas_call(
         functools.partial(fused_kernel, nf, nt),
         out_shape=out_shape,
-        in_specs=[anywhere, inside] + [anywhere] * 4 + [inside] * 3,
+        in_specs=[anywhere] + [inside] * 7 + [anywhere] * 4,
         out_specs=[anywhere, inside] + [anywhere] * 6,
         scratch_shapes=scratch,
         compiler_params=pltpu.CompilerParams(
             collective_id=4, has_side_effects=True, vmem_limit_bytes=VMEM_LIMIT
         ),
         name="fused",
-    )(ends, pack, wq, wo, w1, w2, rope, segc, segr)
+    )(ends, *smalls, segments, wq, wo, w1, w2)
 
 
 def padded(flat):
@@ -1379,17 +1477,11 @@
     bias_qkv, bias_out, bias_fc1, bias_fc2,
 ):
     nf, nt = lax.axis_size("fsdp"), lax.axis_size("tp")
-    pack = jnp.concatenate(
-        [
-            ln_gain, ln_bias, (bias_out.astype(F32) + bias_fc2.astype(F32)),
-            bias_qkv[0], bias_fc1[0].reshape(-1, LANES),
-        ]
-    ).astype(F32)
-    used = pack.shape[0]
-    pack = jnp.pad(pack, ((0, ROWS_OF_PACK - used), (0, 0)))
+    used = 6 + bias_fc1.shape[1] // LANES
     ends_out, sums, act_x, att_x, up_x, dj_x, xc, gc = fused(
-        ends_in[0], pack, w_qkv[0].transpose(1, 0, 2), w_out[0], w_fc1[0], w_fc2[0],
-        rope_tables(segments), segments[:, :, None], segments[:, None, :], nf, nt,
+        ends_in[0],
+        (ln_gain, ln_bias, bias_out, bias_fc2, bias_qkv[0], bias_fc1),
+        segments, w_qkv[0].transpose(1, 0, 2), w_out[0], w_fc1[0], w_fc2[0], nf, nt,
     )
 
     def product(left, right):
@@ -1421,7 +1513,8 @@
     rows, piece = args[0].shape[2], args[2].shape[1]
     small = rows * lax.axis_size("tp") <= 256
     tidy = piece == LANES and args[10].shape[1] // LANES <= ROWS_OF_PACK - 6
-    return (fused_shards if small and tidy else split_shards)(*args)
+    square = lax.axis_size("fsdp") == 4 and args[0].shape[1] == 2
+    return (fused_shards if small and tidy and square else split_shards)(*args)
 
 
 def solution(mesh):

time: 455 us -> 392 us (0.86); the launches traced: 448 us -> 392 us
  Pallas kernels: 404 us -> 359 us
  other arithmetic: 8.83 us -> 1.97 us
  local copies, waits for them, and re-layouts: 10.5 us -> 5.94 us
    pallas_call x1, Pallas kernels: 404 us -> 359 us  [fused(): pl.pallas_call(functools.partial(fused_kernel, nf, nt), out_shape=out_sha...]
where the time goes in v3:
time: 392 us
  Pallas kernels  359 us (92%)
  matrix products  24.5 us (6%)
  local copies, waits for them, and re-layouts  5.94 us (2%)
    pallas_call x1, Pallas kernels, fused(): pl.pallas_call(functools.partial(fused_kernel, nf, nt), out_shape=out_sha...  359 us
    dot_general x6, matrix products, product(): return lax.dot_general(left, right, ROWS, preferred_element_type=F32)  24.5 us

profile of v3, /device:TPU:0, one launch (start us, length us, event | category | flops | bytes accessed | tf_op | source)
XLA Modules:
  0.0 392.2 jit_solution(4533609143930807379)
XLA Ops:
  0.6 359.1 %fused.1 = (f32[2,64,2048]{2,1,0:T(8,128)}, f32[16,128]{1,0:T(8,128)}, bf16[2,4,256,2048]{3,2,1,0:T(8,128)(2,1)}, bf16[2,4,256,512]{3,2,1,0:T(8,128)(2,1)}, bf16...) custom-call(bf16[2,64,2048]{2,1,0:T(8,128)(2,1)} %bitcast.63, ...), custom_call_target="tpu_custom_call" | custom-call | tf_op jit(solution)/shard_map/fused/pallas_call | solution.py:1365
  359.8 1.3 fusion.1
  361.1 0.0 copy-start.2
  361.1 0.7 slice_bitcast_fusion
  361.7 1.3 slice.31
  363.0 0.6 copy.26
  363.6 0.0 copy-start
  363.6 4.6 %convolution_bitcast_fusion.2 = f32[1,512,512]{2,1,0:T(8,128)} fusion(bf16[2,4,256,512]{3,2,1,0:T(8,128)(2,1)} %get-tuple-element.23, bf16[2,4,256,512]{3,2,1,0:T(8,128)(2,1)} %get-tuple-element.24), kind=kOutput, calls=%fused_computation.3 | convolution fusion | flops 1073741824 | bytes 5242880 | tf_op jit(solution)/shard_map/dot_general | solution.py:1490
  368.2 0.0 copy-done
  368.2 0.0 copy-start.3
  368.2 0.0 copy-start.4
  368.2 0.0 slice-start
  368.2 9.8 %convolution_bitcast_fusion = f32[1,512,2048]{2,1,0:T(8,128)} fusion(bf16[2,4,256,512]{3,2,1,0:T(8,128)(2,1)S(1)} %copy-done, bf16[2,4,256,2048]{3,2,1,0:T(8,128)(2,1)} %get-tuple-element.26), kind=kOutput, calls=%fused_computation | convolution fusion | flops 4294967296 | bytes 14680064 | tf_op jit(solution)/shard_map/dot_general | solution.py:1490
  378.0 0.0 copy-done.3
  378.0 0.0 copy-done.4
  378.0 0.0 slice-start.1
  378.0 6.2 %convolution_bitcast_fusion.1 = f32[1,512,2048]{2,1,0:T(8,128)} fusion(bf16[2,4,256,512]{3,2,1,0:T(8,128)(2,1)S(1)} %copy-done.4, bf16[2,4,256,2048]{3,2,1,0:T(8,128)(2,1)S(1)} %copy-done.3), kind=kOutput, calls=%fused_computation.1 | convolution fusion | flops 4294967296 | bytes 14680064 | tf_op jit(solution)/shard_map/dot_general | solution.py:1490
  384.2 0.0 slice-done
  384.2 0.0 slice-done.1
  384.2 0.6 fusion
  384.8 1.3 convolution_bitcast_fusion.5
  386.1 1.3 convolution_bitcast_fusion.3
  387.4 1.3 convolution_bitcast_fusion.4
  388.7 0.0 copy-start.1
  388.7 2.0 maximum_bitcast_fusion
  390.7 0.0 copy-done.2
  390.7 0.5 copy.35
  391.2 0.0 copy-done.1
  391.2 1.0 copy.36
  (1 shorter events, 0.0 us)
Async XLA Ops:
  361.1 29.6 %copy-start.2 = (f32[1,128]{1,0:T(1,128)}, f32[1,128]{1,0:T(1,128)S(1)}, u32[]{:S(2)}) copy-start(f32[1,128]{1,0:T(1,128)S(1)} %get-tuple-element.85) | copy-start | bytes 1540
  363.6 4.6 %copy-start = (bf16[2,4,256,512]{3,2,1,0:T(8,128)(2,1)S(1)}, bf16[2,4,256,512]{3,2,1,0:T(8,128)(2,1)}, u32[]{:S(2)}) copy-start(bf16[2,4,256,512]{3,2,1,0:T(8,128)(2,1)} %get-tuple-element.23) | copy-start | bytes 6291460
  368.2 9.8 %copy-start.3 = (bf16[2,4,256,2048]{3,2,1,0:T(8,128)(2,1)S(1)}, bf16[2,4,256,2048]{3,2,1,0:T(8,128)(2,1)}, u32[]{:S(2)}) copy-start(bf16[2,4,256,2048]{3,2,1,0:T(8,128)(2,1)} %get-tuple-element.25) | copy-start | bytes 25165828
  368.2 9.8 %copy-start.4 = (bf16[2,4,256,512]{3,2,1,0:T(8,128)(2,1)S(1)}, bf16[2,4,256,512]{3,2,1,0:T(8,128)(2,1)}, u32[]{:S(2)}) copy-start(bf16[2,4,256,512]{3,2,1,0:T(8,128)(2,1)} %get-tuple-element.21) | copy-start | bytes 6291460
  368.2 16.0 %slice-start = ((s8[6291456]{0:T(1024)(128)(4,1)}), s8[4194304]{0:T(1024)(128)(4,1)S(1)}, s32[]{:S(2)}) async-start(s8[6291456]{0:T(1024)(128)(4,1)} %bitcast.54), calls=%async_computation | async-start | bytes 8388608
  378.0 6.2 %slice-start.1 = ((s8[6291456]{0:T(1024)(128)(4,1)}), s8[2097152]{0:T(1024)(128)(4,1)S(1)}, s32[]{:S(2)}) async-start(s8[6291456]{0:T(1024)(128)(4,1)} %bitcast.54), calls=%async_computation.1 | async-start | bytes 4194304
  388.7 2.5 copy-start.1

commit v4 on v3

--- a/solution.py
+++ b/solution.py
@@ -681,6 +681,7 @@
 
 
 ROWS_OF_PACK = 16
+PIECES = 4
 
 
 def twist(x, tables, sign):
@@ -716,6 +717,7 @@
     in_sem, wl_sem, ws_sem, wr_sem, pk_s, pk_r, sm_s, sm_r,
     ag_s, ag_r, gg_s, gg_r, rs_s, rs_r, rb_s, rb_r, hx_s, hx_r, hb_s, hb_r,
     xl_sem, xs_s, xs_r, cl_sem, ca_s, ca_r, mx_s, mx_r, o_sem,
+    l1_s, l1_r, l2_s, l2_r, fw_s, fw_r, go_sem,
 ):
     micro, per, width = rin.shape
     length = per * nt
@@ -727,6 +729,7 @@
     mirror, sibling = {"fsdp": flipped(f, 2, nf)}, {"fsdp": flipped(f, 1, nf)}
     count = nf * nt
     other = {"section": 1 - section}
+    across = {"section": 1 - section, "fsdp": flipped(f, 2, nf)}
     me, group = group_peers(nf, nt)
     fblock = [flipped(f, mask, nf) for mask in masks_of(nf)]
 
@@ -744,7 +747,7 @@
     def _():
         load_dy.start()
 
-    greet([peer for _, _, peer in group] + [other])
+    greet([peer for _, _, peer in group] + [other, across])
 
     per_row = hidden // nf // LANES
     segs[0] = jnp.zeros((8, length), F32)
@@ -784,10 +787,44 @@
         block = w_at(table[a][1], fblock[mask])
         return send(block, block, ws_sem.at[a, mask, 0], wr_sem.at[a, mask], other)
 
-    def w_start(a):
+    def w_near(a):
         w_local(a).start()
-        for i, bit in reversed(bits_below(0, nf)):
-            w_send(a, 0, i, bit).start()
+        w_send(a, 0, 0, 1).start()
+
+    def w_far(a):
+        w_send(a, 0, 1, 2).start()
+
+    part_rows = depth // PIECES
+    per_slot = length // part_rows
+
+    def stage(p):
+        return up.at[p // per_slot, pl.ds(p % per_slot * part_rows, part_rows), :]
+
+    def piece_at(a, mask, p):
+        start = pl.multiple_of(fblock[mask] * depth + p * part_rows, part_rows)
+        return table[a][1].at[pl.ds(start, part_rows), :]
+
+    def leg_one(a, p):
+        src = table[a][0].at[pl.ds(p * part_rows, part_rows), :]
+        return send(src, stage(p), l1_s.at[p], l1_r.at[p], across)
+
+    def leg_two(a, p):
+        return send(stage(p), piece_at(a, 2, p), l2_s.at[p], l2_r.at[p], other)
+
+    def passed_on(a, mask, p):
+        block = piece_at(a, mask, p)
+        return send(block, block, fw_s.at[p], fw_r.at[p], sibling)
+
+    def relay(a, p):
+        leg_one(a, p).wait_recv()
+        leg_two(a, p).start()
+
+    def via_ready(a):
+        for p in range(PIECES):
+            leg_two(a, p).wait_recv()
+            passed_on(a, 2, p).start()
+        for p in range(PIECES):
+            passed_on(a, 3, p).wait_recv()
 
     def w_ready(a, mask):
         if mask == 0:
@@ -799,18 +836,26 @@
 
     order = sorted(masks_of(nf), key=lambda m: (m != 0, -(m & -m), m))
     out_order = list(masks_of(nf))
-    w_start(0)
-    w_start(1)
-
-    pack_local.wait()
-    for copy in pack_copies:
-        copy.wait()
-    for j in range(count):
-        wide[:, j * LANES:(j + 1) * LANES] = packs[j]
-    for j in range(nf):
-        for r in range(per_row):
-            c = (j * per_row + r) * LANES
-            fb[0:1, c:c + LANES] = packs[t * nf + j, 6 + r:7 + r, :]
+    for a in range(4):
+        w_near(a)
+
+    @pl.when(first)
+    def _():
+        w_far(0)
+        w_far(2)
+        for p in range(PIECES):
+            leg_one(1, p).start()
+
+    def small_arrive():
+        pack_local.wait()
+        for copy in pack_copies:
+            copy.wait()
+        for j in range(count):
+            wide[:, j * LANES:(j + 1) * LANES] = packs[j]
+        for j in range(nf):
+            for r in range(per_row):
+                c = (j * per_row + r) * LANES
+                fb[0:1, c:c + LANES] = packs[t * nf + j, 6 + r:7 + r, :]
 
     def segment_parts(q):
         row = segs[q // micro, pl.ds(lax.rem(q, micro), 1), :]
@@ -929,7 +974,7 @@
                 copy.wait()
             c_start(0, m, 0)
 
-            @pl.when(second | (k == 1))
+            @pl.when(second)
             def _():
                 mirror_copy(0, m).start()
 
@@ -947,8 +992,7 @@
         def _():
             for mask in order:
                 w_ready(0, mask)
-            w_start(2)
-            w_start(3)
+            w_far(3)
 
         low, lane, tables, allowed = attention_masks(q)
         for part in range(3):
@@ -993,11 +1037,20 @@
         @pl.when(first & (k == 1))
         def _():
             output_finish(0)
+            relay(3, 0)
+
+        @pl.when(k == 0)
+        def _():
+            w_ready(1, 0)
+            w_ready(1, 1)
 
         @pl.when(fresh)
         def _():
-            for mask in order:
-                w_ready(1, mask)
+            via_ready(1)
+
+        @pl.when(second & (k == 0))
+        def _():
+            w_ready(1, 3)
 
         def up_tile(n):
             at = cols(n)
@@ -1033,7 +1086,7 @@
 
         @pl.when(fresh)
         def _():
-            mirror_copy(0, 0).start()
+            pl.semaphore_signal(go_sem, inc=1, device_id=other, device_id_type=MESH)
 
     def store_ends(m):
         return pltpu.make_async_copy(y_f.at[m], ends_o.at[m], o_sem.at[m])
@@ -1112,16 +1165,18 @@
         loop(own // LANES, pair)
         x_start(3, m, who)
 
-        @pl.when(second & (k == 3))
-        def _():
-            backward_finish(0)
-
         @pl.when(who == 0)
         def _():
             for part in range(3):
                 head_sums[part:part + 1, :] += jnp.sum(
                     dj[m, part].astype(F32), axis=0, keepdims=True
                 )
+
+        @pl.when(second & (k == 1))
+        def _():
+            w_ready(3, 0)
+            w_ready(3, 1)
+            via_ready(3)
 
         def up_tile(n):
             at = cols(n)
@@ -1133,6 +1188,10 @@
 
         loop(hidden // TILE, up_tile)
         x_start(2, m, who)
+
+        @pl.when(second & (k == 3))
+        def _():
+            backward_finish(0)
 
         @pl.when(first & (k == 4))
         def _():
@@ -1187,34 +1246,41 @@
 
     @pl.when(first)
     def _():
+        small_arrive()
         load_rows.wait()
         loop(micro, front)
+        seg_copy.wait()
+        loop(2 * micro, rope_of)
 
     @pl.when(second)
     def _():
         load_dy.wait()
         loop(micro, front_back)
 
-    seg_copy.wait()
-    loop(2 * micro, rope_of)
-
     @pl.when(second)
     def _():
+        for p in range(PIECES):
+            relay(1, p)
+        w_far(0)
+        w_far(1)
+        small_arrive()
+        seg_copy.wait()
+        loop(2 * micro, rope_of)
         for mask in order:
             w_ready(0, mask)
-        w_start(2)
-        w_start(3)
-        for a in (1, 2, 3):
-            for mask in order:
-                w_ready(a, mask)
-
-        def dy_out(m):
+        w_far(2)
+        for p in range(PIECES):
+            leg_two(1, p).wait_send()
+        pl.semaphore_wait(go_sem, 1)
+        for p in range(PIECES):
+            leg_one(3, p).start()
+
+        def dy_in(m):
             for copy in ring.gather(gr, m, (gg_s, gg_r)):
                 copy.wait()
-            mirror_copy(1, m).start()
             c_start(1, m, 0)
 
-        loop(micro, dy_out)
+        loop(micro, dy_in)
 
     def slot(k):
         is_f = jnp.where(first, k < 4, (k < 8) & (lax.rem(k, 2) == 0))
@@ -1229,8 +1295,21 @@
             hop_out(k).wait_recv()
             front(k)
 
+        @pl.when(second & (k == 0))
+        def _():
+            w_ready(1, 2)
+
+        @pl.when(second & (k == 1))
+        def _():
+            for i in range(micro):
+                mirror_copy(1, i).start()
+            for mask in order:
+                w_ready(2, mask)
+
         @pl.when(first & (k == 4))
         def _():
+            for p in range(PIECES):
+                leg_two(3, p).wait_send()
             hop_back(0).wait_recv()
             front_back(0)
 
@@ -1246,11 +1325,16 @@
         def _():
             backward_stage(m, who, k)
 
-        @pl.when(first & (k == 2))
-        def _():
+        @pl.when(first & (k == 1))
+        def _():
+            relay(3, 1)
+            relay(3, 2)
             output_finish(1)
-
-        @pl.when(first & (k == 6))
+            relay(3, 3)
+            for i in range(micro):
+                mirror_copy(0, i).start()
+
+        @pl.when(first & (k == 7))
         def _():
             backward_finish(0)
 
@@ -1307,9 +1391,17 @@
             mirror_copy(which, m).wait_send()
         store_ends(m).wait()
     for a in range(4):
-        for mask in masks_of(nf):
-            for i, bit in bits_below(mask, nf):
-                w_send(a, mask, i, bit).wait_send()
+        w_send(a, 0, 0, 1).wait_send()
+    for side, via in ((first, 1), (second, 3)):
+        @pl.when(side)
+        def _(via=via):
+            for a in range(4):
+                if a != via:
+                    w_send(a, 0, 1, 2).wait_send()
+                    w_send(a, 2, 0, 1).wait_send()
+            for p in range(PIECES):
+                leg_one(via, p).wait_send()
+                passed_on(via, 2, p).wait_send()
 
 
 def fused(ends, smalls, segments, wq, wo, w1, w2, nf, nt):
@@ -1361,6 +1453,8 @@
         dma((4, micro, 2)), dma((4, micro, 2)), dma((4, micro, 2)),
         dma((2, micro, 2)), dma((2, micro, 2)), dma((2, micro, 2)),
         dma((3, micro)), dma((3, micro)), dma((micro,)),
+        dma((PIECES,)), dma((PIECES,)), dma((PIECES,)), dma((PIECES,)),
+        dma((PIECES,)), dma((PIECES,)), pltpu.SemaphoreType.REGULAR,
     ]
     return pl.pallas_call(
         functools.partial(fused_kernel, nf, nt),

time: 392 us -> 356 us (0.908)
  Pallas kernels: 359 us -> 322 us
    pallas_call x1, Pallas kernels: 359 us -> 322 us  [fused(): pl.pallas_call(functools.partial(fused_kernel, nf, nt), out_shape=out_sha...]
where the time goes in v4:
time: 356 us; the launch traced here: 355 us
  Pallas kernels  322 us (90%)
  matrix products  24.5 us (7%)
  local copies, waits for them, and re-layouts  5.94 us (2%)
    pallas_call x1, Pallas kernels, fused(): pl.pallas_call(functools.partial(fused_kernel, nf, nt), out_shape=out_sha...  322 us
    dot_general x6, matrix products, product(): return lax.dot_general(left, right, ROWS, preferred_element_type=F32)  24.5 us

profile of v4, /device:TPU:0, one launch (start us, length us, event | category | flops | bytes accessed | tf_op | source)
XLA Modules:
  0.0 355.3 jit_solution(10555713599811977145)
XLA Ops:
  0.6 322.2 %fused.1 = (f32[2,64,2048]{2,1,0:T(8,128)}, f32[16,128]{1,0:T(8,128)}, bf16[2,4,256,2048]{3,2,1,0:T(8,128)(2,1)}, bf16[2,4,256,512]{3,2,1,0:T(8,128)(2,1)}, bf16...) custom-call(bf16[2,64,2048]{2,1,0:T(8,128)(2,1)} %bitcast.63, ...), custom_call_target="tpu_custom_call" | custom-call | tf_op jit(solution)/shard_map/fused/pallas_call | solution.py:1459
  322.9 1.3 fusion.1
  324.2 0.0 copy-start.2
  324.2 0.7 slice_bitcast_fusion
  324.9 1.3 slice.31
  326.1 0.6 copy.26
  326.7 0.0 copy-start
  326.7 4.6 %convolution_bitcast_fusion.2 = f32[1,512,512]{2,1,0:T(8,128)} fusion(bf16[2,4,256,512]{3,2,1,0:T(8,128)(2,1)} %get-tuple-element.23, bf16[2,4,256,512]{3,2,1,0:T(8,128)(2,1)} %get-tuple-element.24), kind=kOutput, calls=%fused_computation.3 | convolution fusion | flops 1073741824 | bytes 5242880 | tf_op jit(solution)/shard_map/dot_general | solution.py:1584
  331.3 0.0 copy-done
  331.3 0.0 copy-start.3
  331.3 0.0 copy-start.4
  331.3 0.0 slice-start
  331.3 9.8 %convolution_bitcast_fusion = f32[1,512,2048]{2,1,0:T(8,128)} fusion(bf16[2,4,256,512]{3,2,1,0:T(8,128)(2,1)S(1)} %copy-done, bf16[2,4,256,2048]{3,2,1,0:T(8,128)(2,1)} %get-tuple-element.26), kind=kOutput, calls=%fused_computation | convolution fusion | flops 4294967296 | bytes 14680064 | tf_op jit(solution)/shard_map/dot_general | solution.py:1584
  341.1 0.0 copy-done.3
  341.1 0.0 copy-done.4
  341.1 0.0 slice-start.1
  341.1 6.2 %convolution_bitcast_fusion.1 = f32[1,512,2048]{2,1,0:T(8,128)} fusion(bf16[2,4,256,512]{3,2,1,0:T(8,128)(2,1)S(1)} %copy-done.4, bf16[2,4,256,2048]{3,2,1,0:T(8,128)(2,1)S(1)} %copy-done.3), kind=kOutput, calls=%fused_computation.1 | convolution fusion | flops 4294967296 | bytes 14680064 | tf_op jit(solution)/shard_map/dot_general | solution.py:1584
  347.3 0.0 slice-done
  347.3 0.0 slice-done.1
  347.3 0.6 fusion
  347.9 1.3 convolution_bitcast_fusion.5
  349.2 1.3 convolution_bitcast_fusion.3
  350.5 1.3 convolution_bitcast_fusion.4
  351.8 0.0 copy-start.1
  351.8 2.0 maximum_bitcast_fusion
  353.8 0.0 copy-done.2
  353.8 0.5 copy.35
  354.3 0.0 copy-done.1
  354.3 1.0 copy.36
  (1 shorter events, 0.0 us)
Async XLA Ops:
  324.2 29.6 %copy-start.2 = (f32[1,128]{1,0:T(1,128)}, f32[1,128]{1,0:T(1,128)S(1)}, u32[]{:S(2)}) copy-start(f32[1,128]{1,0:T(1,128)S(1)} %get-tuple-element.85) | copy-start | bytes 1540
  326.7 4.6 %copy-start = (bf16[2,4,256,512]{3,2,1,0:T(8,128)(2,1)S(1)}, bf16[2,4,256,512]{3,2,1,0:T(8,128)(2,1)}, u32[]{:S(2)}) copy-start(bf16[2,4,256,512]{3,2,1,0:T(8,128)(2,1)} %get-tuple-element.23) | copy-start | bytes 6291460
  331.3 9.8 %copy-start.3 = (bf16[2,4,256,2048]{3,2,1,0:T(8,128)(2,1)S(1)}, bf16[2,4,256,2048]{3,2,1,0:T(8,128)(2,1)}, u32[]{:S(2)}) copy-start(bf16[2,4,256,2048]{3,2,1,0:T(8,128)(2,1)} %get-tuple-element.25) | copy-start | bytes 25165828
  331.3 9.8 %copy-start.4 = (bf16[2,4,256,512]{3,2,1,0:T(8,128)(2,1)S(1)}, bf16[2,4,256,512]{3,2,1,0:T(8,128)(2,1)}, u32[]{:S(2)}) copy-start(bf16[2,4,256,512]{3,2,1,0:T(8,128)(2,1)} %get-tuple-element.21) | copy-start | bytes 6291460
  331.3 16.0 %slice-start = ((s8[6291456]{0:T(1024)(128)(4,1)}), s8[4194304]{0:T(1024)(128)(4,1)S(1)}, s32[]{:S(2)}) async-start(s8[6291456]{0:T(1024)(128)(4,1)} %bitcast.54), calls=%async_computation | async-start | bytes 8388608
  341.1 6.2 %slice-start.1 = ((s8[6291456]{0:T(1024)(128)(4,1)}), s8[2097152]{0:T(1024)(128)(4,1)S(1)}, s32[]{:S(2)}) async-start(s8[6291456]{0:T(1024)(128)(4,1)} %bitcast.54), calls=%async_computation.1 | async-start | bytes 4194304
  351.8 2.5 copy-start.1

commit v5 on v4

--- a/solution.py
+++ b/solution.py
@@ -681,7 +681,11 @@
 
 
 ROWS_OF_PACK = 16
-PIECES = 4
+PIECES = 8
+DIRECT = 2
+LINE_SUMS = False
+LINE_ROWS = False
+WIDE = 512
 
 
 def twist(x, tables, sign):
@@ -717,7 +721,8 @@
     in_sem, wl_sem, ws_sem, wr_sem, pk_s, pk_r, sm_s, sm_r,
     ag_s, ag_r, gg_s, gg_r, rs_s, rs_r, rb_s, rb_r, hx_s, hx_r, hb_s, hb_r,
     xl_sem, xs_s, xs_r, cl_sem, ca_s, ca_r, mx_s, mx_r, o_sem,
-    l1_s, l1_r, l2_s, l2_r, fw_s, fw_r, go_sem,
+    l1_s, l1_r, l2_s, l2_r, fw_s, fw_r, go_sem, nb, wide_b, mf_s, mb_s, wb_sem,
+    out_via, in_via, rv_s, rv_r, bv_s, bv_r,
 ):
     micro, per, width = rin.shape
     length = per * nt
@@ -747,7 +752,11 @@
     def _():
         load_dy.start()
 
-    greet([peer for _, _, peer in group] + [other, across])
+    greet(
+        [peer for _, _, peer in group]
+        + [across, other]
+        + [{"section": 1 - section, "tp": to} for _, to in ring.others]
+    )
 
     per_row = hidden // nf // LANES
     segs[0] = jnp.zeros((8, length), F32)
@@ -815,6 +824,10 @@
         block = piece_at(a, mask, p)
         return send(block, block, fw_s.at[p], fw_r.at[p], sibling)
 
+    def straight(p):
+        src = table[3][0].at[pl.ds(p * part_rows, part_rows), :]
+        return send(src, piece_at(3, 0, p), l1_s.at[p], l2_r.at[p], mirror)
+
     def relay(a, p):
         leg_one(a, p).wait_recv()
         leg_two(a, p).start()
@@ -887,17 +900,108 @@
     def hop_back(m):
         return send(y_b.at[m], dyr.at[m], hb_s.at[m], hb_r.at[m], other)
 
+    line = LINE_SUMS and nt == 4
+    line_rows = LINE_ROWS and nt == 4
+    inner = (t == 1) | (t == 2)
+    far_end = jnp.where(t == 1, 3, 0)
+    near_end = jnp.where(t == 1, 0, 3)
+
+    def is_far(a, b, on=line):
+        return (jnp.abs(a - b) == nt - 1) if on else False
+
+    def unless(flag, do):
+        if flag is False:
+            do()
+        else:
+            pl.when(jnp.logical_not(flag))(do)
+
+    def spread(buf, m, send_sems, recv_sems):
+        here = ring.block(t)
+        return [
+            (
+                is_far(t, to, line_rows),
+                send(
+                    buf.at[m, here], buf.at[m, here], send_sems.at[m, k], recv_sems.at[m, t],
+                    {"tp": to},
+                ),
+            )
+            for k, to in ring.others
+        ]
+
+    def block_wait(buf, m, recv_sems, who):
+        at = ring.block(who)
+        send(buf.at[m, at], buf.at[m, at], o_sem.at[m], recv_sems.at[m, who], other).wait_recv()
+
+    def onward(buf, m, send_sems, recv_sems):
+        at = ring.block(far_end)
+        return send(
+            buf.at[m, at], buf.at[m, at], send_sems.at[m, 0], recv_sems.at[m, far_end],
+            {"tp": near_end},
+        )
+
+    def blocks_wait(buf, m, send_sems, recv_sems):
+        if line_rows:
+            @pl.when(inner)
+            def _():
+                block_wait(buf, m, recv_sems, far_end)
+                onward(buf, m, send_sems, recv_sems).start()
+
+        for _, who in ring.others:
+            unless(
+                (inner & (who == far_end)) if line_rows else False,
+                functools.partial(block_wait, buf, m, recv_sems, who),
+            )
+        if line_rows:
+            @pl.when(inner)
+            def _():
+                onward(buf, m, send_sems, recv_sems).wait_send()
+
+    def spread_start(buf, m, send_sems, recv_sems):
+        for skip, copy in spread(buf, m, send_sems, recv_sems):
+            unless(skip, copy.start)
+
+    def spread_wait(buf, m, send_sems, recv_sems):
+        blocks_wait(buf, m, send_sems, recv_sems)
+        for skip, copy in spread(buf, m, send_sems, recv_sems):
+            unless(skip, copy.wait_send)
+
+    last = micro - 1
+
+    def cast(src, buf, send_sems, recv_sems):
+        here = ring.block(t)
+        return [
+            (
+                is_far(t, to, line_rows),
+                send(
+                    src, buf.at[last, here], send_sems.at[k], recv_sems.at[last, t],
+                    {"section": 1 - section, "tp": to},
+                ),
+            )
+            for k, to in [(0, t)] + ring.others
+        ]
+
+    def cast_wait(buf, send_sems, recv_sems):
+        blocks_wait(buf, last, send_sems, recv_sems)
+        block_wait(buf, last, recv_sems, t)
+
+    def cast_rows():
+        return cast(nb, xg, mf_s, ag_r)
+
+    def cast_back():
+        return cast(y_b.at[last], gr, mb_s, gg_r)
+
+    def wide_copy():
+        return send(wide.at[0:8], wide_b, wb_sem.at[0], wb_sem.at[1], other)
+
     def front(m):
         unit, _ = stats(rin[m].astype(F32))
         normed = unit * wide[0:1, :] + wide[1:2, :]
         xg[m, ring.block(ring.me)] = normed.astype(BF16)
-        for copy in ring.gather(xg, m, (ag_s, ag_r)):
-            copy.start()
+        spread_start(xg, m, ag_s, ag_r)
 
     def front_back(m):
         gr[m, ring.block(ring.me)] = dyr[m]
-        for copy in ring.gather(gr, m, (gg_s, gg_r)):
-            copy.start()
+        spread_start(gr, m, gg_s, gg_r)
 
     def mirror_copy(which, m):
         buf = (xg, gr)[which]
@@ -956,6 +1060,71 @@
         for copy in c_pair(which, m, who):
             copy.start()
 
+    def sum_set(buf, got, via, sems, m, at):
+        send_sems, recv_sems, via_s, via_r = sems
+        found = []
+        for k, to in ring.others:
+            held = (inner & (to == far_end)) if line else False
+            copy = send(
+                buf.at[m, ring.block(to), at], got.at[m, k - 1, :, at],
+                send_sems.at[m, k], recv_sems.at[m, k], {"tp": to},
+            )
+            found.append((k, is_far(t, to), held, copy))
+        detour = send(
+            buf.at[m, ring.block(nt - 1 - t), at], via.at[m, :, at],
+            via_s.at[m], via_r.at[m], {"tp": jnp.where(t == 0, 1, 2)},
+        )
+        return found, detour
+
+    everything = slice(None)
+
+    def sum_tile(buf, got, via, sems, m, at, eager):
+        found, detour = sum_set(buf, got, via, sems, m, at)
+        if line:
+            pl.when(jnp.logical_not(inner))(detour.start)
+        for _, far, held, copy in found:
+            skip = (far | held) if line else False
+            if line and not eager:
+                skip = skip | jnp.logical_not(inner)
+            unless(skip, copy.start)
+
+    def sum_after(buf, got, via, sems, m, eager):
+        if not line:
+            return
+        found, detour = sum_set(buf, got, via, sems, m, everything)
+
+        @pl.when(inner)
+        def _():
+            detour.wait_recv()
+            at = ring.block(far_end)
+            buf[m, at] = (buf[m, at].astype(F32) + via[m].astype(F32)).astype(BF16)
+            for _, _, held, copy in found:
+                pl.when(held)(copy.start)
+
+        if not eager:
+            @pl.when(jnp.logical_not(inner))
+            def _():
+                for _, far, _, copy in found:
+                    unless(far, copy.start)
+
+    def sum_wait(buf, got, via, sems, m):
+        found, detour = sum_set(buf, got, via, sems, m, everything)
+        for k, far, _, copy in found:
+            unless(far, copy.wait_send)
+            unless(is_far(lax.rem(t - k + nt, nt), t), copy.wait_recv)
+        if line:
+            pl.when(jnp.logical_not(inner))(detour.wait_send)
+        total = buf[m, ring.block(t)].astype(F32)
+        for k, _ in ring.others:
+            part = got[m, k - 1].astype(F32)
+            if line:
+                part = jnp.where(is_far(lax.rem(t - k + nt, nt), t), 0.0, part)
+            total = total + part
+        return total
+
+    out_set = (out_bf, out_got, out_via, (rs_s, rs_r, rv_s, rv_r))
+    in_set = (in_bf, in_got, in_via, (rb_s, rb_r, bv_s, bv_r))
+
     def attention_masks(q):
         low = low_half(length)
         lane = lax.broadcasted_iota(jnp.int32, (length, LANES), 1)
@@ -970,8 +1139,15 @@
 
         @pl.when(who == 0)
         def _():
-            for copy in ring.gather(xg, m, (ag_s, ag_r)):
-                copy.wait()
+            @pl.when(first | (m < last))
+            def _():
+                spread_wait(xg, m, ag_s, ag_r)
+
+            @pl.when(second & (m == last))
+            def _():
+                hop_out(last).wait_recv()
+                cast_wait(xg, ag_s, ag_r)
+
             c_start(0, m, 0)
 
             @pl.when(second)
@@ -997,21 +1173,21 @@
         low, lane, tables, allowed = attention_masks(q)
         for part in range(3):
             def qkv_tile(n, part=part):
-                at = cols(n)
+                at = cols(n, WIDE)
                 acc = jnp.dot(xg[q], wq[part, :, at], preferred_element_type=F32)
                 acc = acc + wide[3 + part:4 + part, pl.ds(
-                    pl.multiple_of(t * own + n * TILE, TILE), TILE)]
+                    pl.multiple_of(t * own + n * WIDE, WIDE), WIDE)]
                 if part < 2:
                     acc = jnp.concatenate(
                         [
                             twist(acc[:, c:c + LANES], tables, 1.0)
-                            for c in range(0, TILE, LANES)
+                            for c in range(0, WIDE, LANES)
                         ],
                         axis=1,
                     )
                 qkv[q, part, :, at] = acc.astype(BF16)
 
-            loop(own // TILE, qkv_tile)
+            loop(own // WIDE, qkv_tile)
 
         def pair(p):
             at = cols(p, LANES)
@@ -1038,6 +1214,7 @@
         def _():
             output_finish(0)
             relay(3, 0)
+            relay(3, 1)
 
         @pl.when(k == 0)
         def _():
@@ -1053,7 +1230,7 @@
             w_ready(1, 3)
 
         def up_tile(n):
-            at = cols(n)
+            at = cols(n, WIDE)
             u = jnp.dot(xg[q], w1[:, at], preferred_element_type=F32) + fb[0:1, at]
             c = 0.7978845608028654
             square = u * u
@@ -1063,43 +1240,69 @@
             slope = slope + 0.5 * u * (1.0 - th * th) * (c * (1.0 + 3 * 0.044715 * square))
             gp[q, :, at] = slope.astype(BF16)
 
-        loop(hidden // TILE, up_tile)
+        loop(hidden // WIDE, up_tile)
         x_start(0, m, who)
 
-    def output_stage(m, fresh):
-        for mask in out_order:
-            @pl.when(fresh)
-            def _(mask=mask):
-                w_ready(2, mask)
-                w_ready(3, mask)
-
-            def out_tile(n, mask=mask):
-                start = pl.multiple_of(fblock[mask] * depth + n * TILE, TILE)
-                at = pl.ds(start, TILE)
+    def differ(a, b):
+        return a + b - 2 * a * b
+
+    def output_stage(m, lo, hi, fresh, now):
+        def block(j):
+            if fresh is not None:
+                for mask in masks_of(nf):
+                    @pl.when(fresh & (j == mask))
+                    def _(mask=mask):
+                        w_ready(2, mask)
+                        w_ready(3, mask)
+                        if mask == 2:
+                            pl.semaphore_signal(
+                                go_sem, inc=1, device_id=other, device_id_type=MESH
+                            )
+
+            owner = 2 * differ(f // 2, j // 2) + differ(lax.rem(f, 2), lax.rem(j, 2))
+
+            def out_tile(n):
+                at = pl.ds(pl.multiple_of(owner * depth + n * WIDE, WIDE), WIDE)
                 acc = lax.dot_general(att[m], wo[at, :], COLS, preferred_element_type=F32)
                 acc = acc + lax.dot_general(act[m], w2[at, :], COLS, preferred_element_type=F32)
                 out_bf[m, :, at] = acc.astype(BF16)
-                for copy in ring.scatter(out_bf, out_got, m, (rs_s, rs_r), at):
-                    copy.start()
-
-            loop(depth // TILE, out_tile)
-
-        @pl.when(fresh)
-        def _():
-            pl.semaphore_signal(go_sem, inc=1, device_id=other, device_id_type=MESH)
+                if now is True:
+                    sum_tile(*out_set, m, at, True)
+                else:
+                    pl.when(now)(lambda: sum_tile(*out_set, m, at, True))
+
+            loop(depth // WIDE, out_tile)
+
+        def step(j, carry):
+            block(j)
+            return carry
+
+        lax.fori_loop(lo, hi, step, 0)
+
+    def output_rest(m):
+        half = width // 2
+        start = pl.multiple_of((1 - f // 2) * half, half)
+        sum_tile(*out_set, m, pl.ds(start, half), True)
 
     def store_ends(m):
         return pltpu.make_async_copy(y_f.at[m], ends_o.at[m], o_sem.at[m])
 
     def output_finish(m):
-        for copy in ring.scatter(out_bf, out_got, m, (rs_s, rs_r)):
-            copy.wait()
-        y = rin[m].astype(F32) + ring.total(out_bf, out_got, m) + wide[2:3, :]
+        total = sum_wait(*out_set, m)
+        y = rin[m].astype(F32) + total + wide[2:3, :]
 
         @pl.when(first)
         def _():
             y_b[m] = y.astype(BF16)
             hop_out(m).start()
+
+        @pl.when(first & (m == last))
+        def _():
+            wide_copy().wait_recv()
+            unit, _ = stats(y_b[m].astype(F32))
+            nb[...] = (unit * wide_b[0:1, :] + wide_b[1:2, :]).astype(BF16)
+            for skip, copy in cast_rows():
+                unless(skip, copy.start)
 
         @pl.when(second)
         def _():
@@ -1112,8 +1315,15 @@
 
         @pl.when(first & (who == 0))
         def _():
-            for copy in ring.gather(gr, m, (gg_s, gg_r)):
-                copy.wait()
+            @pl.when(m < last)
+            def _():
+                spread_wait(gr, m, gg_s, gg_r)
+
+            @pl.when(m == last)
+            def _():
+                cast_wait(gr, gg_s, gg_r)
+                dyr[m] = gr[m, ring.block(t)]
+
             mirror_copy(1, m).start()
             c_start(1, m, 0)
 
@@ -1128,10 +1338,10 @@
                 x_sent(3, 0, 1)
 
         def att_tile(n):
-            at = cols(n)
+            at = cols(n, WIDE)
             gatt[:, at] = jnp.dot(gr[q], wo[:, at], preferred_element_type=F32).astype(BF16)
 
-        loop(own // TILE, att_tile)
+        loop(own // WIDE, att_tile)
         low, lane, tables, allowed = attention_masks(q)
 
         def pair(p):
@@ -1176,48 +1386,38 @@
         def _():
             w_ready(3, 0)
             w_ready(3, 1)
+            output_stage(0, 0, 2, None, True)
             via_ready(3)
 
         def up_tile(n):
-            at = cols(n)
+            at = cols(n, WIDE)
             acc = jnp.dot(gr[q], w2[:, at], preferred_element_type=F32)
             rounded = (acc * gp[q, :, at].astype(F32)).astype(BF16)
             up[place, :, at] = rounded
             sums = jnp.sum(rounded.astype(F32), axis=0, keepdims=True)
             up_sums[0:1, at] += jnp.where(who == 0, sums, 0.0)
 
-        loop(hidden // TILE, up_tile)
+        loop(hidden // WIDE, up_tile)
         x_start(2, m, who)
 
-        @pl.when(second & (k == 3))
-        def _():
-            backward_finish(0)
-
-        @pl.when(first & (k == 4))
-        def _():
-            hop_back(1).wait_recv()
-            front_back(1)
-
         def norm_tile(n):
-            at = cols(n)
+            at = cols(n, WIDE)
             acc = lax.dot_general(up[m], w1[at, :], COLS, preferred_element_type=F32)
             for part in range(3):
                 acc = acc + lax.dot_general(
                     dj[m, part], wq[part, at, :], COLS, preferred_element_type=F32
                 )
             in_bf[m, :, at] = acc.astype(BF16)
-            for copy in ring.scatter(in_bf, in_got, m, (rb_s, rb_r), at):
-                copy.start()
+            sum_tile(*in_set, m, at, False)
 
         @pl.when(who == 0)
         def _():
-            loop(width // TILE, norm_tile)
+            loop(width // WIDE, norm_tile)
+            sum_after(*in_set, m, False)
 
 
     def backward_finish(m):
-        for copy in ring.scatter(in_bf, in_got, m, (rb_s, rb_r)):
-            copy.wait()
-        grad_norm = ring.total(in_bf, in_got, m)
+        grad_norm = sum_wait(*in_set, m)
         unit, inv_root = stats(rin[m].astype(F32))
         scaled = grad_norm * wide[0:1, :]
         upstream = dyr[m].astype(F32)
@@ -1230,7 +1430,15 @@
         @pl.when(second)
         def _():
             y_b[m] = dx.astype(BF16)
+
+        @pl.when(second & (m < last))
+        def _():
             hop_back(m).start()
+
+        @pl.when(second & (m == last))
+        def _():
+            for skip, copy in cast_back():
+                unless(skip, copy.start)
 
         @pl.when(first)
         def _():
@@ -1264,6 +1472,7 @@
         w_far(0)
         w_far(1)
         small_arrive()
+        wide_copy().start()
         seg_copy.wait()
         loop(2 * micro, rope_of)
         for mask in order:
@@ -1272,32 +1481,31 @@
         for p in range(PIECES):
             leg_two(1, p).wait_send()
         pl.semaphore_wait(go_sem, 1)
-        for p in range(PIECES):
+        for p in range(PIECES - DIRECT):
             leg_one(3, p).start()
 
         def dy_in(m):
-            for copy in ring.gather(gr, m, (gg_s, gg_r)):
-                copy.wait()
+            spread_wait(gr, m, gg_s, gg_r)
             c_start(1, m, 0)
 
         loop(micro, dy_in)
+
 
     def slot(k):
         is_f = jnp.where(first, k < 4, (k < 8) & (lax.rem(k, 2) == 0))
-        is_o = jnp.where(first, k < 2, (k == 5) | (k == 6))
+        is_o = jnp.where(first, k < 2, (k == 1) | (k == 6))
         who = jnp.where(first, (k // 2) % 2 * (k < 4) + lax.rem(k, 2) * (k >= 4), k // 4)
         m = jnp.where(first, jnp.where(k < 4, lax.rem(k, 2), (k - 4) // 2), lax.rem(k // 2, 2))
-        m_o = jnp.where(first, m, k - 5)
+        m_o = jnp.where(first, m, k // 6)
         fresh = first & (k == 0)
 
-        @pl.when(second & ((k == 0) | (k == 1)))
-        def _():
-            hop_out(k).wait_recv()
-            front(k)
-
         @pl.when(second & (k == 0))
         def _():
+            hop_out(0).wait_recv()
+            front(0)
             w_ready(1, 2)
+            for p in range(PIECES - DIRECT, PIECES):
+                straight(p).start()
 
         @pl.when(second & (k == 1))
         def _():
@@ -1306,10 +1514,8 @@
             for mask in order:
                 w_ready(2, mask)
 
-        @pl.when(first & (k == 4))
-        def _():
-            for p in range(PIECES):
-                leg_two(3, p).wait_send()
+        @pl.when(first & (k == 3))
+        def _():
             hop_back(0).wait_recv()
             front_back(0)
 
@@ -1317,22 +1523,45 @@
         def _():
             forward_stage(m, who, k, fresh)
 
+        @pl.when(jnp.logical_not(is_f))
+        def _():
+            backward_stage(m, who, k)
+
+        @pl.when(second & (k == 6))
+        def _():
+            for skip, copy in cast_back():
+                unless(skip, copy.wait_send)
+
         @pl.when(is_o)
         def _():
-            output_stage(m_o, fresh)
-
-        @pl.when(jnp.logical_not(is_f))
-        def _():
-            backward_stage(m, who, k)
+            held_back = second & (k == 1)
+            output_stage(
+                m_o, jnp.where(held_back, 2, 0), nf, fresh, jnp.logical_not(held_back)
+            )
+
+        @pl.when(first & (k < 2))
+        def _():
+            sum_after(*out_set, m, True)
+
+        @pl.when(second & (k == 6))
+        def _():
+            sum_after(*out_set, 1, True)
+
+        @pl.when(second & (k == 2))
+        def _():
+            backward_finish(0)
+            output_rest(0)
+            sum_after(*out_set, 0, True)
 
         @pl.when(first & (k == 1))
         def _():
-            relay(3, 1)
-            relay(3, 2)
-            output_finish(1)
-            relay(3, 3)
+            for p in range(2, PIECES - DIRECT):
+                relay(3, p)
             for i in range(micro):
                 mirror_copy(0, i).start()
+            for p in range(PIECES - DIRECT):
+                leg_two(3, p).wait_send()
+            output_finish(1)
 
         @pl.when(first & (k == 7))
         def _():
@@ -1364,13 +1593,16 @@
 
     @pl.when(second)
     def _():
-        for m in range(micro):
+        for m in range(last):
             hop_back(m).wait_send()
+        wide_copy().wait_send()
 
     @pl.when(first)
     def _():
         for m in range(micro):
             hop_out(m).wait_send()
+        for skip, copy in cast_rows():
+            unless(skip, copy.wait_send)
 
     total = s_src[me]
     for k, copy in enumerate(small):
@@ -1400,7 +1632,10 @@
                     w_send(a, 0, 1, 2).wait_send()
                     w_send(a, 2, 0, 1).wait_send()
             for p in range(PIECES):
-                leg_one(via, p).wait_send()
+                if via == 3 and p >= PIECES - DIRECT:
+                    straight(p).wait_send()
+                else:
+                    leg_one(via, p).wait_send()
                 passed_on(via, 2, p).wait_send()
 
 
@@ -1455,6 +1690,9 @@
         dma((3, micro)), dma((3, micro)), dma((micro,)),
         dma((PIECES,)), dma((PIECES,)), dma((PIECES,)), dma((PIECES,)),
         dma((PIECES,)), dma((PIECES,)), pltpu.SemaphoreType.REGULAR,
+        vm((per, width), BF16), vm((8, width), F32), dma((nt,)), dma((nt,)), dma((2,)),
+        vm(ends.shape, BF16), vm(ends.shape, BF16),
+        dma((micro,)), dma((micro,)), dma((micro,)), dma((micro,)),
     ]
     return pl.pallas_call(
         functools.partial(fused_kernel, nf, nt),
@@ -1586,7 +1824,10 @@
     grad_fc2 = product(gc, act_x)
     grad_out = product(gc, att_x)
     grad_fc1 = product(xc, up_x)
-    grad_qkv = jnp.stack([product(xc, dj_x[part]) for part in range(3)], axis=1)
+    left, right = xc.reshape(-1, xc.shape[-1]), dj_x.reshape(3, -1, dj_x.shape[-1])
+    grad_qkv = lax.dot_general(
+        left, right, (((0,), (1,)), ((), ())), preferred_element_type=F32
+    )
     row_grad = sums[2:3]
     return (
         ends_out[None],

time: 356 us -> 331 us (0.930)
  Pallas kernels: 322 us -> 298 us
    pallas_call x1, Pallas kernels: 322 us -> 298 us  [fused(): pl.pallas_call(functools.partial(fused_kernel, nf, nt), out_shape=out_sha...]
    dot_general x0 -> x1, matrix products: none -> 5.12 us  [fused_shards(): lax.dot_general(left, right, (((0,), (1,)), ((), ())), preferred_element_...]
    dot_general x6 -> x3, matrix products: 24.5 us -> 21.5 us  [product(): return lax.dot_general(left, right, ROWS, preferred_element_type=F32)]
where the time goes in v5:
time: 331 us
  Pallas kernels  298 us (90%)
  matrix products  26.7 us (8%)
  local copies, waits for them, and re-layouts  5.33 us (2%)
    pallas_call x1, Pallas kernels, fused(): pl.pallas_call(functools.partial(fused_kernel, nf, nt), out_shape=out_sha...  298 us
    dot_general x3, matrix products, product(): return lax.dot_general(left, right, ROWS, preferred_element_type=F32)  21.5 us

profile of v5, /device:TPU:0, one launch (start us, length us, event | category | flops | bytes accessed | tf_op | source)
XLA Modules:
  0.0 331.1 jit_solution(6819935867923475517)
XLA Ops:
  0.6 298.4 %fused.1 = (f32[2,64,2048]{2,1,0:T(8,128)}, f32[16,128]{1,0:T(8,128)}, bf16[2,4,256,2048]{3,2,1,0:T(8,128)(2,1)}, bf16[2,4,256,512]{3,2,1,0:T(8,128)(2,1)}, bf16...) custom-call(bf16[2,64,2048]{2,1,0:T(8,128)(2,1)} %bitcast.60, ...), custom_call_target="tpu_custom_call" | custom-call | tf_op jit(solution)/shard_map/fused/pallas_call | solution.py:1697
  299.1 1.3 fusion.5
  300.4 0.0 copy-start.2
  300.4 0.7 slice_bitcast_fusion
  301.1 1.3 slice.19
  302.3 0.6 copy.27
  302.9 0.0 slice-start
  302.9 4.6 %convolution_bitcast_fusion.2 = f32[1,512,512]{2,1,0:T(8,128)} fusion(bf16[2,4,256,512]{3,2,1,0:T(8,128)(2,1)} %get-tuple-element.23, bf16[2,4,256,512]{3,2,1,0:T(8,128)(2,1)} %get-tuple-element.24), kind=kOutput, calls=%fused_computation.5 | convolution fusion | flops 1073741824 | bytes 5242880 | tf_op jit(solution)/shard_map/dot_general | solution.py:1822
  307.5 0.0 slice-start.1
  307.5 0.0 copy-start
  307.5 0.0 slice-start.2
  307.5 10.7 %convolution_bitcast_fusion = f32[1,512,2048]{2,1,0:T(8,128)} fusion(bf16[2,4,256,512]{3,2,1,0:T(8,128)(2,1)} %get-tuple-element.23, bf16[2,4,256,2048]{3,2,1,0:T(8,128)(2,1)} %get-tuple-element.26), kind=kOutput, calls=%fused_computation | convolution fusion | flops 4294967296 | bytes 14680064 | tf_op jit(solution)/shard_map/dot_general | solution.py:1822
  318.3 0.0 slice-done
  318.3 0.0 slice-done.1
  318.3 0.0 copy-done
  318.3 0.0 slice-start.3
  318.3 5.1 %fusion.2 = f32[1,512,3,512]{3,1,2,0:T(8,128)} fusion(bf16[3,2,4,256,512]{4,3,2,1,0:T(8,128)(2,1)S(1)} %bitcast.55, bf16[2,4,256,512]{3,2,1,0:T(8,128)(2,1)S(1)} %copy-done), kind=kOutput, calls=%fused_computation.4 | convolution fusion | flops 3221225472 | bytes 11534336 | tf_op jit(solution)/shard_map/dot_general | solution.py:1828
  323.4 0.0 slice-done.2
  323.4 0.0 slice-done.3
  323.4 0.0 copy-start.1
  323.4 6.2 %convolution_bitcast_fusion.1 = f32[1,512,2048]{2,1,0:T(8,128)} fusion(bf16[2,4,256,512]{3,2,1,0:T(8,128)(2,1)S(1)} %copy-done, bf16[2,4,256,2048]{3,2,1,0:T(8,128)(2,1)S(1)} %bitcast.65), kind=kOutput, calls=%fused_computation.1 | convolution fusion | flops 4294967296 | bytes 14680064 | tf_op jit(solution)/shard_map/dot_general | solution.py:1822
  329.6 0.0 copy-done.2
  329.6 0.5 copy.41
  330.1 0.0 copy-done.1
  330.1 1.0 copy.42
  (2 shorter events, 0.0 us)
Async XLA Ops:
  300.4 29.2 %copy-start.2 = (f32[1,128]{1,0:T(1,128)}, f32[1,128]{1,0:T(1,128)S(1)}, u32[]{:S(2)}) copy-start(f32[1,128]{1,0:T(1,128)S(1)} %get-tuple-element.82) | copy-start | bytes 1540
  302.9 15.4 %slice-start = ((s8[6291456]{0:T(1024)(128)(4,1)}), s8[4194304]{0:T(1024)(128)(4,1)S(1)}, s32[]{:S(2)}) async-start(s8[6291456]{0:T(1024)(128)(4,1)} %bitcast.54), calls=%async_computation | async-start | bytes 8388608
  307.5 10.7 %slice-start.1 = ((s8[6291456]{0:T(1024)(128)(4,1)}), s8[2097152]{0:T(1024)(128)(4,1)S(1)}, s32[]{:S(2)}) async-start(s8[6291456]{0:T(1024)(128)(4,1)} %bitcast.54), calls=%async_computation.1 | async-start | bytes 4194304
  307.5 10.7 %copy-start = (bf16[2,4,256,512]{3,2,1,0:T(8,128)(2,1)S(1)}, bf16[2,4,256,512]{3,2,1,0:T(8,128)(2,1)}, u32[]{:S(2)}) copy-start(bf16[2,4,256,512]{3,2,1,0:T(8,128)(2,1)} %get-tuple-element.21) | copy-start | bytes 6291460
  307.5 15.9 %slice-start.2 = ((s8[8388608]{0:T(1024)(128)(4,1)}), s8[4194304]{0:T(1024)(128)(4,1)S(1)}, s32[]{:S(2)}) async-start(s8[8388608]{0:T(1024)(128)(4,1)} %bitcast.64), calls=%async_computation.2 | async-start | bytes 8388608
  318.3 5.1 %slice-start.3 = ((s8[8388608]{0:T(1024)(128)(4,1)}), s8[4194304]{0:T(1024)(128)(4,1)S(1)}, s32[]{:S(2)}) async-start(s8[8388608]{0:T(1024)(128)(4,1)} %bitcast.64), calls=%async_computation.3 | async-start | bytes 8388608
  323.4 6.7 %copy-start.1 = (f32[2,64,2048]{2,1,0:T(8,128)S(1)}, f32[2,64,2048]{2,1,0:T(8,128)}, u32[]{:S(2)}) copy-start(f32[2,64,2048]{2,1,0:T(8,128)} %get-tuple-element.19) | copy-start | bytes 3145732

commit v6 on v5

--- a/solution.py
+++ b/solution.py
@@ -683,8 +683,7 @@
 ROWS_OF_PACK = 16
 PIECES = 8
 DIRECT = 2
-LINE_SUMS = False
-LINE_ROWS = False
+STRIPS = 4
 WIDE = 512
 
 
@@ -714,7 +713,8 @@
 def fused_kernel(
     nf, nt,
     ends_h, gain, shift, b_out, b_fc2, b_qkv, b_fc1, seg_in, wq_h, wo_h, w1_h, w2_h,
-    ends_o, sums_o, act_x, att_x, up_x, dj_x, xc_x, gc_x,
+    ends_o, sums_o, fc2_o, fc1_o, out_o, qkv_o, turned_o,
+    act_x, att_x, up_x, dj_x, xc_x, gc_x,
     wq, wo, w1, w2, pack, packs, wide, fb, segs, rope, rin, dyr, xg, qkv, lse, att, gp, act,
     gr, gatt, up, dj, out_bf, out_got, in_bf, in_got, y_f, y_b,
     own_sums, head_sums, up_sums, s_src, s_got,
@@ -722,7 +722,7 @@
     ag_s, ag_r, gg_s, gg_r, rs_s, rs_r, rb_s, rb_r, hx_s, hx_r, hb_s, hb_r,
     xl_sem, xs_s, xs_r, cl_sem, ca_s, ca_r, mx_s, mx_r, o_sem,
     l1_s, l1_r, l2_s, l2_r, fw_s, fw_r, go_sem, nb, wide_b, mf_s, mb_s, wb_sem,
-    out_via, in_via, rv_s, rv_r, bv_s, bv_r,
+    dl_sem, ds_sem,
 ):
     micro, per, width = rin.shape
     length = per * nt
@@ -900,30 +900,12 @@
     def hop_back(m):
         return send(y_b.at[m], dyr.at[m], hb_s.at[m], hb_r.at[m], other)
 
-    line = LINE_SUMS and nt == 4
-    line_rows = LINE_ROWS and nt == 4
-    inner = (t == 1) | (t == 2)
-    far_end = jnp.where(t == 1, 3, 0)
-    near_end = jnp.where(t == 1, 0, 3)
-
-    def is_far(a, b, on=line):
-        return (jnp.abs(a - b) == nt - 1) if on else False
-
-    def unless(flag, do):
-        if flag is False:
-            do()
-        else:
-            pl.when(jnp.logical_not(flag))(do)
-
     def spread(buf, m, send_sems, recv_sems):
         here = ring.block(t)
         return [
-            (
-                is_far(t, to, line_rows),
-                send(
-                    buf.at[m, here], buf.at[m, here], send_sems.at[m, k], recv_sems.at[m, t],
-                    {"tp": to},
-                ),
+            send(
+                buf.at[m, here], buf.at[m, here], send_sems.at[m, k], recv_sems.at[m, t],
+                {"tp": to},
             )
             for k, to in ring.others
         ]
@@ -932,57 +914,31 @@
         at = ring.block(who)
         send(buf.at[m, at], buf.at[m, at], o_sem.at[m], recv_sems.at[m, who], other).wait_recv()
 
-    def onward(buf, m, send_sems, recv_sems):
-        at = ring.block(far_end)
-        return send(
-            buf.at[m, at], buf.at[m, at], send_sems.at[m, 0], recv_sems.at[m, far_end],
-            {"tp": near_end},
-        )
-
-    def blocks_wait(buf, m, send_sems, recv_sems):
-        if line_rows:
-            @pl.when(inner)
-            def _():
-                block_wait(buf, m, recv_sems, far_end)
-                onward(buf, m, send_sems, recv_sems).start()
-
+    def spread_start(buf, m, send_sems, recv_sems):
+        for copy in spread(buf, m, send_sems, recv_sems):
+            copy.start()
+
+    def spread_wait(buf, m, send_sems, recv_sems):
         for _, who in ring.others:
-            unless(
-                (inner & (who == far_end)) if line_rows else False,
-                functools.partial(block_wait, buf, m, recv_sems, who),
-            )
-        if line_rows:
-            @pl.when(inner)
-            def _():
-                onward(buf, m, send_sems, recv_sems).wait_send()
-
-    def spread_start(buf, m, send_sems, recv_sems):
-        for skip, copy in spread(buf, m, send_sems, recv_sems):
-            unless(skip, copy.start)
-
-    def spread_wait(buf, m, send_sems, recv_sems):
-        blocks_wait(buf, m, send_sems, recv_sems)
-        for skip, copy in spread(buf, m, send_sems, recv_sems):
-            unless(skip, copy.wait_send)
+            block_wait(buf, m, recv_sems, who)
+        for copy in spread(buf, m, send_sems, recv_sems):
+            copy.wait_send()
 
     last = micro - 1
 
     def cast(src, buf, send_sems, recv_sems):
         here = ring.block(t)
         return [
-            (
-                is_far(t, to, line_rows),
-                send(
-                    src, buf.at[last, here], send_sems.at[k], recv_sems.at[last, t],
-                    {"section": 1 - section, "tp": to},
-                ),
+            send(
+                src, buf.at[last, here], send_sems.at[k], recv_sems.at[last, t],
+                {"section": 1 - section, "tp": to},
             )
             for k, to in [(0, t)] + ring.others
         ]
 
-    def cast_wait(buf, send_sems, recv_sems):
-        blocks_wait(buf, last, send_sems, recv_sems)
-        block_wait(buf, last, recv_sems, t)
+    def cast_wait(buf, recv_sems):
+        for who in range(nt):
+            block_wait(buf, last, recv_sems, who)
 
     def cast_rows():
         return cast(nb, xg, mf_s, ag_r)
@@ -1015,7 +971,7 @@
     def x_dst(a, m, who):
         block = x_block(who)
         if a == 3:
-            return dj_x.at[:, m, block]
+            return dj_x.at[m, :, block]
         return (act_x, att_x, up_x)[a].at[m, block]
 
     def x_src(a, m, who):
@@ -1060,70 +1016,17 @@
         for copy in c_pair(which, m, who):
             copy.start()
 
-    def sum_set(buf, got, via, sems, m, at):
-        send_sems, recv_sems, via_s, via_r = sems
-        found = []
-        for k, to in ring.others:
-            held = (inner & (to == far_end)) if line else False
-            copy = send(
-                buf.at[m, ring.block(to), at], got.at[m, k - 1, :, at],
-                send_sems.at[m, k], recv_sems.at[m, k], {"tp": to},
-            )
-            found.append((k, is_far(t, to), held, copy))
-        detour = send(
-            buf.at[m, ring.block(nt - 1 - t), at], via.at[m, :, at],
-            via_s.at[m], via_r.at[m], {"tp": jnp.where(t == 0, 1, 2)},
-        )
-        return found, detour
-
-    everything = slice(None)
-
-    def sum_tile(buf, got, via, sems, m, at, eager):
-        found, detour = sum_set(buf, got, via, sems, m, at)
-        if line:
-            pl.when(jnp.logical_not(inner))(detour.start)
-        for _, far, held, copy in found:
-            skip = (far | held) if line else False
-            if line and not eager:
-                skip = skip | jnp.logical_not(inner)
-            unless(skip, copy.start)
-
-    def sum_after(buf, got, via, sems, m, eager):
-        if not line:
-            return
-        found, detour = sum_set(buf, got, via, sems, m, everything)
-
-        @pl.when(inner)
-        def _():
-            detour.wait_recv()
-            at = ring.block(far_end)
-            buf[m, at] = (buf[m, at].astype(F32) + via[m].astype(F32)).astype(BF16)
-            for _, _, held, copy in found:
-                pl.when(held)(copy.start)
-
-        if not eager:
-            @pl.when(jnp.logical_not(inner))
-            def _():
-                for _, far, _, copy in found:
-                    unless(far, copy.start)
-
-    def sum_wait(buf, got, via, sems, m):
-        found, detour = sum_set(buf, got, via, sems, m, everything)
-        for k, far, _, copy in found:
-            unless(far, copy.wait_send)
-            unless(is_far(lax.rem(t - k + nt, nt), t), copy.wait_recv)
-        if line:
-            pl.when(jnp.logical_not(inner))(detour.wait_send)
-        total = buf[m, ring.block(t)].astype(F32)
-        for k, _ in ring.others:
-            part = got[m, k - 1].astype(F32)
-            if line:
-                part = jnp.where(is_far(lax.rem(t - k + nt, nt), t), 0.0, part)
-            total = total + part
-        return total
-
-    out_set = (out_bf, out_got, out_via, (rs_s, rs_r, rv_s, rv_r))
-    in_set = (in_bf, in_got, in_via, (rb_s, rb_r, bv_s, bv_r))
+    def sum_start(buf, got, sems, m, at):
+        for copy in ring.scatter(buf, got, m, sems, at):
+            copy.start()
+
+    def sum_wait(buf, got, sems, m):
+        for copy in ring.scatter(buf, got, m, sems):
+            copy.wait()
+        return ring.total(buf, got, m)
+
+    out_set = (out_bf, out_got, (rs_s, rs_r))
+    in_set = (in_bf, in_got, (rb_s, rb_r))
 
     def attention_masks(q):
         low = low_half(length)
@@ -1146,7 +1049,7 @@
             @pl.when(second & (m == last))
             def _():
                 hop_out(last).wait_recv()
-                cast_wait(xg, ag_s, ag_r)
+                cast_wait(xg, ag_r)
 
             c_start(0, m, 0)
 
@@ -1267,9 +1170,9 @@
                 acc = acc + lax.dot_general(act[m], w2[at, :], COLS, preferred_element_type=F32)
                 out_bf[m, :, at] = acc.astype(BF16)
                 if now is True:
-                    sum_tile(*out_set, m, at, True)
+                    sum_start(*out_set, m, at)
                 else:
-                    pl.when(now)(lambda: sum_tile(*out_set, m, at, True))
+                    pl.when(now)(lambda: sum_start(*out_set, m, at))
 
             loop(depth // WIDE, out_tile)
 
@@ -1282,7 +1185,7 @@
     def output_rest(m):
         half = width // 2
         start = pl.multiple_of((1 - f // 2) * half, half)
-        sum_tile(*out_set, m, pl.ds(start, half), True)
+        sum_start(*out_set, m, pl.ds(start, half))
 
     def store_ends(m):
         return pltpu.make_async_copy(y_f.at[m], ends_o.at[m], o_sem.at[m])
@@ -1301,8 +1204,8 @@
             wide_copy().wait_recv()
             unit, _ = stats(y_b[m].astype(F32))
             nb[...] = (unit * wide_b[0:1, :] + wide_b[1:2, :]).astype(BF16)
-            for skip, copy in cast_rows():
-                unless(skip, copy.start)
+            for copy in cast_rows():
+                copy.start()
 
         @pl.when(second)
         def _():
@@ -1321,7 +1224,7 @@
 
             @pl.when(m == last)
             def _():
-                cast_wait(gr, gg_s, gg_r)
+                cast_wait(gr, gg_r)
                 dyr[m] = gr[m, ring.block(t)]
 
             mirror_copy(1, m).start()
@@ -1332,7 +1235,7 @@
             mirror_copy(1, m).wait_recv()
             c_start(1, m, 1)
 
-            @pl.when(m == 1)
+            @pl.when(second & (m == 1))
             def _():
                 x_sent(2, 0, 1)
                 x_sent(3, 0, 1)
@@ -1408,12 +1311,11 @@
                     dj[m, part], wq[part, at, :], COLS, preferred_element_type=F32
                 )
             in_bf[m, :, at] = acc.astype(BF16)
-            sum_tile(*in_set, m, at, False)
+            sum_start(*in_set, m, at)
 
         @pl.when(who == 0)
         def _():
             loop(width // WIDE, norm_tile)
-            sum_after(*in_set, m, False)
 
 
     def backward_finish(m):
@@ -1437,8 +1339,8 @@
 
         @pl.when(second & (m == last))
         def _():
-            for skip, copy in cast_back():
-                unless(skip, copy.start)
+            for copy in cast_back():
+                copy.start()
 
         @pl.when(first)
         def _():
@@ -1447,6 +1349,134 @@
 
         for i, term in enumerate((grad_norm * unit, grad_norm, upstream)):
             own_sums[i:i + 1, :] += jnp.sum(term, axis=0, keepdims=True)
+
+    def strip(slot):
+        return xg.at[:, :, pl.ds(pl.multiple_of(slot * own, own), own)]
+
+    def strip_copy(src, slot):
+        return pltpu.make_async_copy(src, strip(slot), dl_sem.at[slot])
+
+    wide_strips = hidden // own
+    kinds = 2 * wide_strips
+
+    def strip_start(i, m):
+        slot = lax.rem(i, STRIPS)
+
+        @pl.when(i < wide_strips)
+        def _():
+            strip_copy(act_x.at[m, :, :, cols(i, own)], slot).start()
+
+        @pl.when((i >= wide_strips) & (i < kinds))
+        def _():
+            strip_copy(up_x.at[m, :, :, cols(i - wide_strips, own)], slot).start()
+
+        @pl.when(i == kinds)
+        def _():
+            strip_copy(att_x.at[m], slot).start()
+
+        @pl.when(i > kinds)
+        def _():
+            strip_copy(dj_x.at[m, i - kinds - 1], slot).start()
+
+    half = depth // 2
+
+    def result_copy(dst, h):
+        return pltpu.make_async_copy(att.at[h], dst, ds_sem.at[h])
+
+    def turn_rows(m):
+        strip_copy(xc_x.at[m], 2).start()
+        strip_copy(gc_x.at[m], 3).start()
+        for which in range(2):
+            strip_copy(xc_x.at[m], 2 + which).wait()
+            for b in range(nf):
+                for h in range(2):
+                    block = xg[b, :, pl.ds((2 + which) * own + h * half, half)]
+                    c = (h * nf + b) * length
+                    act[which, :, c:c + length] = block.T
+
+    def turned_copies():
+        span = nf * length
+        return [
+            pltpu.make_async_copy(
+                act.at[which, :, pl.ds(h * span, span)],
+                turned_o.at[which, pl.ds(h * half, half), :],
+                dl_sem.at[2 * which + h],
+            )
+            for which in range(2)
+            for h in range(2)
+        ]
+
+    def weight_stage():
+        m = 0
+        for i in range(micro):
+            for a in (0, 1):
+                x_sent(a, i, 0)
+            mirror_copy(0, i).wait_send()
+            for who in range(2):
+                mine, theirs = c_pair(0, i, who)
+                mine.wait()
+                theirs.wait()
+        for a in (2, 3):
+            x_sent(a, 0, 0)
+
+        @pl.when(first)
+        def _():
+            for a in (2, 3):
+                x_sent(a, 0, 1)
+
+        for who in range(2):
+            for a in range(4):
+                x_send(a, 0, who).wait_recv()
+            mine, theirs = c_pair(1, 0, who)
+            mine.wait()
+            theirs.wait()
+        strip_start(0, m)
+        strip_start(1, m)
+        turn_rows(m)
+        strip_start(2, m)
+        strip_start(3, m)
+
+        def step(i):
+            slot = lax.rem(i, STRIPS)
+            strip_copy(xc_x.at[m], slot).wait()
+            use_dy = (i < wide_strips) | (i == kinds)
+            right = xg[:, :, cols(slot, own)].reshape(nf * length, own)
+            which = jnp.where(use_dy, 1, 0)
+            span = nf * length
+            left = jnp.concatenate([act[which, :, :span], act[which, :, span:]], axis=0)
+            value = jnp.dot(left, right, preferred_element_type=F32)
+            for h in range(2):
+                rows = pl.ds(h * half, half)
+
+                @pl.when(i > 0)
+                def _(h=h):
+                    result_copy(out_o.at[pl.ds(0, half), :], h).wait()
+
+                att[h] = value[h * half:(h + 1) * half].astype(BF16)
+
+                @pl.when(i < wide_strips)
+                def _(h=h, rows=rows):
+                    result_copy(fc2_o.at[rows, cols(i, own)], h).start()
+
+                @pl.when((i >= wide_strips) & (i < kinds))
+                def _(h=h, rows=rows):
+                    result_copy(fc1_o.at[rows, cols(i - wide_strips, own)], h).start()
+
+                @pl.when(i == kinds)
+                def _(h=h, rows=rows):
+                    result_copy(out_o.at[rows, :], h).start()
+
+                @pl.when(i > kinds)
+                def _(h=h, rows=rows):
+                    result_copy(qkv_o.at[i - kinds - 1, rows, :], h).start()
+
+            @pl.when(i + STRIPS < kinds + 4)
+            def _():
+                strip_start(i + STRIPS, m)
+
+        loop(kinds + 4, step)
+        for h in range(2):
+            result_copy(out_o.at[pl.ds(0, half), :], h).wait()
 
     own_sums[...] = jnp.zeros_like(own_sums)
     head_sums[...] = jnp.zeros_like(head_sums)
@@ -1491,6 +1521,22 @@
         loop(micro, dy_in)
 
 
+    small = [
+        send(s_src.at[to], s_got.at[k], sm_s.at[k], sm_r.at[k], peer) for k, to, peer in group
+    ]
+
+    def small_start():
+        s_src[...] = jnp.zeros_like(s_src)
+        for j in range(count):
+            s_src[j, 0:3, :] = own_sums[0:3, j * LANES:(j + 1) * LANES]
+        for j in range(nf):
+            s_src[t * nf + j, 3:6, :] = head_sums[0:3, j * LANES:(j + 1) * LANES]
+            for r in range(per_row):
+                c = (j * per_row + r) * LANES
+                s_src[t * nf + j, 6 + r:7 + r, :] = up_sums[0:1, c:c + LANES]
+        for copy in small:
+            copy.start()
+
     def slot(k):
         is_f = jnp.where(first, k < 4, (k < 8) & (lax.rem(k, 2) == 0))
         is_o = jnp.where(first, k < 2, (k == 1) | (k == 6))
@@ -1529,8 +1575,8 @@
 
         @pl.when(second & (k == 6))
         def _():
-            for skip, copy in cast_back():
-                unless(skip, copy.wait_send)
+            for copy in cast_back():
+                copy.wait_send()
 
         @pl.when(is_o)
         def _():
@@ -1539,19 +1585,11 @@
                 m_o, jnp.where(held_back, 2, 0), nf, fresh, jnp.logical_not(held_back)
             )
 
-        @pl.when(first & (k < 2))
-        def _():
-            sum_after(*out_set, m, True)
-
-        @pl.when(second & (k == 6))
-        def _():
-            sum_after(*out_set, 1, True)
 
         @pl.when(second & (k == 2))
         def _():
             backward_finish(0)
             output_rest(0)
-            sum_after(*out_set, 0, True)
 
         @pl.when(first & (k == 1))
         def _():
@@ -1563,13 +1601,32 @@
                 leg_two(3, p).wait_send()
             output_finish(1)
 
+        @pl.when(second & (k == 4))
+        def _():
+            backward_finish(1)
+
+        @pl.when(second & (k == 7))
+        def _():
+            small_start()
+
+        @pl.when((first & (k == 6)) | (second & (k == 7)))
+        def _():
+            weight_stage()
+
+        @pl.when(k == 7)
+        def _():
+            for who in range(2):
+                mine, theirs = c_pair(1, last, who)
+                mine.wait()
+                theirs.wait()
+            turn_rows(last)
+            for copy in turned_copies():
+                copy.start()
+
         @pl.when(first & (k == 7))
         def _():
-            backward_finish(0)
-
-        @pl.when((first & (k == 7)) | (second & (k == 4)))
-        def _():
-            backward_finish(1)
+            loop(micro, backward_finish)
+            small_start()
 
         @pl.when(second & (k == 7))
         def _():
@@ -1577,19 +1634,13 @@
 
     loop(8, slot)
 
-    s_src[...] = jnp.zeros_like(s_src)
-    for j in range(count):
-        s_src[j, 0:3, :] = own_sums[0:3, j * LANES:(j + 1) * LANES]
-    for j in range(nf):
-        s_src[t * nf + j, 3:6, :] = head_sums[0:3, j * LANES:(j + 1) * LANES]
-        for r in range(per_row):
-            c = (j * per_row + r) * LANES
-            s_src[t * nf + j, 6 + r:7 + r, :] = up_sums[0:1, c:c + LANES]
-    small = [
-        send(s_src.at[to], s_got.at[k], sm_s.at[k], sm_r.at[k], peer) for k, to, peer in group
-    ]
-    for copy in small:
-        copy.start()
+    for a in (2, 3):
+        x_sent(a, last, 0)
+    for who in range(2):
+        for a in range(4):
+            if who == 1:
+                x_sent(a, last, 1)
+            x_send(a, last, who).wait_recv()
 
     @pl.when(second)
     def _():
@@ -1601,26 +1652,19 @@
     def _():
         for m in range(micro):
             hop_out(m).wait_send()
-        for skip, copy in cast_rows():
-            unless(skip, copy.wait_send)
+        for copy in cast_rows():
+            copy.wait_send()
 
     total = s_src[me]
     for k, copy in enumerate(small):
         copy.wait()
         total = total + s_got[k + 1]
     sums_o[...] = total
+    for copy in turned_copies():
+        copy.wait()
     for m in range(micro):
-        for who in range(2):
-            for a in range(4):
-                if (m, who) != (0, 1):
-                    x_sent(a, m, who)
-                x_send(a, m, who).wait_recv()
-            for which in range(2):
-                mine, theirs = c_pair(which, m, who)
-                mine.wait()
-                theirs.wait()
-        for which in range(2):
-            mirror_copy(which, m).wait_send()
+        mirror_copy(1, m).wait_send()
+    for m in range(micro):
         store_ends(m).wait()
     for a in range(4):
         w_send(a, 0, 0, 1).wait_send()
@@ -1656,10 +1700,15 @@
     out_shape = [
         jax.ShapeDtypeStruct(ends.shape, F32),
         jax.ShapeDtypeStruct(piece, F32),
+        jax.ShapeDtypeStruct((depth, hidden), BF16),
+        jax.ShapeDtypeStruct((depth, hidden), BF16),
+        jax.ShapeDtypeStruct((depth, own), BF16),
+        jax.ShapeDtypeStruct((3, depth, own), BF16),
+        jax.ShapeDtypeStruct((2, depth, nf * length), BF16),
         jax.ShapeDtypeStruct((micro, nf, length, hidden), BF16),
         jax.ShapeDtypeStruct((micro, nf, length, own), BF16),
         jax.ShapeDtypeStruct((micro, nf, length, hidden), BF16),
-        jax.ShapeDtypeStruct((3, micro, nf, length, own), BF16),
+        jax.ShapeDtypeStruct((micro, 3, nf, length, own), BF16),
         jax.ShapeDtypeStruct((micro, nf, length, depth), BF16),
         jax.ShapeDtypeStruct((micro, nf, length, depth), BF16),
     ]
@@ -1691,14 +1740,13 @@
         dma((PIECES,)), dma((PIECES,)), dma((PIECES,)), dma((PIECES,)),
         dma((PIECES,)), dma((PIECES,)), pltpu.SemaphoreType.REGULAR,
         vm((per, width), BF16), vm((8, width), F32), dma((nt,)), dma((nt,)), dma((2,)),
-        vm(ends.shape, BF16), vm(ends.shape, BF16),
-        dma((micro,)), dma((micro,)), dma((micro,)), dma((micro,)),
+        dma((STRIPS,)), dma((2,)),
     ]
     return pl.pallas_call(
         functools.partial(fused_kernel, nf, nt),
         out_shape=out_shape,
         in_specs=[anywhere] + [inside] * 7 + [anywhere] * 4,
-        out_specs=[anywhere, inside] + [anywhere] * 6,
+        out_specs=[anywhere, inside] + [anywhere] * 11,
         scratch_shapes=scratch,
         compiler_params=pltpu.CompilerParams(
             collective_id=4, has_side_effects=True, vmem_limit_bytes=VMEM_LIMIT
@@ -1804,43 +1852,131 @@
     )
 
 
+def last_kernel(
+    used, last,
+    ends, sums, turned, fc2, fc1, out, qkv, act, up, att, dj,
+    ends_o, gain_o, shift_o, row_o, row_b, qkv_b, fc1_b, fc2_o, fc1_o, out_o, qkv_o,
+    ends_v, turned_v, early_v, right_v, done_v, e_sem, t_sem, p_sem, r_sem, d_sem,
+):
+    strips, _, own = early_v.shape
+    wide = (strips - 4) // 2
+    copy = pltpu.make_async_copy
+
+    def part(ref, i):
+        return ref.at[:, pl.ds(i * own, own)]
+
+    table = []
+    for i in range(wide):
+        right = act.at[last, :, :, pl.ds(i * own, own)]
+        table.append((1, part(fc2, i), right, part(fc2_o, i)))
+    for i in range(wide):
+        right = up.at[last, :, :, pl.ds(i * own, own)]
+        table.append((0, part(fc1, i), right, part(fc1_o, i)))
+    table.append((1, out, att.at[last], out_o))
+    for i in range(3):
+        table.append((0, qkv.at[i], dj.at[last, i], qkv_o.at[i]))
+    for which in (1, 0):
+        copy(turned.at[which], turned_v.at[which], t_sem.at[which]).start()
+    loads = []
+    for i, (_, early, right, _) in enumerate(table):
+        loads.append((
+            copy(right, right_v.at[i], r_sem.at[i]), copy(early, early_v.at[i], p_sem.at[i])
+        ))
+        for one in loads[-1]:
+            one.start()
+    ends_in = copy(ends, ends_v, e_sem.at[0])
+    ends_in.start()
+    gain_o[...] = sums[0:1, :]
+    shift_o[...] = sums[1:2, :]
+    row_o[...] = sums[2:3, :]
+    row_b[...] = sums[2:3, :]
+    for r in range(3):
+        qkv_b[r] = sums[3 + r:4 + r, :]
+    for r in range(6, used):
+        fc1_b[:, (r - 6) * LANES:(r - 5) * LANES] = sums[r:r + 1, :]
+    ready = set()
+    stores = []
+    for i, (which, _, _, target) in enumerate(table):
+        if which not in ready:
+            copy(turned.at[which], turned_v.at[which], t_sem.at[which]).wait()
+            ready.add(which)
+        for one in loads[i]:
+            one.wait()
+        right = right_v[i].reshape(-1, own)
+        done_v[i] = early_v[i].astype(F32) + jnp.dot(
+            turned_v[which], right, preferred_element_type=F32
+        )
+        stores.append(copy(done_v.at[i], target, d_sem.at[i]))
+        stores[-1].start()
+        if i == 0:
+            ends_in.wait()
+            stores.append(copy(ends_v, ends_o, e_sem.at[1]))
+            stores[-1].start()
+    for one in stores:
+        one.wait()
+
+
+def last_products(used, ends, sums, turned, fc2, fc1, out, qkv, act, up, att, dj):
+    depth, hidden = fc2.shape
+    own = out.shape[1]
+    micro, nf, length = act.shape[:3]
+    strips = 2 * (hidden // own) + 4
+    anywhere = pl.BlockSpec(memory_space=pl.ANY)
+    inside = pl.BlockSpec(memory_space=pltpu.VMEM)
+    small = jax.ShapeDtypeStruct((1, LANES), F32)
+    dma = pltpu.SemaphoreType.DMA
+    return pl.pallas_call(
+        functools.partial(last_kernel, used, micro - 1),
+        out_shape=[
+            jax.ShapeDtypeStruct(ends.shape, F32), small, small, small, small,
+            jax.ShapeDtypeStruct((3, 1, LANES), F32),
+            jax.ShapeDtypeStruct((1, (used - 6) * LANES), F32),
+            jax.ShapeDtypeStruct(fc2.shape, F32), jax.ShapeDtypeStruct(fc1.shape, F32),
+            jax.ShapeDtypeStruct(out.shape, F32), jax.ShapeDtypeStruct(qkv.shape, F32),
+        ],
+        in_specs=[anywhere, inside] + [anywhere] * 9,
+        out_specs=[anywhere] + [inside] * 6 + [anywhere] * 4,
+        scratch_shapes=[
+            pltpu.VMEM(ends.shape, F32), pltpu.VMEM(turned.shape, BF16),
+            pltpu.VMEM((strips, depth, own), BF16),
+            pltpu.VMEM((strips, nf, length, own), BF16),
+            pltpu.VMEM((strips, depth, own), F32),
+            dma((2,)), dma((2,)), dma((strips,)), dma((strips,)), dma((strips,)),
+        ],
+        compiler_params=pltpu.CompilerParams(vmem_limit_bytes=VMEM_LIMIT),
+        name="last_products",
+    )(ends, sums, turned, fc2, fc1, out, qkv, act, up, att, dj)
+
+
 def fused_shards(
     ends_in, segments, ln_gain, ln_bias, w_qkv, w_out, w_fc1, w_fc2,
     bias_qkv, bias_out, bias_fc1, bias_fc2,
 ):
     nf, nt = lax.axis_size("fsdp"), lax.axis_size("tp")
     used = 6 + bias_fc1.shape[1] // LANES
-    ends_out, sums, act_x, att_x, up_x, dj_x, xc, gc = fused(
+    ends_out, sums, fc2, fc1, out, qkv, turned, act_x, att_x, up_x, dj_x, *_ = fused(
         ends_in[0],
         (ln_gain, ln_bias, bias_out, bias_fc2, bias_qkv[0], bias_fc1),
         segments, w_qkv[0].transpose(1, 0, 2), w_out[0], w_fc1[0], w_fc2[0], nf, nt,
     )
 
-    def product(left, right):
-        left = left.reshape(-1, left.shape[-1])
-        right = right.reshape(-1, right.shape[-1])
-        return lax.dot_general(left, right, ROWS, preferred_element_type=F32)
-
-    grad_fc2 = product(gc, act_x)
-    grad_out = product(gc, att_x)
-    grad_fc1 = product(xc, up_x)
-    left, right = xc.reshape(-1, xc.shape[-1]), dj_x.reshape(3, -1, dj_x.shape[-1])
-    grad_qkv = lax.dot_general(
-        left, right, (((0,), (1,)), ((), ())), preferred_element_type=F32
+    ends_out, gain, shift, row, row_again, qkv_bias, fc1_bias, fc2, fc1, out, qkv = (
+        last_products(
+            used, ends_out, sums, turned, fc2, fc1, out, qkv, act_x, up_x, att_x, dj_x
+        )
     )
-    row_grad = sums[2:3]
     return (
         ends_out[None],
-        sums[0:1],
-        sums[1:2],
-        grad_qkv[None],
-        grad_out[None],
-        grad_fc1[None],
-        grad_fc2[None],
-        sums[3:6][None],
-        row_grad,
-        sums[6:used].reshape(1, -1),
-        row_grad,
+        gain,
+        shift,
+        qkv.transpose(1, 0, 2)[None],
+        out[None],
+        fc1[None],
+        fc2[None],
+        qkv_bias.transpose(1, 0, 2),
+        row,
+        fc1_bias,
+        row_again,
     )
 
 

time: 331 us -> 321 us (0.970)
  matrix products: 26.7 us -> 0 us
  Pallas kernels: 298 us -> 320 us
  local copies, waits for them, and re-layouts: 5.33 us -> 0 us
    dot_general x4 -> x0, matrix products: 26.7 us -> none  [the longest x3 21.5 us: product(): return lax.dot_general(left, right, ROWS, preferred_element_type=F32)]
    pallas_call x0 -> x1, Pallas kernels: none -> 17.8 us  [last_products(): pl.pallas_call(functools.partial(last_kernel, used, micro - 1), out_shape...]
    pallas_call x1, Pallas kernels: 298 us -> 302 us  [fused(): pl.pallas_call(functools.partial(fused_kernel, nf, nt), out_shape=out_sha...]
where the time goes in v6:
time: 321 us
  Pallas kernels  320 us (100%)
    pallas_call x1, Pallas kernels, fused(): pl.pallas_call(functools.partial(fused_kernel, nf, nt), out_shape=out_sha...  302 us
    pallas_call x1, Pallas kernels, last_products(): pl.pallas_call(functools.partial(last_kernel, used, micro - 1), out_shape...  17.8 us

profile of v6, /device:TPU:0, one launch (start us, length us, event | category | flops | bytes accessed | tf_op | source)
XLA Modules:
  0.0 321.2 jit_solution(18303000879914442023)
XLA Ops:
  0.6 302.5 %fused.1 = (f32[2,64,2048]{2,1,0:T(8,128)}, f32[16,128]{1,0:T(8,128)}, bf16[512,2048]{1,0:T(8,128)(2,1)}, bf16[512,2048]{1,0:T(8,128)(2,1)}, bf16[512,512]{1,0:T...) custom-call(bf16[2,64,2048]{2,1,0:T(8,128)(2,1)} %bitcast.19, ...), custom_call_target="tpu_custom_call" | custom-call | tf_op jit(solution)/shard_map/fused/pallas_call | solution.py:1745
  303.2 17.8 %last_products.1 = (f32[2,64,2048]{2,1,0:T(8,128)}, f32[1,128]{1,0:T(1,128)}, f32[1,128]{1,0:T(1,128)}, f32[1,128]{1,0:T(1,128)}, f32[1,128]{1,0:T(1,128)}, /*in...) custom-call(f32[2,64,2048]{2,1,0:T(8,128)} %get-tuple-element.33.end, ...), custom_call_target="tpu_custom_call" | custom-call | tf_op jit(solution)/shard_map/last_products/pallas_call | solution.py:1928

commit v7 on v6

--- a/solution.py
+++ b/solution.py
@@ -721,7 +721,7 @@
     in_sem, wl_sem, ws_sem, wr_sem, pk_s, pk_r, sm_s, sm_r,
     ag_s, ag_r, gg_s, gg_r, rs_s, rs_r, rb_s, rb_r, hx_s, hx_r, hb_s, hb_r,
     xl_sem, xs_s, xs_r, cl_sem, ca_s, ca_r, mx_s, mx_r, o_sem,
-    l1_s, l1_r, l2_s, l2_r, fw_s, fw_r, go_sem, nb, wide_b, mf_s, mb_s, wb_sem,
+    mg_s, mg_r, l1_s, l1_r, l2_s, l2_r, fw_s, fw_r, go_sem, nb, wide_b, mf_s, mb_s, wb_sem,
     dl_sem, ds_sem,
 ):
     micro, per, width = rin.shape
@@ -957,12 +957,20 @@
 
     def front_back(m):
         gr[m, ring.block(ring.me)] = dyr[m]
+
+        @pl.when(first)
+        def _():
+            mirror_rows(m, t).start()
+
         spread_start(gr, m, gg_s, gg_r)
 
-    def mirror_copy(which, m):
-        buf = (xg, gr)[which]
+    def mirror_copy(m):
+        return send(xg.at[m], xg.at[micro + m], mx_s.at[0, m], mx_r.at[0, m], mirror)
+
+    def mirror_rows(m, who):
+        at = ring.block(who)
         return send(
-            buf.at[m], buf.at[micro + m], mx_s.at[which, m], mx_r.at[which, m], mirror
+            gr.at[m, at], gr.at[micro + m, at], mg_s.at[m, who], mg_r.at[m, who], mirror
         )
 
     def x_block(who):
@@ -1055,11 +1063,11 @@
 
             @pl.when(second)
             def _():
-                mirror_copy(0, m).start()
+                mirror_copy(m).start()
 
         @pl.when(who == 1)
         def _():
-            mirror_copy(0, m).wait_recv()
+            mirror_copy(m).wait_recv()
             c_start(0, m, 1)
 
             @pl.when(m == 1)
@@ -1220,19 +1228,25 @@
         def _():
             @pl.when(m < last)
             def _():
-                spread_wait(gr, m, gg_s, gg_r)
+                for _, who in ring.others:
+                    block_wait(gr, m, gg_r, who)
+                    mirror_rows(m, who).start()
+                for copy in spread(gr, m, gg_s, gg_r):
+                    copy.wait_send()
 
             @pl.when(m == last)
             def _():
-                cast_wait(gr, gg_r)
+                for who in range(nt):
+                    block_wait(gr, last, gg_r, who)
+                    mirror_rows(last, who).start()
                 dyr[m] = gr[m, ring.block(t)]
 
-            mirror_copy(1, m).start()
             c_start(1, m, 0)
 
         @pl.when(who == 1)
         def _():
-            mirror_copy(1, m).wait_recv()
+            for who in range(nt):
+                mirror_rows(m, who).wait_recv()
             c_start(1, m, 1)
 
             @pl.when(second & (m == 1))
@@ -1278,6 +1292,10 @@
         loop(own // LANES, pair)
         x_start(3, m, who)
 
+        @pl.when(second & (k == 3))
+        def _():
+            backward_finish(0)
+
         @pl.when(who == 0)
         def _():
             for part in range(3):
@@ -1411,7 +1429,7 @@
         for i in range(micro):
             for a in (0, 1):
                 x_sent(a, i, 0)
-            mirror_copy(0, i).wait_send()
+            mirror_copy(i).wait_send()
             for who in range(2):
                 mine, theirs = c_pair(0, i, who)
                 mine.wait()
@@ -1556,7 +1574,8 @@
         @pl.when(second & (k == 1))
         def _():
             for i in range(micro):
-                mirror_copy(1, i).start()
+                for who in range(nt):
+                    mirror_rows(i, who).start()
             for mask in order:
                 w_ready(2, mask)
 
@@ -1586,21 +1605,20 @@
             )
 
 
-        @pl.when(second & (k == 2))
-        def _():
-            backward_finish(0)
-            output_rest(0)
-
         @pl.when(first & (k == 1))
         def _():
             for p in range(2, PIECES - DIRECT):
                 relay(3, p)
             for i in range(micro):
-                mirror_copy(0, i).start()
+                mirror_copy(i).start()
             for p in range(PIECES - DIRECT):
                 leg_two(3, p).wait_send()
             output_finish(1)
 
+        @pl.when(second & (k == 2))
+        def _():
+            output_rest(0)
+
         @pl.when(second & (k == 4))
         def _():
             backward_finish(1)
@@ -1612,6 +1630,11 @@
         @pl.when((first & (k == 6)) | (second & (k == 7)))
         def _():
             weight_stage()
+
+        @pl.when(first & (k == 7))
+        def _():
+            loop(micro, backward_finish)
+            small_start()
 
         @pl.when(k == 7)
         def _():
@@ -1623,11 +1646,6 @@
             for copy in turned_copies():
                 copy.start()
 
-        @pl.when(first & (k == 7))
-        def _():
-            loop(micro, backward_finish)
-            small_start()
-
         @pl.when(second & (k == 7))
         def _():
             loop(micro, output_finish)
@@ -1655,15 +1673,9 @@
         for copy in cast_rows():
             copy.wait_send()
 
-    total = s_src[me]
-    for k, copy in enumerate(small):
-        copy.wait()
-        total = total + s_got[k + 1]
-    sums_o[...] = total
-    for copy in turned_copies():
-        copy.wait()
     for m in range(micro):
-        mirror_copy(1, m).wait_send()
+        for who in range(nt):
+            mirror_rows(m, who).wait_send()
     for m in range(micro):
         store_ends(m).wait()
     for a in range(4):
@@ -1681,6 +1693,13 @@
                 else:
                     leg_one(via, p).wait_send()
                 passed_on(via, 2, p).wait_send()
+    total = s_src[me]
+    for k, copy in enumerate(small):
+        copy.wait()
+        total = total + s_got[k + 1]
+    sums_o[...] = total
+    for copy in turned_copies():
+        copy.wait()
 
 
 def fused(ends, smalls, segments, wq, wo, w1, w2, nf, nt):
@@ -1737,6 +1756,7 @@
         dma((4, micro, 2)), dma((4, micro, 2)), dma((4, micro, 2)),
         dma((2, micro, 2)), dma((2, micro, 2)), dma((2, micro, 2)),
         dma((3, micro)), dma((3, micro)), dma((micro,)),
+        dma((micro, nt)), dma((micro, nt)),
         dma((PIECES,)), dma((PIECES,)), dma((PIECES,)), dma((PIECES,)),
         dma((PIECES,)), dma((PIECES,)), pltpu.SemaphoreType.REGULAR,
         vm((per, width), BF16), vm((8, width), F32), dma((nt,)), dma((nt,)), dma((2,)),
@@ -1852,6 +1872,9 @@
     )
 
 
+AHEAD = 3
+
+
 def last_kernel(
     used, last,
     ends, sums, turned, fc2, fc1, out, qkv, act, up, att, dj,
@@ -1875,17 +1898,18 @@
     table.append((1, out, att.at[last], out_o))
     for i in range(3):
         table.append((0, qkv.at[i], dj.at[last, i], qkv_o.at[i]))
-    for which in (1, 0):
-        copy(turned.at[which], turned_v.at[which], t_sem.at[which]).start()
-    loads = []
-    for i, (_, early, right, _) in enumerate(table):
-        loads.append((
-            copy(right, right_v.at[i], r_sem.at[i]), copy(early, early_v.at[i], p_sem.at[i])
-        ))
-        for one in loads[-1]:
+    def turned_load(which):
+        return copy(turned.at[which], turned_v.at[which], t_sem.at[which])
+
+    def loads(i):
+        _, early, right, _ = table[i]
+        return copy(right, right_v.at[i], r_sem.at[i]), copy(early, early_v.at[i], p_sem.at[i])
+
+    turned_load(table[0][0]).start()
+    for i in range(AHEAD):
+        for one in loads(i):
             one.start()
     ends_in = copy(ends, ends_v, e_sem.at[0])
-    ends_in.start()
     gain_o[...] = sums[0:1, :]
     shift_o[...] = sums[1:2, :]
     row_o[...] = sums[2:3, :]
@@ -1898,17 +1922,24 @@
     stores = []
     for i, (which, _, _, target) in enumerate(table):
         if which not in ready:
-            copy(turned.at[which], turned_v.at[which], t_sem.at[which]).wait()
+            turned_load(which).wait()
             ready.add(which)
-        for one in loads[i]:
+        for one in loads(i):
             one.wait()
+        if i + AHEAD < strips:
+            for one in loads(i + AHEAD):
+                one.start()
+        if i == 0:
+            turned_load(1 - which).start()
+        if i == 1:
+            ends_in.start()
         right = right_v[i].reshape(-1, own)
         done_v[i] = early_v[i].astype(F32) + jnp.dot(
             turned_v[which], right, preferred_element_type=F32
         )
         stores.append(copy(done_v.at[i], target, d_sem.at[i]))
         stores[-1].start()
-        if i == 0:
+        if i == strips - 3:
             ends_in.wait()
             stores.append(copy(ends_v, ends_o, e_sem.at[1]))
             stores[-1].start()

time: 321 us -> 312 us (0.972)
  Pallas kernels: 320 us -> 311 us
    pallas_call x1, Pallas kernels: 302 us -> 297 us  [fused(): pl.pallas_call(functools.partial(fused_kernel, nf, nt), out_shape=out_sha...]
where the time goes in v7:
time: 312 us
  Pallas kernels  311 us (100%)
    pallas_call x1, Pallas kernels, fused(): pl.pallas_call(functools.partial(fused_kernel, nf, nt), out_shape=out_sha...  297 us
    pallas_call x1, Pallas kernels, last_products(): pl.pallas_call(functools.partial(last_kernel, used, micro - 1), out_shape...  14.9 us

profile of v7, /device:TPU:0, one launch (start us, length us, event | category | flops | bytes accessed | tf_op | source)
XLA Modules:
  0.0 312.2 jit_solution(12184953651857413358)
XLA Ops:
  0.6 296.5 %fused.1 = (f32[2,64,2048]{2,1,0:T(8,128)}, f32[16,128]{1,0:T(8,128)}, bf16[512,2048]{1,0:T(8,128)(2,1)}, bf16[512,2048]{1,0:T(8,128)(2,1)}, bf16[512,512]{1,0:T...) custom-call(bf16[2,64,2048]{2,1,0:T(8,128)(2,1)} %bitcast.19, ...), custom_call_target="tpu_custom_call" | custom-call | tf_op jit(solution)/shard_map/fused/pallas_call | solution.py:1765
  297.2 14.9 %last_products.1 = (f32[2,64,2048]{2,1,0:T(8,128)}, f32[1,128]{1,0:T(1,128)}, f32[1,128]{1,0:T(1,128)}, f32[1,128]{1,0:T(1,128)}, f32[1,128]{1,0:T(1,128)}, /*in...) custom-call(f32[2,64,2048]{2,1,0:T(8,128)} %get-tuple-element.33.end, ...), custom_call_target="tpu_custom_call" | custom-call | tf_op jit(solution)/shard_map/last_products/pallas_call | solution.py:1959

commit v8 on v7

--- a/solution.py
+++ b/solution.py
@@ -682,6 +682,7 @@
 
 ROWS_OF_PACK = 16
 PIECES = 8
+DIRECT_FIRST = 0
 DIRECT = 2
 STRIPS = 4
 WIDE = 512
@@ -824,9 +825,9 @@
         block = piece_at(a, mask, p)
         return send(block, block, fw_s.at[p], fw_r.at[p], sibling)
 
-    def straight(p):
-        src = table[3][0].at[pl.ds(p * part_rows, part_rows), :]
-        return send(src, piece_at(3, 0, p), l1_s.at[p], l2_r.at[p], mirror)
+    def straight(a, p):
+        src = table[a][0].at[pl.ds(p * part_rows, part_rows), :]
+        return send(src, piece_at(a, 0, p), l1_s.at[p], l2_r.at[p], mirror)
 
     def relay(a, p):
         leg_one(a, p).wait_recv()
@@ -855,8 +856,10 @@
     @pl.when(first)
     def _():
         w_far(0)
+        for p in range(PIECES - DIRECT_FIRST, PIECES):
+            straight(1, p).start()
         w_far(2)
-        for p in range(PIECES):
+        for p in range(PIECES - DIRECT_FIRST):
             leg_one(1, p).start()
 
     def small_arrive():
@@ -1515,7 +1518,7 @@
 
     @pl.when(second)
     def _():
-        for p in range(PIECES):
+        for p in range(PIECES - DIRECT_FIRST):
             relay(1, p)
         w_far(0)
         w_far(1)
@@ -1526,7 +1529,7 @@
         for mask in order:
             w_ready(0, mask)
         w_far(2)
-        for p in range(PIECES):
+        for p in range(PIECES - DIRECT_FIRST):
             leg_two(1, p).wait_send()
         pl.semaphore_wait(go_sem, 1)
         for p in range(PIECES - DIRECT):
@@ -1569,7 +1572,7 @@
             front(0)
             w_ready(1, 2)
             for p in range(PIECES - DIRECT, PIECES):
-                straight(p).start()
+                straight(3, p).start()
 
         @pl.when(second & (k == 1))
         def _():
@@ -1688,8 +1691,8 @@
                     w_send(a, 0, 1, 2).wait_send()
                     w_send(a, 2, 0, 1).wait_send()
             for p in range(PIECES):
-                if via == 3 and p >= PIECES - DIRECT:
-                    straight(p).wait_send()
+                if p >= PIECES - (DIRECT if via == 3 else DIRECT_FIRST):
+                    straight(via, p).wait_send()
                 else:
                     leg_one(via, p).wait_send()
                 passed_on(via, 2, p).wait_send()
@@ -1880,6 +1883,7 @@
     ends, sums, turned, fc2, fc1, out, qkv, act, up, att, dj,
     ends_o, gain_o, shift_o, row_o, row_b, qkv_b, fc1_b, fc2_o, fc1_o, out_o, qkv_o,
     ends_v, turned_v, early_v, right_v, done_v, e_sem, t_sem, p_sem, r_sem, d_sem,
+    sums_v, row_v, qkv_v, hidden_v, s_sem,
 ):
     strips, _, own = early_v.shape
     wide = (strips - 4) // 2
@@ -1910,14 +1914,16 @@
         for one in loads(i):
             one.start()
     ends_in = copy(ends, ends_v, e_sem.at[0])
-    gain_o[...] = sums[0:1, :]
-    shift_o[...] = sums[1:2, :]
-    row_o[...] = sums[2:3, :]
-    row_b[...] = sums[2:3, :]
-    for r in range(3):
-        qkv_b[r] = sums[3 + r:4 + r, :]
-    for r in range(6, used):
-        fc1_b[:, (r - 6) * LANES:(r - 5) * LANES] = sums[r:r + 1, :]
+    sums_in = copy(sums, sums_v, s_sem.at[0])
+    sums_in.start()
+    tiny = [
+        copy(row_v.at[0], gain_o, s_sem.at[1]),
+        copy(row_v.at[1], shift_o, s_sem.at[2]),
+        copy(row_v.at[2], row_o, s_sem.at[3]),
+        copy(row_v.at[2], row_b, s_sem.at[4]),
+        copy(qkv_v, qkv_b, s_sem.at[5]),
+        copy(hidden_v, fc1_b, s_sem.at[6]),
+    ]
     ready = set()
     stores = []
     for i, (which, _, _, target) in enumerate(table):
@@ -1939,6 +1945,16 @@
         )
         stores.append(copy(done_v.at[i], target, d_sem.at[i]))
         stores[-1].start()
+        if i == 2:
+            sums_in.wait()
+            for r in range(3):
+                row_v[r] = sums_v[r:r + 1, :]
+                qkv_v[r] = sums_v[3 + r:4 + r, :]
+            for r in range(6, used):
+                hidden_v[:, (r - 6) * LANES:(r - 5) * LANES] = sums_v[r:r + 1, :]
+            for one in tiny:
+                one.start()
+            stores.extend(tiny)
         if i == strips - 3:
             ends_in.wait()
             stores.append(copy(ends_v, ends_o, e_sem.at[1]))
@@ -1953,7 +1969,6 @@
     micro, nf, length = act.shape[:3]
     strips = 2 * (hidden // own) + 4
     anywhere = pl.BlockSpec(memory_space=pl.ANY)
-    inside = pl.BlockSpec(memory_space=pltpu.VMEM)
     small = jax.ShapeDtypeStruct((1, LANES), F32)
     dma = pltpu.SemaphoreType.DMA
     return pl.pallas_call(
@@ -1965,14 +1980,17 @@
             jax.ShapeDtypeStruct(fc2.shape, F32), jax.ShapeDtypeStruct(fc1.shape, F32),
             jax.ShapeDtypeStruct(out.shape, F32), jax.ShapeDtypeStruct(qkv.shape, F32),
         ],
-        in_specs=[anywhere, inside] + [anywhere] * 9,
-        out_specs=[anywhere] + [inside] * 6 + [anywhere] * 4,
+        in_specs=[anywhere] * 11,
+        out_specs=[anywhere] * 11,
         scratch_shapes=[
             pltpu.VMEM(ends.shape, F32), pltpu.VMEM(turned.shape, BF16),
             pltpu.VMEM((strips, depth, own), BF16),
             pltpu.VMEM((strips, nf, length, own), BF16),
             pltpu.VMEM((strips, depth, own), F32),
             dma((2,)), dma((2,)), dma((strips,)), dma((strips,)), dma((strips,)),
+            pltpu.VMEM(sums.shape, F32), pltpu.VMEM((3, 1, LANES), F32),
+            pltpu.VMEM((3, 1, LANES), F32), pltpu.VMEM((1, (used - 6) * LANES), F32),
+            dma((7,)),
         ],
         compiler_params=pltpu.CompilerParams(vmem_limit_bytes=VMEM_LIMIT),
         name="last_products",

time: 312 us -> 311 us (level)
  no operation moved by 1% of the time
where the time goes in v8:
time: 311 us
  Pallas kernels  310 us (100%)
    pallas_call x1, Pallas kernels, fused(): pl.pallas_call(functools.partial(fused_kernel, nf, nt), out_shape=out_sha...  297 us
    pallas_call x1, Pallas kernels, last_products(): pl.pallas_call(functools.partial(last_kernel, used, micro - 1), out_shape...  13.6 us

profile of v8, /device:TPU:0, one launch (start us, length us, event | category | flops | bytes accessed | tf_op | source)
XLA Modules:
  0.0 311.0 jit_solution(15479451287031508825)
XLA Ops:
  0.6 296.5 %fused.1 = (f32[2,64,2048]{2,1,0:T(8,128)}, f32[16,128]{1,0:T(8,128)}, bf16[512,2048]{1,0:T(8,128)(2,1)}, bf16[512,2048]{1,0:T(8,128)(2,1)}, bf16[512,512]{1,0:T...) custom-call(bf16[2,64,2048]{2,1,0:T(8,128)(2,1)} %bitcast.19, ...), custom_call_target="tpu_custom_call" | custom-call | tf_op jit(solution)/shard_map/fused/pallas_call | solution.py:1768
  297.2 13.6 %last_products.1 = (f32[2,64,2048]{2,1,0:T(8,128)}, f32[1,128]{1,0:T(1,128)}, f32[1,128]{1,0:T(1,128)}, f32[1,128]{1,0:T(1,128)}, f32[1,128]{1,0:T(1,128)}, /*in...) custom-call(f32[2,64,2048]{2,1,0:T(8,128)} %get-tuple-element.33.end, ...), custom_call_target="tpu_custom_call" | custom-call | tf_op jit(solution)/shard_map/last_products/pallas_call | solution.py:1974
